TPU v7x, 128 devices: a whole 4x4x4 slice. The times are simulated.
128 devices in a mesh: seq: 16 (over x, y_lo, core), tp: 8 (over z, y_hi).
Axes of the slice: x: 4, y: 4 (y_hi: 2, y_lo: 2; y = y_hi * 2 + y_lo), z: 4, core: 2. Of those that a mesh axis runs over, the one named last changes fastest.
Arguments:
- x_old: bfloat16 [8192, 4608], P('seq', 'tp'), may hold values from -6 to 6
- old_blocks: int32 [16], replicated, may hold values from 1 to 4, 32 in all
- new_blocks: int32 [16], replicated, may hold values from 1 to 4, 32 in all
- order: int32 [16], replicated, may hold values from 0 to 15, as said below
- pre_gain: float32 [4608], replicated, may hold values from 0.25 to 1.75
- post_gain: float32 [4608], replicated, may hold values from 0.25 to 1.75
- w_query: bfloat16 [4608, 4096], P('seq', 'tp'), may hold values from -0.59765625 to 0.59765625
- w_key: bfloat16 [4608, 2048], P('seq', 'tp'), may hold values from -0.09375 to 0.09375
- w_value: bfloat16 [4608, 2048], P('seq', 'tp'), may hold values from -0.09375 to 0.09375
- w_out_t: bfloat16 [4608, 4096], P('seq', 'tp'), may hold values from -0.09375 to 0.09375
Outputs:
- layer_out: bfloat16 [8192, 4608], P(('seq', 'tp'))
Inputs may be any that keep to these rules, and one draw needn't show every extreme that they name: `old_blocks`: counts of 128-row blocks, at least one each; they sum to 32, and the largest is exactly 4. `new_blocks`: counts of 128-row blocks, at least one each; they sum to 32, and the largest is exactly 4. A permutation of the seq indices with order[15] = 0 and order[7] = 15; the other indices, taken in increasing order, hold 1 to 14 in increasing order, except that aligned pairs of them (first and second, third and fourth, and so on) are swapped or not, pair by pair.
All inputs are finite; a program needn't handle non-finite values.
Results may differ from a plain program's by a relative error of at most 0.013.
Values may be sent and summed in bfloat16 or wider, within the bound.
No kernel may reach another device: no remote copies, remote signals or barrier semaphores. Data moves between devices by JAX's collectives and lax.ppermute only.
A program may use at most 128 MiB of HBM per device.

v0:
```python
import math

import jax
import jax.numpy as jnp
from jax import lax
from jax.experimental import pallas as pl
from jax.experimental.pallas import tpu as pltpu
from jax.sharding import Mesh
from jax.sharding import PartitionSpec as P

D = 4608
HEADS = 32
HEAD = 128
BLOCK = 128
EPS = 1e-06
F32 = jnp.float32
BF16 = jnp.bfloat16

AXES = ("x", "yl", "c", "z", "yh")
SEQ = ("x", "yl", "c")
TP = ("z", "yh")


SMEM = pl.BlockSpec(memory_space=pltpu.SMEM)


def shift(value, axis, by):
    n = lax.axis_size(axis)
    return lax.ppermute(value, axis, [(i, (i + by) % n) for i in range(n)])


def rope(values, cos, sin):
    half = HEAD // 2
    swapped = jnp.concatenate([values[:, half:], values[:, :half]], axis=1)
    return values * cos + swapped * sin


def spot(flat):
    me = flat[0]
    return me >> 5, (me >> 4) & 1, (me >> 3) & 1, (me >> 1) & 3, me & 1


def starts(blocks):
    result, so_far = [], jnp.int32(0)
    for m in range(16):
        result.append(so_far)
        so_far = so_far + blocks[m]
    return result


VMEM = pl.BlockSpec(memory_space=pltpu.VMEM)
AWAY = pl.BlockSpec(memory_space=pl.ANY)


def grant(mib):
    return pltpu.CompilerParams(vmem_limit_bytes=mib << 20)


def move(jobs):
    for index, sources, target in jobs:
        for k, source in enumerate(sources):

            def copy(source=source, target=target):
                target[...] = source[...]

            if len(sources) == 1:
                copy()
            else:
                pl.when(index == k)(copy)


def lanes(first):
    return pl.ds(pl.multiple_of(first, BLOCK), BLOCK)


def fetch(jobs, sems):
    copies = [pltpu.make_async_copy(s, t, sems.at[n]) for n, (s, t) in enumerate(jobs)]
    for copy in copies:
        copy.start()
    for copy in copies:
        copy.wait()


def join_kernel(key, value, query, joined, sems):
    jobs, at = [], 0
    for source, first, width in (
        (key, 0, HEAD),
        (value, 0, HEAD),
        (key, HEAD, HEAD),
        (value, HEAD, HEAD),
        (query, 0, 4 * HEAD),
    ):
        jobs.append((source.at[:, first : first + width], joined.at[:, at : at + width]))
        at += width
    fetch(jobs, sems)


def leave_kernel(flat, old_blocks, order, x_old, *refs):
    outs, sems = refs[:4], refs[4]
    x, yl, c, _, _ = spot(flat)
    shard = order[4 * x + 2 * yl + c]
    first = jnp.int32(0)
    for m in range(16):
        first = first + jnp.where(m < shard, old_blocks[m], 0)
    jobs = []
    for d in range(4):
        row = jnp.bitwise_and(x + d - first, 3) * BLOCK
        jobs.append((x_old.at[:, lanes(row)], outs[d]))
    fetch(jobs, sems)


def holders(old_blocks, order, blocks):
    begin = starts(old_blocks)
    result = []
    for block in blocks:
        shard = jnp.int32(-1)
        for m in range(16):
            shard = shard + (begin[m] <= block).astype(jnp.int32)
        holder = jnp.int32(0)
        for m in range(16):
            holder = holder + jnp.where(order[m] == shard, m, 0)
        result.append(holder)
    return result


def targets(x, yl, c):
    to = 2 * yl + c
    return [x + 4 * to, x + 28 - 4 * to]


def sort_kernel(flat, old_blocks, order, *refs):
    sources, (mine, cross) = refs[:8], refs[8:]
    x, yl, c, _, _ = spot(flat)
    blocks = targets(x, yl, c) + targets(x, 1 - yl, c)
    jobs = []
    for n, holder in enumerate(holders(old_blocks, order, blocks)):
        index = jnp.bitwise_and(x - (holder >> 2), 3) + 4 * jnp.bitwise_xor(holder & 1, c)
        out, at = (mine, n) if n < 2 else (cross, n - 2)
        jobs.append((index, sources, out.at[:, at * BLOCK : (at + 1) * BLOCK]))
    move(jobs)


def settle_kernel(flat, old_blocks, order, mine, crossed, rows):
    x, yl, c, _, _ = spot(flat)
    jobs = []
    for n, holder in enumerate(holders(old_blocks, order, targets(x, yl, c))):
        at = slice(n * BLOCK, (n + 1) * BLOCK)
        index = jnp.bitwise_xor((holder >> 1) & 1, yl)
        jobs.append((index, [mine.at[:, at], crossed.at[:, at]], rows.at[:, at]))
    move(jobs)


def norm_kernel(flat, *refs):
    pieces, (gain, normed, resident, features, raw) = refs[:8], refs[8:]
    _, _, _, z, yh = spot(flat)
    width, count = pieces[0].shape
    total = jnp.zeros((1, count), F32)
    for n, piece in enumerate(pieces):
        wide = piece[...].astype(F32)
        total = total + jnp.sum(wide * wide, axis=0, keepdims=True)
        t = 2 * jnp.bitwise_and(z - n % 4, 3) + jnp.bitwise_xor(yh, n // 4)
        features[pl.ds(pl.multiple_of(t * width, 64), width), :] = piece[...]
    scale = lax.rsqrt(total / D + EPS)
    scale = jnp.transpose(jnp.broadcast_to(scale, (BLOCK, count)))
    step = 512
    for at in range(0, D, step):
        rows = jnp.transpose(features[at : at + step, :])
        raw[:, at : at + step] = rows
        for k in range(0, step, BLOCK):
            cols = slice(at + k, at + k + BLOCK)
            wide = rows[:, k : k + BLOCK].astype(F32) * scale * gain[:, cols]
            normed[:, cols] = wide.astype(BF16)
    first = pl.multiple_of(64 * yh + 16 * z, 16)
    for block in range(2):
        source = pl.ds(pl.multiple_of(first + block * BLOCK, 16), 16)
        resident[block * 16 : block * 16 + 16, :] = raw[source, :]


def key_value_kernel(normed, weight, cos, sin, kv, buffer, total, sems):
    step = buffer.shape[0] // sems.shape[0]

    def copy(n):
        rows = pl.ds(n * step, step)
        return pltpu.make_async_copy(
            weight.at[rows, : 4 * HEAD], buffer.at[rows, :], sems.at[n]
        )

    for n in range(sems.shape[0]):
        copy(n).start()
    for n in range(sems.shape[0]):
        copy(n).wait()
        rows = slice(n * step, (n + 1) * step)
        part = jnp.dot(normed[:, rows], buffer[rows, :], preferred_element_type=F32)
        total[...] = part if n == 0 else total[...] + part
    for h in range(2):
        at = 2 * h * HEAD
        kv[:, at : at + HEAD] = rope(total[:, at : at + HEAD], cos[...], sin[...]).astype(BF16)
        kv[:, at + HEAD : at + 2 * HEAD] = total[:, at + HEAD : at + 2 * HEAD].astype(BF16)


def query_kernel(normed, weight, cos, sin, query):
    total = jnp.dot(normed[...], weight[...], preferred_element_type=F32)
    at = pl.multiple_of(pl.program_id(0) * 2 * HEAD, 2 * HEAD)
    for h in range(2):
        part = total[:, h * HEAD : (h + 1) * HEAD]
        turned = rope(part, cos[...], sin[...]) * (D // HEADS) ** (-0.5)
        query[:, pl.ds(at + h * HEAD, HEAD)] = turned.astype(BF16)


def attention_kernel(flat, query, *refs):
    kv = [refs[4 * k : 4 * k + 4] for k in range(4)]
    context, numer, denom = refs[16:]
    x, yl, c, _, _ = spot(flat)
    w = 2 * yl + c
    row = lax.broadcasted_iota(jnp.int32, (2 * BLOCK, BLOCK), 0) % BLOCK
    col = lax.broadcasted_iota(jnp.int32, (2 * BLOCK, BLOCK), 1)

    def chunk(first, dw, block, slot, masked):
        near, far = pl.ds(first, HEAD), pl.ds(first + HEAD, HEAD)
        if isinstance(block, int):
            q_rows, k_rows = pl.ds(block * BLOCK, BLOCK), pl.ds(slot * BLOCK, BLOCK)
        else:
            q_rows = pl.ds(pl.multiple_of(block * BLOCK, BLOCK), BLOCK)
            k_rows = pl.ds(pl.multiple_of(slot * BLOCK, BLOCK), BLOCK)
        q2 = jnp.concatenate([query[q_rows, near], query[q_rows, far]], axis=0)
        keys = jnp.concatenate([kv[dw][d][k_rows, near] for d in range(4)], axis=0)
        values = jnp.concatenate([kv[dw][d][k_rows, far] for d in range(4)], axis=0)
        score = lax.dot_general(q2, keys, (((1,), (1,)), ((), ())), preferred_element_type=F32)
        weight = jnp.exp(50.0 * jnp.tanh(score * (1.0 / 50.0)))
        parts = [weight[:, d * BLOCK : (d + 1) * BLOCK] for d in range(4)]
        if masked:
            parts = [jnp.where(col <= row, parts[0], 0.0)] + [
                jnp.where(x >= d, parts[d], 0.0) for d in range(1, 4)
            ]
            weight = jnp.concatenate(parts, axis=1)
        denom[block] += (parts[0] + parts[1]) + (parts[2] + parts[3])
        numer[block] += jnp.dot(weight.astype(BF16), values, preferred_element_type=F32)

    @pl.loop(0, 2)
    def _(head):
        first = pl.multiple_of(head * 2 * HEAD, 2 * HEAD)
        numer[...] = jnp.zeros_like(numer)
        denom[...] = jnp.zeros_like(denom)
        chunk(first, 0, 0, 0, True)
        chunk(first, 0, 1, 0, False)
        chunk(first, 0, 1, 1, True)
        for dw in range(1, 4):
            later = (jnp.bitwise_xor(w, dw) > w).astype(jnp.int32)
            chunk(first, dw, 1, 0, False)
            chunk(first, dw, later, later, False)
        for block in range(2):
            out = numer[block] / jnp.sum(denom[block], axis=1, keepdims=True)
            rows = slice(block * BLOCK, (block + 1) * BLOCK)
            context[rows, pl.ds(first, HEAD)] = out[:BLOCK].astype(BF16)
            context[rows, pl.ds(first + HEAD, HEAD)] = out[BLOCK:].astype(BF16)


def out_kernel(flat, context, weight, *refs):
    outs, (buffer, scratch, sems) = refs[:8], refs[8:]
    _, _, _, z, yh = spot(flat)
    tile, steps = scratch.shape[1], sems.shape[0]

    def copy(n):
        rows = pl.ds(pl.multiple_of(n * tile, tile), tile)
        return pltpu.make_async_copy(weight.at[rows, :], buffer.at[rows, :], sems.at[n])

    @pl.loop(0, steps)
    def _(n):
        copy(n).start()

    @pl.loop(0, steps)
    def _(n):
        copy(n).wait()
        cols = pl.ds(pl.multiple_of(n * tile, tile), tile)
        scratch[...] = lax.dot_general(
            context[...], buffer[cols, :], (((1,), (1,)), ((), ())), preferred_element_type=F32
        ).astype(BF16)
        for dy in range(2):
            for dz in range(4):
                first = jnp.bitwise_xor(yh, dy) * 64 + jnp.bitwise_and(z + dz, 3) * 16
                for block in range(2):
                    rows = pl.ds(pl.multiple_of(first + block * BLOCK, 16), 16)
                    outs[4 * dy + dz][block * 16 : block * 16 + 16, cols] = scratch[rows, :]


def finish_kernel(resident, gain, *refs):
    terms, out = refs[:8], refs[8]
    total = terms[0][...].astype(F32)
    for term in terms[1:]:
        total = total + term[...].astype(F32)
    scale = lax.rsqrt(jnp.mean(total * total, axis=1, keepdims=True) + EPS)
    out[...] = (resident[...].astype(F32) + total * scale * gain[...]).astype(BF16)


def before(blocks, shard):
    result = jnp.int32(0)
    for m in range(16):
        result = result + jnp.where(m < shard, blocks[m], 0)
    return result


def owner_kernel(flat, new_blocks, *refs):
    by_w, outs = refs[:4], refs[4:]
    x, yl, c, _, _ = spot(flat)
    w = 2 * yl + c
    jobs = []
    for d in range(4):
        start = before(new_blocks, 4 * jnp.bitwise_and(x + d, 3) + w)
        level = (start + jnp.bitwise_and(x - start, 3)) >> 2
        slot = (level >= 4).astype(jnp.int32)
        source = jnp.bitwise_and(jnp.where(level < 4, level, 7 - level), 3)
        row = pl.ds(pl.multiple_of(slot * 16, 16), 16)
        jobs.append((jnp.bitwise_xor(source, w), [part.at[row, :] for part in by_w], outs[d]))
    move(jobs)


def place_kernel(flat, new_blocks, *refs):
    gathered, outs = refs[:4], refs[4:]
    x, yl, c, z, _ = spot(flat)
    start = before(new_blocks, 4 * x + 2 * yl + c)
    move([(jnp.bitwise_and(x - start - (z + d), 3), gathered, outs[d]) for d in range(4)])


def close_kernel(flat, new_blocks, *refs):
    parts, out = refs[:4], refs[4]
    x, yl, c, z, _ = spot(flat)
    count = new_blocks[4 * x + 2 * yl + c]

    @pl.when(z >= count)
    def _():
        out[...] = jnp.zeros_like(out)

    @pl.when(z < count)
    def _():
        for d in range(4):
            row = pl.multiple_of(jnp.bitwise_and(z - d, 3) * 16, 16)
            out[pl.ds(row, 16), :] = parts[d][...]


def per_device(
    x_old, old_blocks, new_blocks, order, pre_gain, post_gain, w_query, w_key, w_value, w_out_t
):
    flat = lax.axis_index(AXES).astype(jnp.int32).reshape(1)
    width = x_old.shape[1]
    count = 2 * BLOCK

    def near_by(arrays):
        return [pltpu.with_memory_space_constraint(a, pltpu.VMEM) for a in arrays]

    def far_off(arrays):
        return [pltpu.with_memory_space_constraint(a, pltpu.HBM) for a in arrays]

    def call(kernel, tables, arrays, shapes):
        results = pl.pallas_call(
            kernel,
            in_specs=[SMEM] * (1 + len(tables)) + [VMEM] * len(arrays),
            out_specs=[VMEM] * len(shapes),
            out_shape=[pltpu.VMEM(s, BF16) for s in shapes],
            compiler_params=grant(8),
        )(flat, *tables, *near_by(arrays))
        return list(results)

    def bring(kernel, tables, arrays, shapes, copies, kind):
        results = pl.pallas_call(
            kernel,
            in_specs=[SMEM] * len(tables) + [AWAY] * len(arrays),
            out_specs=[VMEM] * len(shapes),
            out_shape=[kind(s, BF16) for s in shapes],
            scratch_shapes=[pltpu.SemaphoreType.DMA((copies,))],
            compiler_params=grant(8),
        )(*tables, *far_off(arrays))
        return list(results)

    (joined,) = bring(
        join_kernel,
        (),
        (w_key, w_value, w_query),
        [(w_key.shape[0], 8 * HEAD)],
        5,
        jax.ShapeDtypeStruct,
    )
    qkv_full = lax.all_gather(joined, SEQ, axis=0, tiled=True)
    out_full = lax.all_gather(w_out_t, SEQ, axis=0, tiled=True)

    old = far_off((old_blocks, order))
    near = bring(leave_kernel, (flat, *old), (x_old.T,), [(width, BLOCK)] * 4, 4, pltpu.VMEM)
    near = near[:1] + [shift(near[d], "x", d) for d in range(1, 4)]
    far = [shift(part, "c", 1) for part in near]
    mine, cross = call(sort_kernel, old, near + far, [(width, count)] * 2)
    cross = shift(cross, "yl", 1)
    (rows,) = call(settle_kernel, old, (mine, cross), [(width, count)])

    facing = shift(rows, "yh", 1)
    pieces = [rows] + [shift(rows, "z", d) for d in range(1, 4)]
    pieces += [facing] + [shift(facing, "z", d) for d in range(1, 4)]

    slot_rows = jnp.arange(BLOCK, dtype=jnp.int32)
    x, w = flat[0] >> 5, (flat[0] >> 3) & 3
    positions = jnp.concatenate(
        [b * BLOCK + slot_rows for b in (x + 4 * w, x + 28 - 4 * w)]
    )
    inverse = jnp.exp(jnp.arange(HEAD // 2, dtype=F32) * (-2.0 * math.log(10000.0) / HEAD))
    angles = positions.astype(F32)[:, None] * inverse[None, :]
    cosine, sine = jnp.cos(angles), jnp.sin(angles)
    cosine = jnp.concatenate([cosine, cosine], axis=1)
    sine = jnp.concatenate([-sine, sine], axis=1)

    normed, resident = pl.pallas_call(
        norm_kernel,
        in_specs=[SMEM] + [VMEM] * 9,
        out_specs=[VMEM] * 2,
        out_shape=[pltpu.VMEM((count, D), BF16), pltpu.VMEM((32, D), BF16)],
        scratch_shapes=[pltpu.VMEM((D, count), BF16), pltpu.VMEM((count, D), BF16)],
        compiler_params=grant(24),
        name="norm",
    )(flat, *near_by(pieces), pre_gain.reshape(1, D))
    tables = near_by((cosine, sine))

    def heads(kernel, first):
        return pl.pallas_call(
            kernel,
            grid=(2,),
            in_specs=[VMEM, pl.BlockSpec((D, 2 * HEAD), lambda n: (0, n + first)), VMEM, VMEM],
            out_specs=VMEM,
            out_shape=pltpu.VMEM((count, 4 * HEAD), BF16),
            compiler_params=grant(24),
        )(*near_by((normed,)), *far_off((qkv_full,)), *tables)

    kv = pl.pallas_call(
        key_value_kernel,
        in_specs=[VMEM, AWAY, VMEM, VMEM],
        out_specs=VMEM,
        out_shape=pltpu.VMEM((count, 4 * HEAD), BF16),
        scratch_shapes=[
            pltpu.VMEM((D, 4 * HEAD), BF16),
            pltpu.VMEM((count, 4 * HEAD), F32),
            pltpu.SemaphoreType.DMA((4,)),
        ],
        compiler_params=grant(24),
        name="key_value",
    )(*near_by((normed,)), *far_off((qkv_full,)), *tables)

    opposite = shift(kv, "x", 2)
    same = [kv, shift(kv, "x", 1), opposite, shift(kv, "x", 3)]
    pair = shift(kv, "yl", 1)
    other = [pair, shift(pair, "x", 1), shift(same[2], "yl", 1), shift(pair, "x", 3)]
    spread = []
    for part in (same, other):
        spread += part
        spread += [shift(s, "c", 1) for s in part]

    query = heads(query_kernel, 2)
    context = pl.pallas_call(
        attention_kernel,
        in_specs=[SMEM] + [VMEM] * 17,
        out_specs=VMEM,
        out_shape=pltpu.VMEM((count, 4 * HEAD), BF16),
        scratch_shapes=[pltpu.VMEM((2, 2 * BLOCK, HEAD), F32), pltpu.VMEM((2, 2 * BLOCK, HEAD), F32)],
        compiler_params=grant(24),
        name="attention",
    )(flat, *near_by((query, *spread)))

    tile = 512
    shares = pl.pallas_call(
        out_kernel,
        in_specs=[SMEM, VMEM, AWAY],
        out_specs=[VMEM] * 8,
        out_shape=[pltpu.VMEM((32, D), BF16)] * 8,
        scratch_shapes=[
            pltpu.VMEM((D, 4 * HEAD), BF16),
            pltpu.VMEM((count, tile), BF16),
            pltpu.SemaphoreType.DMA((D // tile,)),
        ],
        compiler_params=grant(16),
        name="project",
    )(flat, *near_by((context,)), *far_off((out_full,)))
    received = []
    for dy in range(2):
        for dz in range(4):
            part = shares[4 * dy + dz]
            if dy and dz:
                n = [(i, j) for i in range(4) for j in range(2)]
                part = lax.ppermute(
                    part, TP, [(2 * i + j, 2 * ((i + dz) % 4) + (j ^ dy)) for i, j in n]
                )
            elif dy:
                part = shift(part, "yh", 1)
            elif dz:
                part = shift(part, "z", dz)
            received.append(part)

    refreshed = pl.pallas_call(
        finish_kernel,
        in_specs=[VMEM] * 10,
        out_specs=VMEM,
        out_shape=pltpu.VMEM((32, D), BF16),
        compiler_params=grant(8),
        name="finish",
    )(*near_by((resident, post_gain.reshape(1, D), *received)))

    by_yl = shift(refreshed, "yl", 1)
    by_w = [refreshed, shift(refreshed, "c", 1), by_yl, shift(by_yl, "c", 1)]
    new = far_off((new_blocks,))
    slices = [(16, D)] * 4
    gathered = call(owner_kernel, new, by_w, slices)
    gathered = gathered[:1] + [shift(gathered[d], "x", d) for d in range(1, 4)]
    final = call(place_kernel, new, gathered, slices)
    final = final[:1] + [shift(final[d], "z", d) for d in range(1, 4)]
    (layer_out,) = call(close_kernel, new, final, [(64, D)])
    return layer_out


def solution(mesh):
    torus = Mesh(mesh.devices.reshape(4, 2, 2, 4, 2), AXES)
    in_specs = (
        P(SEQ, TP),
        P(),
        P(),
        P(),
        P(),
        P(),
        P(SEQ, TP),
        P(SEQ, TP),
        P(SEQ, TP),
        P(SEQ, TP),
    )
    out_specs = P(SEQ + TP, None)

    return jax.shard_map(
        per_device, mesh=torus, in_specs=in_specs, out_specs=out_specs, check_vma=False
    )
```

profile of v0, /device:TPU:1, one launch (start us, length us, event | category | flops | bytes accessed | tf_op | source)
XLA Modules:
  0.0 215.9 jit_solution(151759333888319196)
XLA Ops:
  6.5 2.0 shard_map.103
  9.3 1.9 shard_map.100
  11.2 2.1 collective-permute-start
  13.3 2.5 %collective-permute-start.1 = (bf16[576,128]{1,0:T(8,128)(2,1)S(1)}, bf16[576,128]{1,0:T(8,128)(2,1)S(1)}, u32[]{:S(2)}, u32[]{:S(2)}) collective-permute-start(bf16[576,128]{1,0:T(8,128)(2,1)S(1)} %get-tuple-element.31), channel_id=1, source_target_pairs={{0,64},{32,96},{64,0},{96,32},{1,65},{33,97},{65,1},{97,33},{2,66}... | collective-permute-start | bytes 442376 | tf_op jit(solution)/shard_map/ppermute | solution.py:29
  15.7 1.2 collective-permute-start.2
  16.9 1.5 collective-permute-start.3
  19.4 2.8 %collective-permute-done.1.refs_2_ = bf16[576,128]{1,0:T(8,128)(2,1)S(1)} collective-permute-done((bf16[576,128]{1,0:T(8,128)(2,1)S(1)}, bf16[576,128]{1,0:T(8,128)(2,1)S(1)}, u32[]{:S(2)}, u32[]{:S(2)}) %collective-permute-start.1) | collective-permute-done | bytes 147488 | tf_op jit(solution)/shard_map/ppermute | solution.py:29
  22.2 1.5 collective-permute-start.5
  26.2 1.4 collective-permute-start.7
  27.6 14.1 %collective-permute-done.7.crossed = bf16[576,256]{1,0:T(8,128)(2,1)S(1)} collective-permute-done((bf16[576,256]{1,0:T(8,128)(2,1)S(1)}, bf16[576,256]{1,0:T(8,128)(2,1)S(1)}, u32[]{:S(2)}, u32[]{:S(2)}) %collective-permute-start.7) | collective-permute-done | bytes 294944 | tf_op jit(solution)/shard_map/ppermute | solution.py:29
  42.5 1.7 collective-permute-start.8
  44.2 2.9 %collective-permute-start.11 = (bf16[576,256]{1,0:T(8,128)(2,1)S(1)}, bf16[576,256]{1,0:T(8,128)(2,1)S(1)}, u32[]{:S(2)}, u32[]{:S(2)}) collective-permute-start(bf16[576,256]{1,0:T(8,128)(2,1)S(1)} %shard_map.102.refs_0_), channel_id=1, source_target_pairs={{0,1},{1,0},{2,3},{3,2},{4,5},{5,4},{6,7},{7,6},{8,9},{9,8},{10,11... | collective-permute-start | bytes 884744 | tf_op jit(solution)/shard_map/ppermute | solution.py:29
  47.2 3.6 %collective-permute-start.9 = (bf16[576,256]{1,0:T(8,128)(2,1)S(1)}, bf16[576,256]{1,0:T(8,128)(2,1)S(1)}, u32[]{:S(2)}, u32[]{:S(2)}) collective-permute-start(bf16[576,256]{1,0:T(8,128)(2,1)S(1)} %shard_map.102.refs_0_), channel_id=1, source_target_pairs={{0,4},{2,6},{4,0},{6,2},{1,5},{3,7},{5,1},{7,3},{8,12},{10,14},{12... | collective-permute-start | bytes 884744 | tf_op jit(solution)/shard_map/ppermute | solution.py:29
  51.2 9.5 %collective-permute-done.11.refs_4_ = bf16[576,256]{1,0:T(8,128)(2,1)S(1)} collective-permute-done((bf16[576,256]{1,0:T(8,128)(2,1)S(1)}, bf16[576,256]{1,0:T(8,128)(2,1)S(1)}, u32[]{:S(2)}, u32[]{:S(2)}) %collective-permute-start.11) | collective-permute-done | bytes 294944 | tf_op jit(solution)/shard_map/ppermute | solution.py:29
  60.7 1.6 collective-permute-start.12
  62.4 2.1 collective-permute-start.13
  64.4 1.9 collective-permute-start.14
  67.1 1.5 collective-permute-done.12.refs_5_
  68.6 7.7 %collective-permute-done.13.refs_6_ = bf16[576,256]{1,0:T(8,128)(2,1)S(1)} collective-permute-done((bf16[576,256]{1,0:T(8,128)(2,1)S(1)}, bf16[576,256]{1,0:T(8,128)(2,1)S(1)}, u32[]{:S(2)}, u32[]{:S(2)}) %collective-permute-start.13) | collective-permute-done | bytes 294944 | tf_op jit(solution)/shard_map/ppermute | solution.py:29
  77.5 4.8 %all-gather.3.cloned.1.call-done.weight = bf16[4608,1024]{1,0:T(8,128)(2,1)} async-done(((bf16[288,1024]{1,0:T(8,128)(2,1)}), bf16[4608,1024]{1,0:T(8,128)(2,1)}) %all-gather.3.cloned.1.call-update) | async-done | bytes 9437200 | tf_op jit(solution)/shard_map/all_gather | solution.py:382
  82.3 3.0 %key_value.1.refs_0_ = bf16[256,512]{1,0:T(8,128)(2,1)S(1)} custom-call(bf16[256,4608]{1,0:T(8,128)(2,1)S(1)} %get-tuple-element.36.normed, bf16[4608,1024]{1,0:T(8,128)(2,1)} %all-gather.3.cloned.1.call-done.weight, f32[256,128]{1,0:T(8,128)S(1)} %pad_maximum_fusion.cos, f32[256,128]{1,0:T(8,128)S(1)} %pad_maximum_fusion.1.sin), custom_call_target="tpu_custom_call" | custom-call | tf_op jit(solution)/shard_map/key_value/pallas_call | solution.py:429
  85.4 3.5 %collective-permute-start.16 = (bf16[256,512]{1,0:T(8,128)(2,1)S(1)}, bf16[256,512]{1,0:T(8,128)(2,1)S(1)}, u32[]{:S(2)}, u32[]{:S(2)}) collective-permute-start(bf16[256,512]{1,0:T(8,128)(2,1)S(1)} %key_value.1.refs_0_), channel_id=1, source_target_pairs={{0,64},{32,96},{64,0},{96,32},{1,65},{33,97},{65,1},{97,33},{2,66}... | collective-permute-start | bytes 786440 | tf_op jit(solution)/shard_map/ppermute | solution.py:29
  90.4 3.8 %collective-permute-done.15.refs_1_ = bf16[256,512]{1,0:T(8,128)(2,1)S(1)} collective-permute-done((bf16[256,512]{1,0:T(8,128)(2,1)S(1)}, bf16[256,512]{1,0:T(8,128)(2,1)S(1)}, u32[]{:S(2)}, u32[]{:S(2)}) %collective-permute-start.15) | collective-permute-done | bytes 262176 | tf_op jit(solution)/shard_map/ppermute | solution.py:29
  95.3 8.9 %collective-permute-done.16.refs_2_ = bf16[256,512]{1,0:T(8,128)(2,1)S(1)} collective-permute-done((bf16[256,512]{1,0:T(8,128)(2,1)S(1)}, bf16[256,512]{1,0:T(8,128)(2,1)S(1)}, u32[]{:S(2)}, u32[]{:S(2)}) %collective-permute-start.16) | collective-permute-done | bytes 262176 | tf_op jit(solution)/shard_map/ppermute | solution.py:29
  104.2 2.6 %collective-permute-start.20 = (bf16[256,512]{1,0:T(8,128)(2,1)S(1)}, bf16[256,512]{1,0:T(8,128)(2,1)S(1)}, u32[]{:S(2)}, u32[]{:S(2)}) collective-permute-start(bf16[256,512]{1,0:T(8,128)(2,1)S(1)} %collective-permute-done.16.refs_2_), channel_id=1, source_target_pairs={{0,8},{8,0},{1,9},{9,1},{2,10},{10,2},{3,11},{11,3},{4,12},{12,4},... | collective-permute-start | bytes 786440 | tf_op jit(solution)/shard_map/ppermute | solution.py:29
  107.1 2.5 %collective-permute-start.25 = (bf16[256,512]{1,0:T(8,128)(2,1)S(1)}, bf16[256,512]{1,0:T(8,128)(2,1)S(1)}, u32[]{:S(2)}, u32[]{:S(2)}) collective-permute-start(bf16[256,512]{1,0:T(8,128)(2,1)S(1)} %collective-permute-done.22.refs_8_), channel_id=1, source_target_pairs={{0,96},{32,0},{64,32},{96,64},{1,97},{33,1},{65,33},{97,65},{2,98}... | collective-permute-start | bytes 786440 | tf_op jit(solution)/shard_map/ppermute | solution.py:29
  110.3 7.6 %collective-permute-done.23.refs_9_ = bf16[256,512]{1,0:T(8,128)(2,1)S(1)} collective-permute-done((bf16[256,512]{1,0:T(8,128)(2,1)S(1)}, bf16[256,512]{1,0:T(8,128)(2,1)S(1)}, u32[]{:S(2)}, u32[]{:S(2)}) %collective-permute-start.23) | collective-permute-done | bytes 262176 | tf_op jit(solution)/shard_map/ppermute | solution.py:29
  118.8 1.7 collective-permute-done.24.refs_10_
  120.5 1.9 collective-permute-start.28
  122.6 3.5 %shard_map.104.query = bf16[256,512]{1,0:T(8,128)(2,1)S(1)} custom-call(bf16[256,4608]{1,0:T(8,128)(2,1)S(1)} %get-tuple-element.36.normed, bf16[4608,1024]{1,0:T(8,128)(2,1)} %all-gather.3.cloned.1.call-done.weight, f32[256,128]{1,0:T(8,128)S(1)} %pad_maximum_fusion.cos, f32[256,128]{1,0:T(8,128)S(1)} %pad_maximum_fusion.1.sin), custom_call_target="tpu_custom_call" | custom-call | tf_op jit(solution)/shard_map/pallas_call | solution.py:420
  126.1 5.4 %attention.1.context = bf16[256,512]{1,0:T(8,128)(2,1)S(1)} custom-call(s32[1]{0:T(128)} %bitcast.flat, bf16[256,512]{1,0:T(8,128)(2,1)S(1)} %shard_map.104.query, bf16[256,512]{1,0:T(8,128)(2,1)S(1)} %key_value.1.refs_0_, bf16[256,512]{1,0:T(8,128)(2,1)S(1)} %collective-permute-done.15.refs_1_, bf16[256,512]{1,0:T(8,128)(2,1)S(1)} %collective-permute-done.16.refs_2_, ...), custom_call_target="tpu_custom_call" | custom-call | tf_op jit(solution)/shard_map/attention/pallas_call | solution.py:453
  131.6 4.3 %project.1 = (bf16[32,4608]{1,0:T(8,128)(2,1)S(1)}, bf16[32,4608]{1,0:T(8,128)(2,1)S(1)}, bf16[32,4608]{1,0:T(8,128)(2,1)S(1)}, bf16[32,4608]{1,0:T(8,128)(2,1)S...) custom-call(s32[1]{0:T(128)} %bitcast.flat, ...), custom_call_target="tpu_custom_call" | custom-call | tf_op jit(solution)/shard_map/project/pallas_call | solution.py:464
  135.8 1.3 collective-permute-start.30
  137.2 2.6 %collective-permute-start.31 = (bf16[32,4608]{1,0:T(8,128)(2,1)S(1)}, bf16[32,4608]{1,0:T(8,128)(2,1)S(1)}, u32[]{:S(2)}, u32[]{:S(2)}) collective-permute-start(bf16[32,4608]{1,0:T(8,128)(2,1)S(1)} %get-tuple-element.39), channel_id=1, source_target_pairs={{0,4},{2,6},{4,0},{6,2},{1,5},{3,7},{5,1},{7,3},{8,12},{10,14},{12... | collective-permute-start | bytes 884744 | tf_op jit(solution)/shard_map/ppermute | solution.py:29
  140.8 2.5 %collective-permute-start.33 = (bf16[32,4608]{1,0:T(8,128)(2,1)S(1)}, bf16[32,4608]{1,0:T(8,128)(2,1)S(1)}, u32[]{:S(2)}, u32[]{:S(2)}) collective-permute-start(bf16[32,4608]{1,0:T(8,128)(2,1)S(1)} %get-tuple-element.41), channel_id=1, source_target_pairs={{0,1},{1,0},{2,3},{3,2},{4,5},{5,4},{6,7},{7,6},{8,9},{9,8},{10,11... | collective-permute-start | bytes 884744 | tf_op jit(solution)/shard_map/ppermute | solution.py:29
  143.9 1.4 collective-permute-done.30.refs_1_
  145.3 4.3 %collective-permute-start.35 = (bf16[32,4608]{1,0:T(8,128)(2,1)S(1)}, bf16[32,4608]{1,0:T(8,128)(2,1)S(1)}, u32[]{:S(2)}, u32[]{:S(2)}) collective-permute-start(bf16[32,4608]{1,0:T(8,128)(2,1)S(1)} %get-tuple-element.43), channel_id=1, source_target_pairs={{0,5},{1,4},{2,7},{3,6},{4,1},{5,0},{6,3},{7,2},{8,13},{9,12},{10,... | collective-permute-start | bytes 884744 | tf_op jit(solution)/shard_map/ppermute | solution.py:483
  149.6 12.6 %collective-permute-done.31.refs_2_ = bf16[32,4608]{1,0:T(8,128)(2,1)S(1)} collective-permute-done((bf16[32,4608]{1,0:T(8,128)(2,1)S(1)}, bf16[32,4608]{1,0:T(8,128)(2,1)S(1)}, u32[]{:S(2)}, u32[]{:S(2)}) %collective-permute-start.31) | collective-permute-done | bytes 294944 | tf_op jit(solution)/shard_map/ppermute | solution.py:29
  162.3 8.2 %collective-permute-done.36.refs_7_ = bf16[32,4608]{1,0:T(8,128)(2,1)S(1)} collective-permute-done((bf16[32,4608]{1,0:T(8,128)(2,1)S(1)}, bf16[32,4608]{1,0:T(8,128)(2,1)S(1)}, u32[]{:S(2)}, u32[]{:S(2)}) %collective-permute-start.36) | collective-permute-done | bytes 294944 | tf_op jit(solution)/shard_map/ppermute | solution.py:483
  171.0 7.0 %collective-permute-start.38 = (bf16[32,4608]{1,0:T(8,128)(2,1)S(1)}, bf16[32,4608]{1,0:T(8,128)(2,1)S(1)}, u32[]{:S(2)}, u32[]{:S(2)}) collective-permute-start(bf16[32,4608]{1,0:T(8,128)(2,1)S(1)} %finish.1.refs_0_), channel_id=1, source_target_pairs={{0,16},{16,0},{1,17},{17,1},{2,18},{18,2},{3,19},{19,3},{4,20},{20... | collective-permute-start | bytes 884744 | tf_op jit(solution)/shard_map/ppermute | solution.py:29
  178.0 2.3 %collective-permute-start.37 = (bf16[32,4608]{1,0:T(8,128)(2,1)S(1)}, bf16[32,4608]{1,0:T(8,128)(2,1)S(1)}, u32[]{:S(2)}, u32[]{:S(2)}) collective-permute-start(bf16[32,4608]{1,0:T(8,128)(2,1)S(1)} %finish.1.refs_0_), channel_id=1, source_target_pairs={{0,8},{8,0},{1,9},{9,1},{2,10},{10,2},{3,11},{11,3},{4,12},{12,4},... | collective-permute-start | bytes 884744 | tf_op jit(solution)/shard_map/ppermute | solution.py:29
  180.3 3.1 %collective-permute-done.38.refs_2_ = bf16[32,4608]{1,0:T(8,128)(2,1)S(1)} collective-permute-done((bf16[32,4608]{1,0:T(8,128)(2,1)S(1)}, bf16[32,4608]{1,0:T(8,128)(2,1)S(1)}, u32[]{:S(2)}, u32[]{:S(2)}) %collective-permute-start.38) | collective-permute-done | bytes 294944 | tf_op jit(solution)/shard_map/ppermute | solution.py:29
  183.4 2.6 %collective-permute-start.39 = (bf16[32,4608]{1,0:T(8,128)(2,1)S(1)}, bf16[32,4608]{1,0:T(8,128)(2,1)S(1)}, u32[]{:S(2)}, u32[]{:S(2)}) collective-permute-start(bf16[32,4608]{1,0:T(8,128)(2,1)S(1)} %collective-permute-done.38.refs_2_), channel_id=1, source_target_pairs={{0,8},{8,0},{1,9},{9,1},{2,10},{10,2},{3,11},{11,3},{4,12},{12,4},... | collective-permute-start | bytes 884744 | tf_op jit(solution)/shard_map/ppermute | solution.py:29
  186.0 1.2 collective-permute-done.39.refs_3_
  188.9 2.0 collective-permute-start.42
  190.9 6.7 %collective-permute-done.40.refs_1_ = bf16[16,4608]{1,0:T(8,128)(2,1)S(1)} collective-permute-done((bf16[16,4608]{1,0:T(8,128)(2,1)S(1)}, bf16[16,4608]{1,0:T(8,128)(2,1)S(1)}, u32[]{:S(2)}, u32[]{:S(2)}) %collective-permute-start.40) | collective-permute-done | bytes 147488 | tf_op jit(solution)/shard_map/ppermute | solution.py:29
  198.8 2.3 %collective-permute-start.44 = (bf16[16,4608]{1,0:T(8,128)(2,1)S(1)}, bf16[16,4608]{1,0:T(8,128)(2,1)S(1)}, u32[]{:S(2)}, u32[]{:S(2)}) collective-permute-start(bf16[16,4608]{1,0:T(8,128)(2,1)S(1)} %get-tuple-element.51), channel_id=1, source_target_pairs={{0,4},{2,6},{4,0},{6,2},{1,5},{3,7},{5,1},{7,3},{8,12},{10,14},{12... | collective-permute-start | bytes 442376 | tf_op jit(solution)/shard_map/ppermute | solution.py:29
  201.5 4.0 %collective-permute-done.43.refs_1_ = bf16[16,4608]{1,0:T(8,128)(2,1)S(1)} collective-permute-done((bf16[16,4608]{1,0:T(8,128)(2,1)S(1)}, bf16[16,4608]{1,0:T(8,128)(2,1)S(1)}, u32[]{:S(2)}, u32[]{:S(2)}) %collective-permute-start.43) | collective-permute-done | bytes 147488 | tf_op jit(solution)/shard_map/ppermute | solution.py:29
  (76 shorter events, 21.1 us)
Async XLA Ops:
  6.5 75.7 %all-gather.3.cloned.1.call-start = ((), (), s32[]{:S(2)}) async-start(), calls=%async_computation | async-start | bytes 10027008 | tf_op jit(solution)/shard_map/all_gather | solution.py:382
  8.5 123.0 %all-gather.5.cloned.1.call-start = ((), (), s32[]{:S(2)}) async-start(), calls=%async_computation.1 | async-start | bytes 5013504 | tf_op jit(solution)/shard_map/all_gather | solution.py:383
  11.2 7.2 %collective-permute-start = (bf16[576,128]{1,0:T(8,128)(2,1)S(1)}, bf16[576,128]{1,0:T(8,128)(2,1)S(1)}, u32[]{:S(2)}, u32[]{:S(2)}) collective-permute-start(bf16[576,128]{1,0:T(8,128)(2,1)S(1)} %get-tuple-element.30), channel_id=1, source_target_pairs={{0,32},{32,64},{64,96},{96,0},{1,33},{33,65},{65,97},{97,1},{2,34}... | collective-permute-start | bytes 442376 | tf_op jit(solution)/shard_map/ppermute | solution.py:29
  13.3 8.9 %collective-permute-start.1 = (bf16[576,128]{1,0:T(8,128)(2,1)S(1)}, bf16[576,128]{1,0:T(8,128)(2,1)S(1)}, u32[]{:S(2)}, u32[]{:S(2)}) collective-permute-start(bf16[576,128]{1,0:T(8,128)(2,1)S(1)} %get-tuple-element.31), channel_id=1, source_target_pairs={{0,64},{32,96},{64,0},{96,32},{1,65},{33,97},{65,1},{97,33},{2,66}... | collective-permute-start | bytes 442376 | tf_op jit(solution)/shard_map/ppermute | solution.py:29
  15.7 8.0 %collective-permute-start.2 = (bf16[576,128]{1,0:T(8,128)(2,1)S(1)}, bf16[576,128]{1,0:T(8,128)(2,1)S(1)}, u32[]{:S(2)}, u32[]{:S(2)}) collective-permute-start(bf16[576,128]{1,0:T(8,128)(2,1)S(1)} %get-tuple-element.32), channel_id=1, source_target_pairs={{0,96},{32,0},{64,32},{96,64},{1,97},{33,1},{65,33},{97,65},{2,98}... | collective-permute-start | bytes 442376 | tf_op jit(solution)/shard_map/ppermute | solution.py:29
  16.9 6.8 %collective-permute-start.3 = (bf16[576,128]{1,0:T(8,128)(2,1)S(1)}, bf16[576,128]{1,0:T(8,128)(2,1)S(1)}, u32[]{:S(2)}, u32[]{:S(2)}) collective-permute-start(bf16[576,128]{1,0:T(8,128)(2,1)S(1)} %get-tuple-element.29.refs_0_), channel_id=1, source_target_pairs={{0,8},{8,0},{1,9},{9,1},{2,10},{10,2},{3,11},{11,3},{4,12},{12,4},... | collective-permute-start | bytes 442376 | tf_op jit(solution)/shard_map/ppermute | solution.py:29
  18.4 5.3 %collective-permute-start.4 = (bf16[576,128]{1,0:T(8,128)(2,1)S(1)}, bf16[576,128]{1,0:T(8,128)(2,1)S(1)}, u32[]{:S(2)}, u32[]{:S(2)}) collective-permute-start(bf16[576,128]{1,0:T(8,128)(2,1)S(1)} %collective-permute-done.refs_1_), channel_id=1, source_target_pairs={{0,8},{8,0},{1,9},{9,1},{2,10},{10,2},{3,11},{11,3},{4,12},{12,4},... | collective-permute-start | bytes 442376 | tf_op jit(solution)/shard_map/ppermute | solution.py:29
  22.2 2.5 %collective-permute-start.5 = (bf16[576,128]{1,0:T(8,128)(2,1)S(1)}, bf16[576,128]{1,0:T(8,128)(2,1)S(1)}, u32[]{:S(2)}, u32[]{:S(2)}) collective-permute-start(bf16[576,128]{1,0:T(8,128)(2,1)S(1)} %collective-permute-done.1.refs_2_), channel_id=1, source_target_pairs={{0,8},{8,0},{1,9},{9,1},{2,10},{10,2},{3,11},{11,3},{4,12},{12,4},... | collective-permute-start | bytes 442376 | tf_op jit(solution)/shard_map/ppermute | solution.py:29
  23.7 1.4 collective-permute-start.6
  26.2 15.5 %collective-permute-start.7 = (bf16[576,256]{1,0:T(8,128)(2,1)S(1)}, bf16[576,256]{1,0:T(8,128)(2,1)S(1)}, u32[]{:S(2)}, u32[]{:S(2)}) collective-permute-start(bf16[576,256]{1,0:T(8,128)(2,1)S(1)} %get-tuple-element.34), channel_id=1, source_target_pairs={{0,16},{16,0},{1,17},{17,1},{2,18},{18,2},{3,19},{19,3},{4,20},{20... | collective-permute-start | bytes 884744 | tf_op jit(solution)/shard_map/ppermute | solution.py:29
  42.5 21.9 %collective-permute-start.8 = (bf16[576,256]{1,0:T(8,128)(2,1)S(1)}, bf16[576,256]{1,0:T(8,128)(2,1)S(1)}, u32[]{:S(2)}, u32[]{:S(2)}) collective-permute-start(bf16[576,256]{1,0:T(8,128)(2,1)S(1)} %shard_map.102.refs_0_), channel_id=1, source_target_pairs={{0,2},{2,4},{4,6},{6,0},{1,3},{3,5},{5,7},{7,1},{8,10},{10,12},{12... | collective-permute-start | bytes 884744 | tf_op jit(solution)/shard_map/ppermute | solution.py:29
  44.2 16.5 %collective-permute-start.11 = (bf16[576,256]{1,0:T(8,128)(2,1)S(1)}, bf16[576,256]{1,0:T(8,128)(2,1)S(1)}, u32[]{:S(2)}, u32[]{:S(2)}) collective-permute-start(bf16[576,256]{1,0:T(8,128)(2,1)S(1)} %shard_map.102.refs_0_), channel_id=1, source_target_pairs={{0,1},{1,0},{2,3},{3,2},{4,5},{5,4},{6,7},{7,6},{8,9},{9,8},{10,11... | collective-permute-start | bytes 884744 | tf_op jit(solution)/shard_map/ppermute | solution.py:29
  47.2 19.9 %collective-permute-start.9 = (bf16[576,256]{1,0:T(8,128)(2,1)S(1)}, bf16[576,256]{1,0:T(8,128)(2,1)S(1)}, u32[]{:S(2)}, u32[]{:S(2)}) collective-permute-start(bf16[576,256]{1,0:T(8,128)(2,1)S(1)} %shard_map.102.refs_0_), channel_id=1, source_target_pairs={{0,4},{2,6},{4,0},{6,2},{1,5},{3,7},{5,1},{7,3},{8,12},{10,14},{12... | collective-permute-start | bytes 884744 | tf_op jit(solution)/shard_map/ppermute | solution.py:29
  50.8 16.3 %collective-permute-start.10 = (bf16[576,256]{1,0:T(8,128)(2,1)S(1)}, bf16[576,256]{1,0:T(8,128)(2,1)S(1)}, u32[]{:S(2)}, u32[]{:S(2)}) collective-permute-start(bf16[576,256]{1,0:T(8,128)(2,1)S(1)} %shard_map.102.refs_0_), channel_id=1, source_target_pairs={{0,6},{2,0},{4,2},{6,4},{1,7},{3,1},{5,3},{7,5},{8,14},{10,8},{12,... | collective-permute-start | bytes 884744 | tf_op jit(solution)/shard_map/ppermute | solution.py:29
  60.7 7.9 %collective-permute-start.12 = (bf16[576,256]{1,0:T(8,128)(2,1)S(1)}, bf16[576,256]{1,0:T(8,128)(2,1)S(1)}, u32[]{:S(2)}, u32[]{:S(2)}) collective-permute-start(bf16[576,256]{1,0:T(8,128)(2,1)S(1)} %collective-permute-done.11.refs_4_), channel_id=1, source_target_pairs={{0,2},{2,4},{4,6},{6,0},{1,3},{3,5},{5,7},{7,1},{8,10},{10,12},{12... | collective-permute-start | bytes 884744 | tf_op jit(solution)/shard_map/ppermute | solution.py:29
  62.4 14.0 %collective-permute-start.13 = (bf16[576,256]{1,0:T(8,128)(2,1)S(1)}, bf16[576,256]{1,0:T(8,128)(2,1)S(1)}, u32[]{:S(2)}, u32[]{:S(2)}) collective-permute-start(bf16[576,256]{1,0:T(8,128)(2,1)S(1)} %collective-permute-done.11.refs_4_), channel_id=1, source_target_pairs={{0,4},{2,6},{4,0},{6,2},{1,5},{3,7},{5,1},{7,3},{8,12},{10,14},{12... | collective-permute-start | bytes 884744 | tf_op jit(solution)/shard_map/ppermute | solution.py:29
  64.4 11.9 %collective-permute-start.14 = (bf16[576,256]{1,0:T(8,128)(2,1)S(1)}, bf16[576,256]{1,0:T(8,128)(2,1)S(1)}, u32[]{:S(2)}, u32[]{:S(2)}) collective-permute-start(bf16[576,256]{1,0:T(8,128)(2,1)S(1)} %collective-permute-done.11.refs_4_), channel_id=1, source_target_pairs={{0,6},{2,0},{4,2},{6,4},{1,7},{3,1},{5,3},{7,5},{8,14},{10,8},{12,... | collective-permute-start | bytes 884744 | tf_op jit(solution)/shard_map/ppermute | solution.py:29
  85.3 8.9 %collective-permute-start.15 = (bf16[256,512]{1,0:T(8,128)(2,1)S(1)}, bf16[256,512]{1,0:T(8,128)(2,1)S(1)}, u32[]{:S(2)}, u32[]{:S(2)}) collective-permute-start(bf16[256,512]{1,0:T(8,128)(2,1)S(1)} %key_value.1.refs_0_), channel_id=1, source_target_pairs={{0,32},{32,64},{64,96},{96,0},{1,33},{33,65},{65,97},{97,1},{2,34}... | collective-permute-start | bytes 786440 | tf_op jit(solution)/shard_map/ppermute | solution.py:29
  85.4 18.8 %collective-permute-start.16 = (bf16[256,512]{1,0:T(8,128)(2,1)S(1)}, bf16[256,512]{1,0:T(8,128)(2,1)S(1)}, u32[]{:S(2)}, u32[]{:S(2)}) collective-permute-start(bf16[256,512]{1,0:T(8,128)(2,1)S(1)} %key_value.1.refs_0_), channel_id=1, source_target_pairs={{0,64},{32,96},{64,0},{96,32},{1,65},{33,97},{65,1},{97,33},{2,66}... | collective-permute-start | bytes 786440 | tf_op jit(solution)/shard_map/ppermute | solution.py:29
  88.9 17.9 %collective-permute-start.22 = (bf16[256,512]{1,0:T(8,128)(2,1)S(1)}, bf16[256,512]{1,0:T(8,128)(2,1)S(1)}, u32[]{:S(2)}, u32[]{:S(2)}) collective-permute-start(bf16[256,512]{1,0:T(8,128)(2,1)S(1)} %key_value.1.refs_0_), channel_id=1, source_target_pairs={{0,16},{16,0},{1,17},{17,1},{2,18},{18,2},{3,19},{19,3},{4,20},{20... | collective-permute-start | bytes 786440 | tf_op jit(solution)/shard_map/ppermute | solution.py:29
  89.3 17.6 %collective-permute-start.17 = (bf16[256,512]{1,0:T(8,128)(2,1)S(1)}, bf16[256,512]{1,0:T(8,128)(2,1)S(1)}, u32[]{:S(2)}, u32[]{:S(2)}) collective-permute-start(bf16[256,512]{1,0:T(8,128)(2,1)S(1)} %key_value.1.refs_0_), channel_id=1, source_target_pairs={{0,96},{32,0},{64,32},{96,64},{1,97},{33,1},{65,33},{97,65},{2,98}... | collective-permute-start | bytes 786440 | tf_op jit(solution)/shard_map/ppermute | solution.py:29
  89.3 17.9 %collective-permute-start.18 = (bf16[256,512]{1,0:T(8,128)(2,1)S(1)}, bf16[256,512]{1,0:T(8,128)(2,1)S(1)}, u32[]{:S(2)}, u32[]{:S(2)}) collective-permute-start(bf16[256,512]{1,0:T(8,128)(2,1)S(1)} %key_value.1.refs_0_), channel_id=1, source_target_pairs={{0,8},{8,0},{1,9},{9,1},{2,10},{10,2},{3,11},{11,3},{4,12},{12,4},... | collective-permute-start | bytes 786440 | tf_op jit(solution)/shard_map/ppermute | solution.py:29
  94.2 15.4 %collective-permute-start.19 = (bf16[256,512]{1,0:T(8,128)(2,1)S(1)}, bf16[256,512]{1,0:T(8,128)(2,1)S(1)}, u32[]{:S(2)}, u32[]{:S(2)}) collective-permute-start(bf16[256,512]{1,0:T(8,128)(2,1)S(1)} %collective-permute-done.15.refs_1_), channel_id=1, source_target_pairs={{0,8},{8,0},{1,9},{9,1},{2,10},{10,2},{3,11},{11,3},{4,12},{12,4},... | collective-permute-start | bytes 786440 | tf_op jit(solution)/shard_map/ppermute | solution.py:29
  104.2 5.9 %collective-permute-start.20 = (bf16[256,512]{1,0:T(8,128)(2,1)S(1)}, bf16[256,512]{1,0:T(8,128)(2,1)S(1)}, u32[]{:S(2)}, u32[]{:S(2)}) collective-permute-start(bf16[256,512]{1,0:T(8,128)(2,1)S(1)} %collective-permute-done.16.refs_2_), channel_id=1, source_target_pairs={{0,8},{8,0},{1,9},{9,1},{2,10},{10,2},{3,11},{11,3},{4,12},{12,4},... | collective-permute-start | bytes 786440 | tf_op jit(solution)/shard_map/ppermute | solution.py:29
  106.8 11.0 %collective-permute-start.23 = (bf16[256,512]{1,0:T(8,128)(2,1)S(1)}, bf16[256,512]{1,0:T(8,128)(2,1)S(1)}, u32[]{:S(2)}, u32[]{:S(2)}) collective-permute-start(bf16[256,512]{1,0:T(8,128)(2,1)S(1)} %collective-permute-done.22.refs_8_), channel_id=1, source_target_pairs={{0,32},{32,64},{64,96},{96,0},{1,33},{33,65},{65,97},{97,1},{2,34}... | collective-permute-start | bytes 786440 | tf_op jit(solution)/shard_map/ppermute | solution.py:29
  106.8 13.7 %collective-permute-start.24 = (bf16[256,512]{1,0:T(8,128)(2,1)S(1)}, bf16[256,512]{1,0:T(8,128)(2,1)S(1)}, u32[]{:S(2)}, u32[]{:S(2)}) collective-permute-start(bf16[256,512]{1,0:T(8,128)(2,1)S(1)} %collective-permute-done.16.refs_2_), channel_id=1, source_target_pairs={{0,16},{16,0},{1,17},{17,1},{2,18},{18,2},{3,19},{19,3},{4,20},{20... | collective-permute-start | bytes 786440 | tf_op jit(solution)/shard_map/ppermute | solution.py:29
  107.1 15.3 %collective-permute-start.25 = (bf16[256,512]{1,0:T(8,128)(2,1)S(1)}, bf16[256,512]{1,0:T(8,128)(2,1)S(1)}, u32[]{:S(2)}, u32[]{:S(2)}) collective-permute-start(bf16[256,512]{1,0:T(8,128)(2,1)S(1)} %collective-permute-done.22.refs_8_), channel_id=1, source_target_pairs={{0,96},{32,0},{64,32},{96,64},{1,97},{33,1},{65,33},{97,65},{2,98}... | collective-permute-start | bytes 786440 | tf_op jit(solution)/shard_map/ppermute | solution.py:29
  109.6 16.5 %collective-permute-start.26 = (bf16[256,512]{1,0:T(8,128)(2,1)S(1)}, bf16[256,512]{1,0:T(8,128)(2,1)S(1)}, u32[]{:S(2)}, u32[]{:S(2)}) collective-permute-start(bf16[256,512]{1,0:T(8,128)(2,1)S(1)} %collective-permute-done.22.refs_8_), channel_id=1, source_target_pairs={{0,8},{8,0},{1,9},{9,1},{2,10},{10,2},{3,11},{11,3},{4,12},{12,4},... | collective-permute-start | bytes 786440 | tf_op jit(solution)/shard_map/ppermute | solution.py:29
  110.2 15.9 %collective-permute-start.21 = (bf16[256,512]{1,0:T(8,128)(2,1)S(1)}, bf16[256,512]{1,0:T(8,128)(2,1)S(1)}, u32[]{:S(2)}, u32[]{:S(2)}) collective-permute-start(bf16[256,512]{1,0:T(8,128)(2,1)S(1)} %collective-permute-done.17.refs_3_), channel_id=1, source_target_pairs={{0,8},{8,0},{1,9},{9,1},{2,10},{10,2},{3,11},{11,3},{4,12},{12,4},... | collective-permute-start | bytes 786440 | tf_op jit(solution)/shard_map/ppermute | solution.py:29
  117.8 8.2 %collective-permute-start.27 = (bf16[256,512]{1,0:T(8,128)(2,1)S(1)}, bf16[256,512]{1,0:T(8,128)(2,1)S(1)}, u32[]{:S(2)}, u32[]{:S(2)}) collective-permute-start(bf16[256,512]{1,0:T(8,128)(2,1)S(1)} %collective-permute-done.23.refs_9_), channel_id=1, source_target_pairs={{0,8},{8,0},{1,9},{9,1},{2,10},{10,2},{3,11},{11,3},{4,12},{12,4},... | collective-permute-start | bytes 786440 | tf_op jit(solution)/shard_map/ppermute | solution.py:29
  120.5 5.5 %collective-permute-start.28 = (bf16[256,512]{1,0:T(8,128)(2,1)S(1)}, bf16[256,512]{1,0:T(8,128)(2,1)S(1)}, u32[]{:S(2)}, u32[]{:S(2)}) collective-permute-start(bf16[256,512]{1,0:T(8,128)(2,1)S(1)} %collective-permute-done.24.refs_10_), channel_id=1, source_target_pairs={{0,8},{8,0},{1,9},{9,1},{2,10},{10,2},{3,11},{11,3},{4,12},{12,4},... | collective-permute-start | bytes 786440 | tf_op jit(solution)/shard_map/ppermute | solution.py:29
  122.5 3.6 %collective-permute-start.29 = (bf16[256,512]{1,0:T(8,128)(2,1)S(1)}, bf16[256,512]{1,0:T(8,128)(2,1)S(1)}, u32[]{:S(2)}, u32[]{:S(2)}) collective-permute-start(bf16[256,512]{1,0:T(8,128)(2,1)S(1)} %collective-permute-done.25.refs_11_), channel_id=1, source_target_pairs={{0,8},{8,0},{1,9},{9,1},{2,10},{10,2},{3,11},{11,3},{4,12},{12,4},... | collective-permute-start | bytes 786440 | tf_op jit(solution)/shard_map/ppermute | solution.py:29
  135.8 9.4 %collective-permute-start.30 = (bf16[32,4608]{1,0:T(8,128)(2,1)S(1)}, bf16[32,4608]{1,0:T(8,128)(2,1)S(1)}, u32[]{:S(2)}, u32[]{:S(2)}) collective-permute-start(bf16[32,4608]{1,0:T(8,128)(2,1)S(1)} %get-tuple-element.38), channel_id=1, source_target_pairs={{0,2},{2,4},{4,6},{6,0},{1,3},{3,5},{5,7},{7,1},{8,10},{10,12},{12... | collective-permute-start | bytes 884744 | tf_op jit(solution)/shard_map/ppermute | solution.py:29
  137.2 25.1 %collective-permute-start.31 = (bf16[32,4608]{1,0:T(8,128)(2,1)S(1)}, bf16[32,4608]{1,0:T(8,128)(2,1)S(1)}, u32[]{:S(2)}, u32[]{:S(2)}) collective-permute-start(bf16[32,4608]{1,0:T(8,128)(2,1)S(1)} %get-tuple-element.39), channel_id=1, source_target_pairs={{0,4},{2,6},{4,0},{6,2},{1,5},{3,7},{5,1},{7,3},{8,12},{10,14},{12... | collective-permute-start | bytes 884744 | tf_op jit(solution)/shard_map/ppermute | solution.py:29
  139.7 22.5 %collective-permute-start.32 = (bf16[32,4608]{1,0:T(8,128)(2,1)S(1)}, bf16[32,4608]{1,0:T(8,128)(2,1)S(1)}, u32[]{:S(2)}, u32[]{:S(2)}) collective-permute-start(bf16[32,4608]{1,0:T(8,128)(2,1)S(1)} %get-tuple-element.40), channel_id=1, source_target_pairs={{0,6},{2,0},{4,2},{6,4},{1,7},{3,1},{5,3},{7,5},{8,14},{10,8},{12,... | collective-permute-start | bytes 884744 | tf_op jit(solution)/shard_map/ppermute | solution.py:29
  140.8 21.4 %collective-permute-start.33 = (bf16[32,4608]{1,0:T(8,128)(2,1)S(1)}, bf16[32,4608]{1,0:T(8,128)(2,1)S(1)}, u32[]{:S(2)}, u32[]{:S(2)}) collective-permute-start(bf16[32,4608]{1,0:T(8,128)(2,1)S(1)} %get-tuple-element.41), channel_id=1, source_target_pairs={{0,1},{1,0},{2,3},{3,2},{4,5},{5,4},{6,7},{7,6},{8,9},{9,8},{10,11... | collective-permute-start | bytes 884744 | tf_op jit(solution)/shard_map/ppermute | solution.py:29
  143.3 19.0 %collective-permute-start.34 = (bf16[32,4608]{1,0:T(8,128)(2,1)S(1)}, bf16[32,4608]{1,0:T(8,128)(2,1)S(1)}, u32[]{:S(2)}, u32[]{:S(2)}) collective-permute-start(bf16[32,4608]{1,0:T(8,128)(2,1)S(1)} %get-tuple-element.42), channel_id=1, source_target_pairs={{0,3},{1,2},{2,5},{3,4},{4,7},{5,6},{6,1},{7,0},{8,11},{9,10},{10,... | collective-permute-start | bytes 884744 | tf_op jit(solution)/shard_map/ppermute | solution.py:483
  145.3 17.0 %collective-permute-start.35 = (bf16[32,4608]{1,0:T(8,128)(2,1)S(1)}, bf16[32,4608]{1,0:T(8,128)(2,1)S(1)}, u32[]{:S(2)}, u32[]{:S(2)}) collective-permute-start(bf16[32,4608]{1,0:T(8,128)(2,1)S(1)} %get-tuple-element.43), channel_id=1, source_target_pairs={{0,5},{1,4},{2,7},{3,6},{4,1},{5,0},{6,3},{7,2},{8,13},{9,12},{10,... | collective-permute-start | bytes 884744 | tf_op jit(solution)/shard_map/ppermute | solution.py:483
  162.2 8.3 %collective-permute-start.36 = (bf16[32,4608]{1,0:T(8,128)(2,1)S(1)}, bf16[32,4608]{1,0:T(8,128)(2,1)S(1)}, u32[]{:S(2)}, u32[]{:S(2)}) collective-permute-start(bf16[32,4608]{1,0:T(8,128)(2,1)S(1)} %get-tuple-element.44), channel_id=1, source_target_pairs={{0,7},{1,6},{2,1},{3,0},{4,3},{5,2},{6,5},{7,4},{8,15},{9,14},{10,... | collective-permute-start | bytes 884744 | tf_op jit(solution)/shard_map/ppermute | solution.py:483
  171.0 12.4 %collective-permute-start.38 = (bf16[32,4608]{1,0:T(8,128)(2,1)S(1)}, bf16[32,4608]{1,0:T(8,128)(2,1)S(1)}, u32[]{:S(2)}, u32[]{:S(2)}) collective-permute-start(bf16[32,4608]{1,0:T(8,128)(2,1)S(1)} %finish.1.refs_0_), channel_id=1, source_target_pairs={{0,16},{16,0},{1,17},{17,1},{2,18},{18,2},{3,19},{19,3},{4,20},{20... | collective-permute-start | bytes 884744 | tf_op jit(solution)/shard_map/ppermute | solution.py:29
  178.0 8.0 %collective-permute-start.37 = (bf16[32,4608]{1,0:T(8,128)(2,1)S(1)}, bf16[32,4608]{1,0:T(8,128)(2,1)S(1)}, u32[]{:S(2)}, u32[]{:S(2)}) collective-permute-start(bf16[32,4608]{1,0:T(8,128)(2,1)S(1)} %finish.1.refs_0_), channel_id=1, source_target_pairs={{0,8},{8,0},{1,9},{9,1},{2,10},{10,2},{3,11},{11,3},{4,12},{12,4},... | collective-permute-start | bytes 884744 | tf_op jit(solution)/shard_map/ppermute | solution.py:29
  183.4 3.8 %collective-permute-start.39 = (bf16[32,4608]{1,0:T(8,128)(2,1)S(1)}, bf16[32,4608]{1,0:T(8,128)(2,1)S(1)}, u32[]{:S(2)}, u32[]{:S(2)}) collective-permute-start(bf16[32,4608]{1,0:T(8,128)(2,1)S(1)} %collective-permute-done.38.refs_2_), channel_id=1, source_target_pairs={{0,8},{8,0},{1,9},{9,1},{2,10},{10,2},{3,11},{11,3},{4,12},{12,4},... | collective-permute-start | bytes 884744 | tf_op jit(solution)/shard_map/ppermute | solution.py:29
  188.1 9.6 %collective-permute-start.40 = (bf16[16,4608]{1,0:T(8,128)(2,1)S(1)}, bf16[16,4608]{1,0:T(8,128)(2,1)S(1)}, u32[]{:S(2)}, u32[]{:S(2)}) collective-permute-start(bf16[16,4608]{1,0:T(8,128)(2,1)S(1)} %get-tuple-element.46), channel_id=1, source_target_pairs={{0,32},{32,64},{64,96},{96,0},{1,33},{33,65},{65,97},{97,1},{2,34}... | collective-permute-start | bytes 442376 | tf_op jit(solution)/shard_map/ppermute | solution.py:29
  188.2 9.5 %collective-permute-start.41 = (bf16[16,4608]{1,0:T(8,128)(2,1)S(1)}, bf16[16,4608]{1,0:T(8,128)(2,1)S(1)}, u32[]{:S(2)}, u32[]{:S(2)}) collective-permute-start(bf16[16,4608]{1,0:T(8,128)(2,1)S(1)} %get-tuple-element.47), channel_id=1, source_target_pairs={{0,64},{32,96},{64,0},{96,32},{1,65},{33,97},{65,1},{97,33},{2,66}... | collective-permute-start | bytes 442376 | tf_op jit(solution)/shard_map/ppermute | solution.py:29
  188.9 9.0 %collective-permute-start.42 = (bf16[16,4608]{1,0:T(8,128)(2,1)S(1)}, bf16[16,4608]{1,0:T(8,128)(2,1)S(1)}, u32[]{:S(2)}, u32[]{:S(2)}) collective-permute-start(bf16[16,4608]{1,0:T(8,128)(2,1)S(1)} %get-tuple-element.48), channel_id=1, source_target_pairs={{0,96},{32,0},{64,32},{96,64},{1,97},{33,1},{65,33},{97,65},{2,98}... | collective-permute-start | bytes 442376 | tf_op jit(solution)/shard_map/ppermute | solution.py:29
  198.7 6.7 %collective-permute-start.43 = (bf16[16,4608]{1,0:T(8,128)(2,1)S(1)}, bf16[16,4608]{1,0:T(8,128)(2,1)S(1)}, u32[]{:S(2)}, u32[]{:S(2)}) collective-permute-start(bf16[16,4608]{1,0:T(8,128)(2,1)S(1)} %get-tuple-element.50), channel_id=1, source_target_pairs={{0,2},{2,4},{4,6},{6,0},{1,3},{3,5},{5,7},{7,1},{8,10},{10,12},{12... | collective-permute-start | bytes 442376 | tf_op jit(solution)/shard_map/ppermute | solution.py:29
  198.8 7.6 %collective-permute-start.44 = (bf16[16,4608]{1,0:T(8,128)(2,1)S(1)}, bf16[16,4608]{1,0:T(8,128)(2,1)S(1)}, u32[]{:S(2)}, u32[]{:S(2)}) collective-permute-start(bf16[16,4608]{1,0:T(8,128)(2,1)S(1)} %get-tuple-element.51), channel_id=1, source_target_pairs={{0,4},{2,6},{4,0},{6,2},{1,5},{3,7},{5,1},{7,3},{8,12},{10,14},{12... | collective-permute-start | bytes 442376 | tf_op jit(solution)/shard_map/ppermute | solution.py:29
  201.1 6.4 %collective-permute-start.45 = (bf16[16,4608]{1,0:T(8,128)(2,1)S(1)}, bf16[16,4608]{1,0:T(8,128)(2,1)S(1)}, u32[]{:S(2)}, u32[]{:S(2)}) collective-permute-start(bf16[16,4608]{1,0:T(8,128)(2,1)S(1)} %get-tuple-element.52), channel_id=1, source_target_pairs={{0,6},{2,0},{4,2},{6,4},{1,7},{3,1},{5,3},{7,5},{8,14},{10,8},{12,... | collective-permute-start | bytes 442376 | tf_op jit(solution)/shard_map/ppermute | solution.py:29
  (2 other events, 96.5 us)
Sparse Core Ops, SparseCore 0:
  9.0 73.1 all-gather.2
  84.0 46.9 all-gather.4
where the time goes:
time: 218 us; the launch traced here: 216 us
  waiting for transfers between devices  104 us (48%)
  starting transfers between devices  70.3 us (32%)
  Pallas kernels  26 us (12%)
  between operations  13.8 us (6%)
    ppermute x43, waiting for transfers between devices, shift(): return lax.ppermute(value, axis, [(i, (i + by) % n) for i in range(n)])  90.4 us
    ppermute x43, starting transfers between devices, shift(): return lax.ppermute(value, axis, [(i, (i + by) % n) for i in range(n)])  65.4 us
    ppermute x3, waiting for transfers between devices, per_device(): lax.ppermute(part, TP, [(2 * i + j, 2 * ((i + dz) % 4) + (j ^ dy)) for i,...  8.21 us
    pallas_call x1, Pallas kernels, per_device(): pl.pallas_call(attention_kernel, in_specs=[SMEM] + [VMEM] * 17, out_specs...  5.43 us
    ppermute x3, starting transfers between devices, per_device(): lax.ppermute(part, TP, [(2 * i + j, 2 * ((i + dz) % 4) + (j ^ dy)) for i,...  4.89 us
    all_gather x1, waiting for transfers between devices, per_device(): qkv_full = lax.all_gather(joined, SEQ, axis=0, tiled=True)  4.82 us
  transfers between devices with their start and end apart: 48, of which 22 were waited for; matrix products, arithmetic and copies ran while one was open for 0% of the time, Pallas kernels for 8%

commit v1 on v0

--- a/solution.py
+++ b/solution.py
@@ -93,6 +93,21 @@
         jobs.append((source.at[:, first : first + width], joined.at[:, at : at + width]))
         at += width
     fetch(jobs, sems)
+
+
+def hold_kernel(source, after, target, sems):
+    del after
+    fetch([(source, target)], sems)
+
+
+def pack_kernel(flat, *refs):
+    parts, whole = refs[:16], refs[16]
+    x, yl, c, _, _ = spot(flat)
+    size = parts[0].shape[0]
+    for n, part in enumerate(parts):
+        w = jnp.bitwise_xor(2 * yl + c, n // 4)
+        first = (4 * jnp.bitwise_and(x - n % 4, 3) + w) * size
+        whole[pl.ds(pl.multiple_of(first, 32), size), :] = part[...]
 
 
 def leave_kernel(flat, old_blocks, order, x_old, *refs):
@@ -256,24 +271,15 @@
 
 
 def out_kernel(flat, context, weight, *refs):
-    outs, (buffer, scratch, sems) = refs[:8], refs[8:]
+    outs, scratch = refs[:8], refs[8]
     _, _, _, z, yh = spot(flat)
-    tile, steps = scratch.shape[1], sems.shape[0]
-
-    def copy(n):
-        rows = pl.ds(pl.multiple_of(n * tile, tile), tile)
-        return pltpu.make_async_copy(weight.at[rows, :], buffer.at[rows, :], sems.at[n])
-
-    @pl.loop(0, steps)
+    tile = scratch.shape[1]
+
+    @pl.loop(0, weight.shape[0] // tile)
     def _(n):
-        copy(n).start()
-
-    @pl.loop(0, steps)
-    def _(n):
-        copy(n).wait()
         cols = pl.ds(pl.multiple_of(n * tile, tile), tile)
         scratch[...] = lax.dot_general(
-            context[...], buffer[cols, :], (((1,), (1,)), ((), ())), preferred_element_type=F32
+            context[...], weight[cols, :], (((1,), (1,)), ((), ())), preferred_element_type=F32
         ).astype(BF16)
         for dy in range(2):
             for dz in range(4):
@@ -371,6 +377,17 @@
         )(*tables, *far_off(arrays))
         return list(results)
 
+    def everywhere(part):
+        opposite = shift(part, "x", 2)
+        pair = shift(part, "yl", 1)
+        same = [part, shift(part, "x", 1), opposite, shift(part, "x", 3)]
+        other = [pair, shift(pair, "x", 1), shift(opposite, "yl", 1), shift(pair, "x", 3)]
+        result = []
+        for parts in (same, other):
+            result += parts
+            result += [shift(s, "c", 1) for s in parts]
+        return result
+
     (joined,) = bring(
         join_kernel,
         (),
@@ -380,7 +397,6 @@
         jax.ShapeDtypeStruct,
     )
     qkv_full = lax.all_gather(joined, SEQ, axis=0, tiled=True)
-    out_full = lax.all_gather(w_out_t, SEQ, axis=0, tiled=True)
 
     old = far_off((old_blocks, order))
     near = bring(leave_kernel, (flat, *old), (x_old.T,), [(width, BLOCK)] * 4, 4, pltpu.VMEM)
@@ -389,6 +405,17 @@
     mine, cross = call(sort_kernel, old, near + far, [(width, count)] * 2)
     cross = shift(cross, "yl", 1)
     (rows,) = call(settle_kernel, old, (mine, cross), [(width, count)])
+
+    (held,) = pl.pallas_call(
+        hold_kernel,
+        in_specs=[AWAY, VMEM],
+        out_specs=[VMEM],
+        out_shape=[pltpu.VMEM(w_out_t.shape, BF16)],
+        scratch_shapes=[pltpu.SemaphoreType.DMA((1,))],
+        compiler_params=grant(8),
+        name="hold",
+    )(*far_off((w_out_t,)), *near_by((rows,)))
+    spread_out = everywhere(held)
 
     facing = shift(rows, "yh", 1)
     pieces = [rows] + [shift(rows, "z", d) for d in range(1, 4)]
@@ -440,16 +467,10 @@
         name="key_value",
     )(*near_by((normed,)), *far_off((qkv_full,)), *tables)
 
-    opposite = shift(kv, "x", 2)
-    same = [kv, shift(kv, "x", 1), opposite, shift(kv, "x", 3)]
-    pair = shift(kv, "yl", 1)
-    other = [pair, shift(pair, "x", 1), shift(same[2], "yl", 1), shift(pair, "x", 3)]
-    spread = []
-    for part in (same, other):
-        spread += part
-        spread += [shift(s, "c", 1) for s in part]
+    spread = everywhere(kv)
 
     query = heads(query_kernel, 2)
+    (out_full,) = call(pack_kernel, (), spread_out, [(D, 4 * HEAD)])
     context = pl.pallas_call(
         attention_kernel,
         in_specs=[SMEM] + [VMEM] * 17,
@@ -463,17 +484,13 @@
     tile = 512
     shares = pl.pallas_call(
         out_kernel,
-        in_specs=[SMEM, VMEM, AWAY],
+        in_specs=[SMEM, VMEM, VMEM],
         out_specs=[VMEM] * 8,
         out_shape=[pltpu.VMEM((32, D), BF16)] * 8,
-        scratch_shapes=[
-            pltpu.VMEM((D, 4 * HEAD), BF16),
-            pltpu.VMEM((count, tile), BF16),
-            pltpu.SemaphoreType.DMA((D // tile,)),
-        ],
+        scratch_shapes=[pltpu.VMEM((count, tile), BF16)],
         compiler_params=grant(16),
         name="project",
-    )(flat, *near_by((context,)), *far_off((out_full,)))
+    )(flat, *near_by((context, out_full)))
     received = []
     for dy in range(2):
         for dz in range(4):

time: 218 us -> 234 us (1.073)
  local copies, waits for them, and re-layouts: 0.86 us -> 14.8 us
  starting transfers between devices: 70.3 us -> 80.8 us
  waiting for transfers between devices: 104 us -> 94.8 us
    unnamed x5 -> x53, local copies, waits for them, and re-layouts: 0.83 us -> 14.7 us
    ppermute x43 -> x58, starting transfers between devices: 65.4 us -> 78.3 us  [shift(): return lax.ppermute(value, axis, [(i, (i + by) % n) for i in range(n)])]
    ppermute x43 -> x58, waiting for transfers between devices: 90.4 us -> 83.7 us  [shift(): return lax.ppermute(value, axis, [(i, (i + by) % n) for i in range(n)])]
    all_gather x1, waiting for transfers between devices: 4.82 us -> 0.01 us  [per_device(): qkv_full = lax.all_gather(joined, SEQ, axis=0, tiled=True)]
    ppermute x3, waiting for transfers between devices: 8.21 us -> 11.1 us  [per_device(): lax.ppermute(part, TP, [(2 * i + j, 2 * ((i + dz) % 4) + (j ^ dy)) for i,...]
    ppermute x3, starting transfers between devices: 4.89 us -> 2.44 us  [per_device(): lax.ppermute(part, TP, [(2 * i + j, 2 * ((i + dz) % 4) + (j ^ dy)) for i,...]
    pallas_call x5 -> x6, Pallas kernels: 4.34 us -> 6.42 us  [call(): pl.pallas_call(kernel, in_specs=[SMEM] * (1 + len(tables)) + [VMEM] * len...]
  transfers between devices with their start and end apart: 48 -> 62, of which waited for: 22 -> 22; matrix products, arithmetic and copies ran while one was open for 0% -> 0% of each run, Pallas kernels for 8% -> 6%
where the time goes in v1:
time: 234 us; the launch traced here: 233 us
  waiting for transfers between devices  94.8 us (41%)
  starting transfers between devices  80.8 us (35%)
  Pallas kernels  28 us (12%)
  local copies, waits for them, and re-layouts  14.8 us (6%)
  between operations  13.8 us (6%)
    ppermute x58, waiting for transfers between devices, shift(): return lax.ppermute(value, axis, [(i, (i + by) % n) for i in range(n)])  83.7 us
    ppermute x58, starting transfers between devices, shift(): return lax.ppermute(value, axis, [(i, (i + by) % n) for i in range(n)])  78.3 us
    unnamed x53, local copies, waits for them, and re-layouts  14.7 us
    ppermute x3, waiting for transfers between devices, per_device(): lax.ppermute(part, TP, [(2 * i + j, 2 * ((i + dz) % 4) + (j ^ dy)) for i,...  11.1 us
    pallas_call x6, Pallas kernels, call(): pl.pallas_call(kernel, in_specs=[SMEM] * (1 + len(tables)) + [VMEM] * len...  6.42 us
    pallas_call x1, Pallas kernels, per_device(): pl.pallas_call(attention_kernel, in_specs=[SMEM] + [VMEM] * 17, out_specs...  5.43 us
  transfers between devices with their start and end apart: 62, of which 22 were waited for; matrix products, arithmetic and copies ran while one was open for 0% of the time, Pallas kernels for 6%

profile of v1, /device:TPU:1, one launch (start us, length us, event | category | flops | bytes accessed | tf_op | source)
XLA Modules:
  0.0 232.9 jit_solution(8280345130128549406)
XLA Ops:
  6.5 2.0 shard_map.103
  8.6 1.9 shard_map.100
  10.4 2.1 collective-permute-start
  12.5 2.5 %collective-permute-start.1 = (bf16[576,128]{1,0:T(8,128)(2,1)S(1)}, bf16[576,128]{1,0:T(8,128)(2,1)S(1)}, u32[]{:S(2)}, u32[]{:S(2)}) collective-permute-start(bf16[576,128]{1,0:T(8,128)(2,1)S(1)} %get-tuple-element.31), channel_id=1, source_target_pairs={{0,64},{32,96},{64,0},{96,32},{1,65},{33,97},{65,1},{97,33},{2,66}... | collective-permute-start | bytes 442376 | tf_op jit(solution)/shard_map/ppermute | solution.py:29
  16.1 1.5 collective-permute-start.3
  18.6 2.8 %collective-permute-done.1.refs_2_ = bf16[576,128]{1,0:T(8,128)(2,1)S(1)} collective-permute-done((bf16[576,128]{1,0:T(8,128)(2,1)S(1)}, bf16[576,128]{1,0:T(8,128)(2,1)S(1)}, u32[]{:S(2)}, u32[]{:S(2)}) %collective-permute-start.1) | collective-permute-done | bytes 147488 | tf_op jit(solution)/shard_map/ppermute | solution.py:29
  21.4 1.5 collective-permute-start.5
  25.4 1.4 collective-permute-start.7
  26.8 14.1 %collective-permute-done.7.crossed = bf16[576,256]{1,0:T(8,128)(2,1)S(1)} collective-permute-done((bf16[576,256]{1,0:T(8,128)(2,1)S(1)}, bf16[576,256]{1,0:T(8,128)(2,1)S(1)}, u32[]{:S(2)}, u32[]{:S(2)}) %collective-permute-start.7) | collective-permute-done | bytes 294944 | tf_op jit(solution)/shard_map/ppermute | solution.py:29
  41.8 1.7 collective-permute-start.8
  43.5 3.3 %collective-permute-start.9 = (bf16[576,256]{1,0:T(8,128)(2,1)S(1)}, bf16[576,256]{1,0:T(8,128)(2,1)S(1)}, u32[]{:S(2)}, u32[]{:S(2)}) collective-permute-start(bf16[576,256]{1,0:T(8,128)(2,1)S(1)} %shard_map.102.refs_0_.after), channel_id=1, source_target_pairs={{0,4},{2,6},{4,0},{6,2},{1,5},{3,7},{5,1},{7,3},{8,12},{10,14},{12... | collective-permute-start | bytes 884744 | tf_op jit(solution)/shard_map/ppermute | solution.py:29
  47.5 2.9 %collective-permute-start.11 = (bf16[576,256]{1,0:T(8,128)(2,1)S(1)}, bf16[576,256]{1,0:T(8,128)(2,1)S(1)}, u32[]{:S(2)}, u32[]{:S(2)}) collective-permute-start(bf16[576,256]{1,0:T(8,128)(2,1)S(1)} %shard_map.102.refs_0_.after), channel_id=1, source_target_pairs={{0,1},{1,0},{2,3},{3,2},{4,5},{5,4},{6,7},{7,6},{8,9},{9,8},{10,11... | collective-permute-start | bytes 884744 | tf_op jit(solution)/shard_map/ppermute | solution.py:29
  52.9 2.1 collective-permute-start.31
  54.9 4.4 %collective-permute-done.9.refs_2_ = bf16[576,256]{1,0:T(8,128)(2,1)S(1)} collective-permute-done((bf16[576,256]{1,0:T(8,128)(2,1)S(1)}, bf16[576,256]{1,0:T(8,128)(2,1)S(1)}, u32[]{:S(2)}, u32[]{:S(2)}) %collective-permute-start.9) | collective-permute-done | bytes 294944 | tf_op jit(solution)/shard_map/ppermute | solution.py:29
  60.1 1.4 collective-permute-start.32
  62.2 2.1 collective-permute-start.33
  64.4 1.3 collective-permute-start.37
  65.8 13.5 %collective-permute-done.31.refs_2_ = bf16[288,512]{1,0:T(8,128)(2,1)S(1)} collective-permute-done((bf16[288,512]{1,0:T(8,128)(2,1)S(1)}, bf16[288,512]{1,0:T(8,128)(2,1)S(1)}, u32[]{:S(2)}, u32[]{:S(2)}) %collective-permute-start.31) | collective-permute-done | bytes 294944 | tf_op jit(solution)/shard_map/ppermute | solution.py:29
  80.6 2.3 %collective-permute-start.14 = (bf16[576,256]{1,0:T(8,128)(2,1)S(1)}, bf16[576,256]{1,0:T(8,128)(2,1)S(1)}, u32[]{:S(2)}, u32[]{:S(2)}) collective-permute-start(bf16[576,256]{1,0:T(8,128)(2,1)S(1)} %collective-permute-done.11.refs_4_), channel_id=1, source_target_pairs={{0,6},{2,0},{4,2},{6,4},{1,7},{3,1},{5,3},{7,5},{8,14},{10,8},{12,... | collective-permute-start | bytes 884744 | tf_op jit(solution)/shard_map/ppermute | solution.py:29
  83.6 3.5 %collective-permute-start.35 = (bf16[288,512]{1,0:T(8,128)(2,1)S(1)}, bf16[288,512]{1,0:T(8,128)(2,1)S(1)}, u32[]{:S(2)}, u32[]{:S(2)}) collective-permute-start(bf16[288,512]{1,0:T(8,128)(2,1)S(1)} %collective-permute-done.31.refs_2_), channel_id=1, source_target_pairs={{0,8},{8,0},{1,9},{9,1},{2,10},{10,2},{3,11},{11,3},{4,12},{12,4},... | collective-permute-start | bytes 884744 | tf_op jit(solution)/shard_map/ppermute | solution.py:29
  89.0 2.7 %collective-permute-start.40 = (bf16[288,512]{1,0:T(8,128)(2,1)}, bf16[288,512]{1,0:T(8,128)(2,1)}, u32[]{:S(2)}, u32[]{:S(2)}) collective-permute-start(bf16[288,512]{1,0:T(8,128)(2,1)} %collective-permute-done.37.refs_8_), channel_id=1, source_target_pairs={{0,96},{32,0},{64,32},{96,64},{1,97},{33,1},{65,33},{97,65},{2,98}... | collective-permute-start | bytes 884744 | tf_op jit(solution)/shard_map/ppermute | solution.py:29
  92.5 3.0 %collective-permute-start.34 = (bf16[288,512]{1,0:T(8,128)(2,1)S(1)}, bf16[288,512]{1,0:T(8,128)(2,1)S(1)}, u32[]{:S(2)}, u32[]{:S(2)}) collective-permute-start(bf16[288,512]{1,0:T(8,128)(2,1)S(1)} %collective-permute-done.30.refs_1_), channel_id=1, source_target_pairs={{0,8},{8,0},{1,9},{9,1},{2,10},{10,2},{3,11},{11,3},{4,12},{12,4},... | collective-permute-start | bytes 884744 | tf_op jit(solution)/shard_map/ppermute | solution.py:29
  109.2 3.1 %key_value.1.refs_0_ = bf16[256,512]{1,0:T(8,128)(2,1)S(1)} custom-call(bf16[256,4608]{1,0:T(8,128)(2,1)S(1)} %get-tuple-element.36.normed, bf16[4608,1024]{1,0:T(8,128)(2,1)} %all-gather.2.cloned.1.call-done.weight, f32[256,128]{1,0:T(8,128)S(1)} %pad_maximum_fusion.cos, f32[256,128]{1,0:T(8,128)S(1)} %pad_maximum_fusion.1.sin), custom_call_target="tpu_custom_call" | custom-call | tf_op jit(solution)/shard_map/key_value/pallas_call | solution.py:456
  112.4 4.0 %collective-permute-start.16 = (bf16[256,512]{1,0:T(8,128)(2,1)S(1)}, bf16[256,512]{1,0:T(8,128)(2,1)S(1)}, u32[]{:S(2)}, u32[]{:S(2)}) collective-permute-start(bf16[256,512]{1,0:T(8,128)(2,1)S(1)} %key_value.1.refs_0_), channel_id=1, source_target_pairs={{0,64},{32,96},{64,0},{96,32},{1,65},{33,97},{65,1},{97,33},{2,66}... | collective-permute-start | bytes 786440 | tf_op jit(solution)/shard_map/ppermute | solution.py:29
  118.4 3.2 %collective-permute-done.15.refs_1_ = bf16[256,512]{1,0:T(8,128)(2,1)S(1)} collective-permute-done((bf16[256,512]{1,0:T(8,128)(2,1)S(1)}, bf16[256,512]{1,0:T(8,128)(2,1)S(1)}, u32[]{:S(2)}, u32[]{:S(2)}) %collective-permute-start.15) | collective-permute-done | bytes 262176 | tf_op jit(solution)/shard_map/ppermute | solution.py:29
  122.5 5.9 %collective-permute-done.16.refs_2_ = bf16[256,512]{1,0:T(8,128)(2,1)S(1)} collective-permute-done((bf16[256,512]{1,0:T(8,128)(2,1)S(1)}, bf16[256,512]{1,0:T(8,128)(2,1)S(1)}, u32[]{:S(2)}, u32[]{:S(2)}) %collective-permute-start.16) | collective-permute-done | bytes 262176 | tf_op jit(solution)/shard_map/ppermute | solution.py:29
  130.4 2.6 %collective-permute-start.25 = (bf16[256,512]{1,0:T(8,128)(2,1)S(1)}, bf16[256,512]{1,0:T(8,128)(2,1)S(1)}, u32[]{:S(2)}, u32[]{:S(2)}) collective-permute-start(bf16[256,512]{1,0:T(8,128)(2,1)S(1)} %collective-permute-done.22.refs_8_), channel_id=1, source_target_pairs={{0,96},{32,0},{64,32},{96,64},{1,97},{33,1},{65,33},{97,65},{2,98}... | collective-permute-start | bytes 786440 | tf_op jit(solution)/shard_map/ppermute | solution.py:29
  134.0 4.4 %collective-permute-done.23.refs_9_ = bf16[256,512]{1,0:T(8,128)(2,1)S(1)} collective-permute-done((bf16[256,512]{1,0:T(8,128)(2,1)S(1)}, bf16[256,512]{1,0:T(8,128)(2,1)S(1)}, u32[]{:S(2)}, u32[]{:S(2)}) %collective-permute-start.23) | collective-permute-done | bytes 262176 | tf_op jit(solution)/shard_map/ppermute | solution.py:29
  139.8 2.1 shard_map.105.weight
  141.9 3.4 %shard_map.104.query = bf16[256,512]{1,0:T(8,128)(2,1)S(1)} custom-call(bf16[256,4608]{1,0:T(8,128)(2,1)S(1)} %get-tuple-element.36.normed, bf16[4608,1024]{1,0:T(8,128)(2,1)} %all-gather.2.cloned.1.call-done.weight, f32[256,128]{1,0:T(8,128)S(1)} %pad_maximum_fusion.cos, f32[256,128]{1,0:T(8,128)S(1)} %pad_maximum_fusion.1.sin), custom_call_target="tpu_custom_call" | custom-call | tf_op jit(solution)/shard_map/pallas_call | solution.py:447
  145.4 5.4 %attention.1.context = bf16[256,512]{1,0:T(8,128)(2,1)S(1)} custom-call(s32[1]{0:T(128)} %bitcast.flat, bf16[256,512]{1,0:T(8,128)(2,1)S(1)} %shard_map.104.query, bf16[256,512]{1,0:T(8,128)(2,1)S(1)} %key_value.1.refs_0_, bf16[256,512]{1,0:T(8,128)(2,1)S(1)} %collective-permute-done.15.refs_1_, bf16[256,512]{1,0:T(8,128)(2,1)S(1)} %collective-permute-done.16.refs_2_, ...), custom_call_target="tpu_custom_call" | custom-call | tf_op jit(solution)/shard_map/attention/pallas_call | solution.py:474
  150.8 3.1 %project.1 = (bf16[32,4608]{1,0:T(8,128)(2,1)S(1)}, bf16[32,4608]{1,0:T(8,128)(2,1)S(1)}, bf16[32,4608]{1,0:T(8,128)(2,1)S(1)}, bf16[32,4608]{1,0:T(8,128)(2,1)S...) custom-call(s32[1]{0:T(128)} %bitcast.flat, ...), custom_call_target="tpu_custom_call" | custom-call | tf_op jit(solution)/shard_map/project/pallas_call | solution.py:485
  154.0 1.4 collective-permute-start.45
  156.3 2.0 collective-permute-start.47
  158.7 1.7 collective-permute-start.49
  160.4 3.8 %collective-permute-done.45.refs_1_ = bf16[32,4608]{1,0:T(8,128)(2,1)S(1)} collective-permute-done((bf16[32,4608]{1,0:T(8,128)(2,1)S(1)}, bf16[32,4608]{1,0:T(8,128)(2,1)S(1)}, u32[]{:S(2)}, u32[]{:S(2)}) %collective-permute-start.45) | collective-permute-done | bytes 294944 | tf_op jit(solution)/shard_map/ppermute | solution.py:29
  165.0 14.1 %collective-permute-done.46.refs_2_ = bf16[32,4608]{1,0:T(8,128)(2,1)S(1)} collective-permute-done((bf16[32,4608]{1,0:T(8,128)(2,1)S(1)}, bf16[32,4608]{1,0:T(8,128)(2,1)S(1)}, u32[]{:S(2)}, u32[]{:S(2)}) %collective-permute-start.46) | collective-permute-done | bytes 294944 | tf_op jit(solution)/shard_map/ppermute | solution.py:29
  179.1 11.1 %collective-permute-done.51.refs_7_ = bf16[32,4608]{1,0:T(8,128)(2,1)S(1)} collective-permute-done((bf16[32,4608]{1,0:T(8,128)(2,1)S(1)}, bf16[32,4608]{1,0:T(8,128)(2,1)S(1)}, u32[]{:S(2)}, u32[]{:S(2)}) %collective-permute-start.51) | collective-permute-done | bytes 294944 | tf_op jit(solution)/shard_map/ppermute | solution.py:500
  190.9 4.2 %collective-permute-start.52 = (bf16[32,4608]{1,0:T(8,128)(2,1)S(1)}, bf16[32,4608]{1,0:T(8,128)(2,1)S(1)}, u32[]{:S(2)}, u32[]{:S(2)}) collective-permute-start(bf16[32,4608]{1,0:T(8,128)(2,1)S(1)} %finish.1.refs_0_), channel_id=1, source_target_pairs={{0,8},{8,0},{1,9},{9,1},{2,10},{10,2},{3,11},{11,3},{4,12},{12,4},... | collective-permute-start | bytes 884744 | tf_op jit(solution)/shard_map/ppermute | solution.py:29
  195.1 1.3 collective-permute-done.53.refs_2_
  196.4 5.3 %collective-permute-start.54 = (bf16[32,4608]{1,0:T(8,128)(2,1)S(1)}, bf16[32,4608]{1,0:T(8,128)(2,1)S(1)}, u32[]{:S(2)}, u32[]{:S(2)}) collective-permute-start(bf16[32,4608]{1,0:T(8,128)(2,1)S(1)} %collective-permute-done.53.refs_2_), channel_id=1, source_target_pairs={{0,8},{8,0},{1,9},{9,1},{2,10},{10,2},{3,11},{11,3},{4,12},{12,4},... | collective-permute-start | bytes 884744 | tf_op jit(solution)/shard_map/ppermute | solution.py:29
  201.7 1.2 collective-permute-done.54.refs_3_
  203.9 3.0 %collective-permute-start.56 = (bf16[16,4608]{1,0:T(8,128)(2,1)S(1)}, bf16[16,4608]{1,0:T(8,128)(2,1)S(1)}, u32[]{:S(2)}, u32[]{:S(2)}) collective-permute-start(bf16[16,4608]{1,0:T(8,128)(2,1)S(1)} %get-tuple-element.47), channel_id=1, source_target_pairs={{0,64},{32,96},{64,0},{96,32},{1,65},{33,97},{65,1},{97,33},{2,66}... | collective-permute-start | bytes 442376 | tf_op jit(solution)/shard_map/ppermute | solution.py:29
  206.9 3.3 %collective-permute-done.55.refs_1_ = bf16[16,4608]{1,0:T(8,128)(2,1)S(1)} collective-permute-done((bf16[16,4608]{1,0:T(8,128)(2,1)S(1)}, bf16[16,4608]{1,0:T(8,128)(2,1)S(1)}, u32[]{:S(2)}, u32[]{:S(2)}) %collective-permute-start.55) | collective-permute-done | bytes 147488 | tf_op jit(solution)/shard_map/ppermute | solution.py:29
  210.1 3.5 %collective-permute-done.56.refs_2_ = bf16[16,4608]{1,0:T(8,128)(2,1)S(1)} collective-permute-done((bf16[16,4608]{1,0:T(8,128)(2,1)S(1)}, bf16[16,4608]{1,0:T(8,128)(2,1)S(1)}, u32[]{:S(2)}, u32[]{:S(2)}) %collective-permute-start.56) | collective-permute-done | bytes 147488 | tf_op jit(solution)/shard_map/ppermute | solution.py:29
  214.4 2.9 %collective-permute-start.58 = (bf16[16,4608]{1,0:T(8,128)(2,1)S(1)}, bf16[16,4608]{1,0:T(8,128)(2,1)S(1)}, u32[]{:S(2)}, u32[]{:S(2)}) collective-permute-start(bf16[16,4608]{1,0:T(8,128)(2,1)S(1)} %get-tuple-element.50), channel_id=1, source_target_pairs={{0,2},{2,4},{4,6},{6,0},{1,3},{3,5},{5,7},{7,1},{8,10},{10,12},{12... | collective-permute-start | bytes 442376 | tf_op jit(solution)/shard_map/ppermute | solution.py:29
  217.4 1.3 collective-permute-start.59
  220.0 4.4 %collective-permute-done.59.refs_2_ = bf16[16,4608]{1,0:T(8,128)(2,1)S(1)} collective-permute-done((bf16[16,4608]{1,0:T(8,128)(2,1)S(1)}, bf16[16,4608]{1,0:T(8,128)(2,1)S(1)}, u32[]{:S(2)}, u32[]{:S(2)}) %collective-permute-start.59) | collective-permute-done | bytes 147488 | tf_op jit(solution)/shard_map/ppermute | solution.py:29
  (153 shorter events, 43.2 us)
Async XLA Ops:
  6.5 102.6 %all-gather.2.cloned.1.call-start = ((), (), s32[]{:S(2)}) async-start(), calls=%async_computation | async-start | bytes 10027008 | tf_op jit(solution)/shard_map/all_gather | solution.py:399
  10.4 7.2 %collective-permute-start = (bf16[576,128]{1,0:T(8,128)(2,1)S(1)}, bf16[576,128]{1,0:T(8,128)(2,1)S(1)}, u32[]{:S(2)}, u32[]{:S(2)}) collective-permute-start(bf16[576,128]{1,0:T(8,128)(2,1)S(1)} %get-tuple-element.30), channel_id=1, source_target_pairs={{0,32},{32,64},{64,96},{96,0},{1,33},{33,65},{65,97},{97,1},{2,34}... | collective-permute-start | bytes 442376 | tf_op jit(solution)/shard_map/ppermute | solution.py:29
  12.5 8.9 %collective-permute-start.1 = (bf16[576,128]{1,0:T(8,128)(2,1)S(1)}, bf16[576,128]{1,0:T(8,128)(2,1)S(1)}, u32[]{:S(2)}, u32[]{:S(2)}) collective-permute-start(bf16[576,128]{1,0:T(8,128)(2,1)S(1)} %get-tuple-element.31), channel_id=1, source_target_pairs={{0,64},{32,96},{64,0},{96,32},{1,65},{33,97},{65,1},{97,33},{2,66}... | collective-permute-start | bytes 442376 | tf_op jit(solution)/shard_map/ppermute | solution.py:29
  15.0 8.0 %collective-permute-start.2 = (bf16[576,128]{1,0:T(8,128)(2,1)S(1)}, bf16[576,128]{1,0:T(8,128)(2,1)S(1)}, u32[]{:S(2)}, u32[]{:S(2)}) collective-permute-start(bf16[576,128]{1,0:T(8,128)(2,1)S(1)} %get-tuple-element.32), channel_id=1, source_target_pairs={{0,96},{32,0},{64,32},{96,64},{1,97},{33,1},{65,33},{97,65},{2,98}... | collective-permute-start | bytes 442376 | tf_op jit(solution)/shard_map/ppermute | solution.py:29
  25.4 15.5 %collective-permute-start.7 = (bf16[576,256]{1,0:T(8,128)(2,1)S(1)}, bf16[576,256]{1,0:T(8,128)(2,1)S(1)}, u32[]{:S(2)}, u32[]{:S(2)}) collective-permute-start(bf16[576,256]{1,0:T(8,128)(2,1)S(1)} %get-tuple-element.34), channel_id=1, source_target_pairs={{0,16},{16,0},{1,17},{17,1},{2,18},{18,2},{3,19},{19,3},{4,20},{20... | collective-permute-start | bytes 884744 | tf_op jit(solution)/shard_map/ppermute | solution.py:29
  41.8 10.4 %collective-permute-start.8 = (bf16[576,256]{1,0:T(8,128)(2,1)S(1)}, bf16[576,256]{1,0:T(8,128)(2,1)S(1)}, u32[]{:S(2)}, u32[]{:S(2)}) collective-permute-start(bf16[576,256]{1,0:T(8,128)(2,1)S(1)} %shard_map.102.refs_0_.after), channel_id=1, source_target_pairs={{0,2},{2,4},{4,6},{6,0},{1,3},{3,5},{5,7},{7,1},{8,10},{10,12},{12... | collective-permute-start | bytes 884744 | tf_op jit(solution)/shard_map/ppermute | solution.py:29
  43.5 15.9 %collective-permute-start.9 = (bf16[576,256]{1,0:T(8,128)(2,1)S(1)}, bf16[576,256]{1,0:T(8,128)(2,1)S(1)}, u32[]{:S(2)}, u32[]{:S(2)}) collective-permute-start(bf16[576,256]{1,0:T(8,128)(2,1)S(1)} %shard_map.102.refs_0_.after), channel_id=1, source_target_pairs={{0,4},{2,6},{4,0},{6,2},{1,5},{3,7},{5,1},{7,3},{8,12},{10,14},{12... | collective-permute-start | bytes 884744 | tf_op jit(solution)/shard_map/ppermute | solution.py:29
  46.8 14.7 %collective-permute-start.10 = (bf16[576,256]{1,0:T(8,128)(2,1)S(1)}, bf16[576,256]{1,0:T(8,128)(2,1)S(1)}, u32[]{:S(2)}, u32[]{:S(2)}) collective-permute-start(bf16[576,256]{1,0:T(8,128)(2,1)S(1)} %shard_map.102.refs_0_.after), channel_id=1, source_target_pairs={{0,6},{2,0},{4,2},{6,4},{1,7},{3,1},{5,3},{7,5},{8,14},{10,8},{12,... | collective-permute-start | bytes 884744 | tf_op jit(solution)/shard_map/ppermute | solution.py:29
  47.5 16.9 %collective-permute-start.11 = (bf16[576,256]{1,0:T(8,128)(2,1)S(1)}, bf16[576,256]{1,0:T(8,128)(2,1)S(1)}, u32[]{:S(2)}, u32[]{:S(2)}) collective-permute-start(bf16[576,256]{1,0:T(8,128)(2,1)S(1)} %shard_map.102.refs_0_.after), channel_id=1, source_target_pairs={{0,1},{1,0},{2,3},{3,2},{4,5},{5,4},{6,7},{7,6},{8,9},{9,8},{10,11... | collective-permute-start | bytes 884744 | tf_op jit(solution)/shard_map/ppermute | solution.py:29
  51.4 14.2 %collective-permute-start.30 = (bf16[288,512]{1,0:T(8,128)(2,1)S(1)}, bf16[288,512]{1,0:T(8,128)(2,1)S(1)}, u32[]{:S(2)}, u32[]{:S(2)}) collective-permute-start(bf16[288,512]{1,0:T(8,128)(2,1)S(1)} %hold.1.refs_0_), channel_id=1, source_target_pairs={{0,32},{32,64},{64,96},{96,0},{1,33},{33,65},{65,97},{97,1},{2,34}... | collective-permute-start | bytes 884744 | tf_op jit(solution)/shard_map/ppermute | solution.py:29
  52.9 26.5 %collective-permute-start.31 = (bf16[288,512]{1,0:T(8,128)(2,1)S(1)}, bf16[288,512]{1,0:T(8,128)(2,1)S(1)}, u32[]{:S(2)}, u32[]{:S(2)}) collective-permute-start(bf16[288,512]{1,0:T(8,128)(2,1)S(1)} %hold.1.refs_0_), channel_id=1, source_target_pairs={{0,64},{32,96},{64,0},{96,32},{1,65},{33,97},{65,1},{97,33},{2,66}... | collective-permute-start | bytes 884744 | tf_op jit(solution)/shard_map/ppermute | solution.py:29
  60.1 20.5 %collective-permute-start.32 = (bf16[288,512]{1,0:T(8,128)(2,1)S(1)}, bf16[288,512]{1,0:T(8,128)(2,1)}, u32[]{:S(2)}, u32[]{:S(2)}) collective-permute-start(bf16[288,512]{1,0:T(8,128)(2,1)S(1)} %hold.1.refs_0_), channel_id=1, source_target_pairs={{0,96},{32,0},{64,32},{96,64},{1,97},{33,1},{65,33},{97,65},{2,98}... | collective-permute-start | bytes 884744 | tf_op jit(solution)/shard_map/ppermute | solution.py:29
  62.2 21.4 %collective-permute-start.33 = (bf16[288,512]{1,0:T(8,128)(2,1)S(1)}, bf16[288,512]{1,0:T(8,128)(2,1)S(1)}, u32[]{:S(2)}, u32[]{:S(2)}) collective-permute-start(bf16[288,512]{1,0:T(8,128)(2,1)S(1)} %hold.1.refs_0_), channel_id=1, source_target_pairs={{0,8},{8,0},{1,9},{9,1},{2,10},{10,2},{3,11},{11,3},{4,12},{12,4},... | collective-permute-start | bytes 884744 | tf_op jit(solution)/shard_map/ppermute | solution.py:29
  64.4 22.8 %collective-permute-start.37 = (bf16[288,512]{1,0:T(8,128)(2,1)S(1)}, bf16[288,512]{1,0:T(8,128)(2,1)}, u32[]{:S(2)}, u32[]{:S(2)}) collective-permute-start(bf16[288,512]{1,0:T(8,128)(2,1)S(1)} %hold.1.refs_0_), channel_id=1, source_target_pairs={{0,16},{16,0},{1,17},{17,1},{2,18},{18,2},{3,19},{19,3},{4,20},{20... | collective-permute-start | bytes 884744 | tf_op jit(solution)/shard_map/ppermute | solution.py:29
  65.6 21.9 %collective-permute-start.12 = (bf16[576,256]{1,0:T(8,128)(2,1)S(1)}, bf16[576,256]{1,0:T(8,128)(2,1)S(1)}, u32[]{:S(2)}, u32[]{:S(2)}) collective-permute-start(bf16[576,256]{1,0:T(8,128)(2,1)S(1)} %collective-permute-done.11.refs_4_), channel_id=1, source_target_pairs={{0,2},{2,4},{4,6},{6,0},{1,3},{3,5},{5,7},{7,1},{8,10},{10,12},{12... | collective-permute-start | bytes 884744 | tf_op jit(solution)/shard_map/ppermute | solution.py:29
  79.4 8.9 %collective-permute-start.13 = (bf16[576,256]{1,0:T(8,128)(2,1)S(1)}, bf16[576,256]{1,0:T(8,128)(2,1)S(1)}, u32[]{:S(2)}, u32[]{:S(2)}) collective-permute-start(bf16[576,256]{1,0:T(8,128)(2,1)S(1)} %collective-permute-done.11.refs_4_), channel_id=1, source_target_pairs={{0,4},{2,6},{4,0},{6,2},{1,5},{3,7},{5,1},{7,3},{8,12},{10,14},{12... | collective-permute-start | bytes 884744 | tf_op jit(solution)/shard_map/ppermute | solution.py:29
  80.6 11.2 %collective-permute-start.14 = (bf16[576,256]{1,0:T(8,128)(2,1)S(1)}, bf16[576,256]{1,0:T(8,128)(2,1)S(1)}, u32[]{:S(2)}, u32[]{:S(2)}) collective-permute-start(bf16[576,256]{1,0:T(8,128)(2,1)S(1)} %collective-permute-done.11.refs_4_), channel_id=1, source_target_pairs={{0,6},{2,0},{4,2},{6,4},{1,7},{3,1},{5,3},{7,5},{8,14},{10,8},{12,... | collective-permute-start | bytes 884744 | tf_op jit(solution)/shard_map/ppermute | solution.py:29
  83.6 14.2 %collective-permute-start.35 = (bf16[288,512]{1,0:T(8,128)(2,1)S(1)}, bf16[288,512]{1,0:T(8,128)(2,1)S(1)}, u32[]{:S(2)}, u32[]{:S(2)}) collective-permute-start(bf16[288,512]{1,0:T(8,128)(2,1)S(1)} %collective-permute-done.31.refs_2_), channel_id=1, source_target_pairs={{0,8},{8,0},{1,9},{9,1},{2,10},{10,2},{3,11},{11,3},{4,12},{12,4},... | collective-permute-start | bytes 884744 | tf_op jit(solution)/shard_map/ppermute | solution.py:29
  87.1 12.1 %collective-permute-start.39 = (bf16[288,512]{1,0:T(8,128)(2,1)S(1)}, bf16[288,512]{1,0:T(8,128)(2,1)}, u32[]{:S(2)}, u32[]{:S(2)}) collective-permute-start(bf16[288,512]{1,0:T(8,128)(2,1)S(1)} %collective-permute-done.31.refs_2_), channel_id=1, source_target_pairs={{0,16},{16,0},{1,17},{17,1},{2,18},{18,2},{3,19},{19,3},{4,20},{20... | collective-permute-start | bytes 884744 | tf_op jit(solution)/shard_map/ppermute | solution.py:29
  88.3 10.4 %collective-permute-start.38 = (bf16[288,512]{1,0:T(8,128)(2,1)}, bf16[288,512]{1,0:T(8,128)(2,1)}, u32[]{:S(2)}, u32[]{:S(2)}) collective-permute-start(bf16[288,512]{1,0:T(8,128)(2,1)} %collective-permute-done.37.refs_8_), channel_id=1, source_target_pairs={{0,32},{32,64},{64,96},{96,0},{1,33},{33,65},{65,97},{97,1},{2,34}... | collective-permute-start | bytes 884744 | tf_op jit(solution)/shard_map/ppermute | solution.py:29
  89.0 10.2 %collective-permute-start.40 = (bf16[288,512]{1,0:T(8,128)(2,1)}, bf16[288,512]{1,0:T(8,128)(2,1)}, u32[]{:S(2)}, u32[]{:S(2)}) collective-permute-start(bf16[288,512]{1,0:T(8,128)(2,1)} %collective-permute-done.37.refs_8_), channel_id=1, source_target_pairs={{0,96},{32,0},{64,32},{96,64},{1,97},{33,1},{65,33},{97,65},{2,98}... | collective-permute-start | bytes 884744 | tf_op jit(solution)/shard_map/ppermute | solution.py:29
  97.4 15.0 %collective-permute-start.41 = (bf16[288,512]{1,0:T(8,128)(2,1)}, bf16[288,512]{1,0:T(8,128)(2,1)}, u32[]{:S(2)}, u32[]{:S(2)}) collective-permute-start(bf16[288,512]{1,0:T(8,128)(2,1)} %collective-permute-done.37.refs_8_), channel_id=1, source_target_pairs={{0,8},{8,0},{1,9},{9,1},{2,10},{10,2},{3,11},{11,3},{4,12},{12,4},... | collective-permute-start | bytes 884744 | tf_op jit(solution)/shard_map/ppermute | solution.py:29
  98.5 13.8 %collective-permute-start.36 = (bf16[288,512]{1,0:T(8,128)(2,1)}, bf16[288,512]{1,0:T(8,128)(2,1)}, u32[]{:S(2)}, u32[]{:S(2)}) collective-permute-start(bf16[288,512]{1,0:T(8,128)(2,1)} %collective-permute-done.32.refs_3_), channel_id=1, source_target_pairs={{0,8},{8,0},{1,9},{9,1},{2,10},{10,2},{3,11},{11,3},{4,12},{12,4},... | collective-permute-start | bytes 884744 | tf_op jit(solution)/shard_map/ppermute | solution.py:29
  98.7 17.8 %collective-permute-start.42 = (bf16[288,512]{1,0:T(8,128)(2,1)}, bf16[288,512]{1,0:T(8,128)(2,1)}, u32[]{:S(2)}, u32[]{:S(2)}) collective-permute-start(bf16[288,512]{1,0:T(8,128)(2,1)} %collective-permute-done.38.refs_9_), channel_id=1, source_target_pairs={{0,8},{8,0},{1,9},{9,1},{2,10},{10,2},{3,11},{11,3},{4,12},{12,4},... | collective-permute-start | bytes 884744 | tf_op jit(solution)/shard_map/ppermute | solution.py:29
  99.2 18.2 %collective-permute-start.43 = (bf16[288,512]{1,0:T(8,128)(2,1)}, bf16[288,512]{1,0:T(8,128)(2,1)}, u32[]{:S(2)}, u32[]{:S(2)}) collective-permute-start(bf16[288,512]{1,0:T(8,128)(2,1)} %collective-permute-done.39.refs_10_), channel_id=1, source_target_pairs={{0,8},{8,0},{1,9},{9,1},{2,10},{10,2},{3,11},{11,3},{4,12},{12,4},... | collective-permute-start | bytes 884744 | tf_op jit(solution)/shard_map/ppermute | solution.py:29
  99.3 18.2 %collective-permute-start.44 = (bf16[288,512]{1,0:T(8,128)(2,1)}, bf16[288,512]{1,0:T(8,128)(2,1)}, u32[]{:S(2)}, u32[]{:S(2)}) collective-permute-start(bf16[288,512]{1,0:T(8,128)(2,1)} %collective-permute-done.40.refs_11_), channel_id=1, source_target_pairs={{0,8},{8,0},{1,9},{9,1},{2,10},{10,2},{3,11},{11,3},{4,12},{12,4},... | collective-permute-start | bytes 884744 | tf_op jit(solution)/shard_map/ppermute | solution.py:29
  112.3 9.3 %collective-permute-start.15 = (bf16[256,512]{1,0:T(8,128)(2,1)S(1)}, bf16[256,512]{1,0:T(8,128)(2,1)S(1)}, u32[]{:S(2)}, u32[]{:S(2)}) collective-permute-start(bf16[256,512]{1,0:T(8,128)(2,1)S(1)} %key_value.1.refs_0_), channel_id=1, source_target_pairs={{0,32},{32,64},{64,96},{96,0},{1,33},{33,65},{65,97},{97,1},{2,34}... | collective-permute-start | bytes 786440 | tf_op jit(solution)/shard_map/ppermute | solution.py:29
  112.4 16.0 %collective-permute-start.16 = (bf16[256,512]{1,0:T(8,128)(2,1)S(1)}, bf16[256,512]{1,0:T(8,128)(2,1)S(1)}, u32[]{:S(2)}, u32[]{:S(2)}) collective-permute-start(bf16[256,512]{1,0:T(8,128)(2,1)S(1)} %key_value.1.refs_0_), channel_id=1, source_target_pairs={{0,64},{32,96},{64,0},{96,32},{1,65},{33,97},{65,1},{97,33},{2,66}... | collective-permute-start | bytes 786440 | tf_op jit(solution)/shard_map/ppermute | solution.py:29
  116.5 12.9 %collective-permute-start.22 = (bf16[256,512]{1,0:T(8,128)(2,1)S(1)}, bf16[256,512]{1,0:T(8,128)(2,1)S(1)}, u32[]{:S(2)}, u32[]{:S(2)}) collective-permute-start(bf16[256,512]{1,0:T(8,128)(2,1)S(1)} %key_value.1.refs_0_), channel_id=1, source_target_pairs={{0,16},{16,0},{1,17},{17,1},{2,18},{18,2},{3,19},{19,3},{4,20},{20... | collective-permute-start | bytes 786440 | tf_op jit(solution)/shard_map/ppermute | solution.py:29
  117.5 11.9 %collective-permute-start.17 = (bf16[256,512]{1,0:T(8,128)(2,1)S(1)}, bf16[256,512]{1,0:T(8,128)(2,1)S(1)}, u32[]{:S(2)}, u32[]{:S(2)}) collective-permute-start(bf16[256,512]{1,0:T(8,128)(2,1)S(1)} %key_value.1.refs_0_), channel_id=1, source_target_pairs={{0,96},{32,0},{64,32},{96,64},{1,97},{33,1},{65,33},{97,65},{2,98}... | collective-permute-start | bytes 786440 | tf_op jit(solution)/shard_map/ppermute | solution.py:29
  117.5 12.9 %collective-permute-start.18 = (bf16[256,512]{1,0:T(8,128)(2,1)S(1)}, bf16[256,512]{1,0:T(8,128)(2,1)S(1)}, u32[]{:S(2)}, u32[]{:S(2)}) collective-permute-start(bf16[256,512]{1,0:T(8,128)(2,1)S(1)} %key_value.1.refs_0_), channel_id=1, source_target_pairs={{0,8},{8,0},{1,9},{9,1},{2,10},{10,2},{3,11},{11,3},{4,12},{12,4},... | collective-permute-start | bytes 786440 | tf_op jit(solution)/shard_map/ppermute | solution.py:29
  121.6 11.4 %collective-permute-start.19 = (bf16[256,512]{1,0:T(8,128)(2,1)S(1)}, bf16[256,512]{1,0:T(8,128)(2,1)S(1)}, u32[]{:S(2)}, u32[]{:S(2)}) collective-permute-start(bf16[256,512]{1,0:T(8,128)(2,1)S(1)} %collective-permute-done.15.refs_1_), channel_id=1, source_target_pairs={{0,8},{8,0},{1,9},{9,1},{2,10},{10,2},{3,11},{11,3},{4,12},{12,4},... | collective-permute-start | bytes 786440 | tf_op jit(solution)/shard_map/ppermute | solution.py:29
  129.3 9.1 %collective-permute-start.23 = (bf16[256,512]{1,0:T(8,128)(2,1)S(1)}, bf16[256,512]{1,0:T(8,128)(2,1)S(1)}, u32[]{:S(2)}, u32[]{:S(2)}) collective-permute-start(bf16[256,512]{1,0:T(8,128)(2,1)S(1)} %collective-permute-done.22.refs_8_), channel_id=1, source_target_pairs={{0,32},{32,64},{64,96},{96,0},{1,33},{33,65},{65,97},{97,1},{2,34}... | collective-permute-start | bytes 786440 | tf_op jit(solution)/shard_map/ppermute | solution.py:29
  129.3 9.9 %collective-permute-start.24 = (bf16[256,512]{1,0:T(8,128)(2,1)S(1)}, bf16[256,512]{1,0:T(8,128)(2,1)S(1)}, u32[]{:S(2)}, u32[]{:S(2)}) collective-permute-start(bf16[256,512]{1,0:T(8,128)(2,1)S(1)} %collective-permute-done.16.refs_2_), channel_id=1, source_target_pairs={{0,16},{16,0},{1,17},{17,1},{2,18},{18,2},{3,19},{19,3},{4,20},{20... | collective-permute-start | bytes 786440 | tf_op jit(solution)/shard_map/ppermute | solution.py:29
  130.4 8.8 %collective-permute-start.25 = (bf16[256,512]{1,0:T(8,128)(2,1)S(1)}, bf16[256,512]{1,0:T(8,128)(2,1)S(1)}, u32[]{:S(2)}, u32[]{:S(2)}) collective-permute-start(bf16[256,512]{1,0:T(8,128)(2,1)S(1)} %collective-permute-done.22.refs_8_), channel_id=1, source_target_pairs={{0,96},{32,0},{64,32},{96,64},{1,97},{33,1},{65,33},{97,65},{2,98}... | collective-permute-start | bytes 786440 | tf_op jit(solution)/shard_map/ppermute | solution.py:29
  133.0 12.3 %collective-permute-start.26 = (bf16[256,512]{1,0:T(8,128)(2,1)S(1)}, bf16[256,512]{1,0:T(8,128)(2,1)S(1)}, u32[]{:S(2)}, u32[]{:S(2)}) collective-permute-start(bf16[256,512]{1,0:T(8,128)(2,1)S(1)} %collective-permute-done.22.refs_8_), channel_id=1, source_target_pairs={{0,8},{8,0},{1,9},{9,1},{2,10},{10,2},{3,11},{11,3},{4,12},{12,4},... | collective-permute-start | bytes 786440 | tf_op jit(solution)/shard_map/ppermute | solution.py:29
  133.9 11.5 %collective-permute-start.21 = (bf16[256,512]{1,0:T(8,128)(2,1)S(1)}, bf16[256,512]{1,0:T(8,128)(2,1)S(1)}, u32[]{:S(2)}, u32[]{:S(2)}) collective-permute-start(bf16[256,512]{1,0:T(8,128)(2,1)S(1)} %collective-permute-done.17.refs_3_), channel_id=1, source_target_pairs={{0,8},{8,0},{1,9},{9,1},{2,10},{10,2},{3,11},{11,3},{4,12},{12,4},... | collective-permute-start | bytes 786440 | tf_op jit(solution)/shard_map/ppermute | solution.py:29
  138.4 7.0 %collective-permute-start.27 = (bf16[256,512]{1,0:T(8,128)(2,1)S(1)}, bf16[256,512]{1,0:T(8,128)(2,1)S(1)}, u32[]{:S(2)}, u32[]{:S(2)}) collective-permute-start(bf16[256,512]{1,0:T(8,128)(2,1)S(1)} %collective-permute-done.23.refs_9_), channel_id=1, source_target_pairs={{0,8},{8,0},{1,9},{9,1},{2,10},{10,2},{3,11},{11,3},{4,12},{12,4},... | collective-permute-start | bytes 786440 | tf_op jit(solution)/shard_map/ppermute | solution.py:29
  154.0 10.2 %collective-permute-start.45 = (bf16[32,4608]{1,0:T(8,128)(2,1)S(1)}, bf16[32,4608]{1,0:T(8,128)(2,1)S(1)}, u32[]{:S(2)}, u32[]{:S(2)}) collective-permute-start(bf16[32,4608]{1,0:T(8,128)(2,1)S(1)} %get-tuple-element.38), channel_id=1, source_target_pairs={{0,2},{2,4},{4,6},{6,0},{1,3},{3,5},{5,7},{7,1},{8,10},{10,12},{12... | collective-permute-start | bytes 884744 | tf_op jit(solution)/shard_map/ppermute | solution.py:29
  155.4 23.7 %collective-permute-start.46 = (bf16[32,4608]{1,0:T(8,128)(2,1)S(1)}, bf16[32,4608]{1,0:T(8,128)(2,1)S(1)}, u32[]{:S(2)}, u32[]{:S(2)}) collective-permute-start(bf16[32,4608]{1,0:T(8,128)(2,1)S(1)} %get-tuple-element.39), channel_id=1, source_target_pairs={{0,4},{2,6},{4,0},{6,2},{1,5},{3,7},{5,1},{7,3},{8,12},{10,14},{12... | collective-permute-start | bytes 884744 | tf_op jit(solution)/shard_map/ppermute | solution.py:29
  156.3 22.9 %collective-permute-start.47 = (bf16[32,4608]{1,0:T(8,128)(2,1)S(1)}, bf16[32,4608]{1,0:T(8,128)(2,1)S(1)}, u32[]{:S(2)}, u32[]{:S(2)}) collective-permute-start(bf16[32,4608]{1,0:T(8,128)(2,1)S(1)} %get-tuple-element.40), channel_id=1, source_target_pairs={{0,6},{2,0},{4,2},{6,4},{1,7},{3,1},{5,3},{7,5},{8,14},{10,8},{12,... | collective-permute-start | bytes 884744 | tf_op jit(solution)/shard_map/ppermute | solution.py:29
  158.2 20.9 %collective-permute-start.48 = (bf16[32,4608]{1,0:T(8,128)(2,1)S(1)}, bf16[32,4608]{1,0:T(8,128)(2,1)S(1)}, u32[]{:S(2)}, u32[]{:S(2)}) collective-permute-start(bf16[32,4608]{1,0:T(8,128)(2,1)S(1)} %get-tuple-element.41), channel_id=1, source_target_pairs={{0,1},{1,0},{2,3},{3,2},{4,5},{5,4},{6,7},{7,6},{8,9},{9,8},{10,11... | collective-permute-start | bytes 884744 | tf_op jit(solution)/shard_map/ppermute | solution.py:29
  158.7 20.4 %collective-permute-start.49 = (bf16[32,4608]{1,0:T(8,128)(2,1)S(1)}, bf16[32,4608]{1,0:T(8,128)(2,1)S(1)}, u32[]{:S(2)}, u32[]{:S(2)}) collective-permute-start(bf16[32,4608]{1,0:T(8,128)(2,1)S(1)} %get-tuple-element.42), channel_id=1, source_target_pairs={{0,3},{1,2},{2,5},{3,4},{4,7},{5,6},{6,1},{7,0},{8,11},{9,10},{10,... | collective-permute-start | bytes 884744 | tf_op jit(solution)/shard_map/ppermute | solution.py:500
  164.2 14.9 %collective-permute-start.50 = (bf16[32,4608]{1,0:T(8,128)(2,1)S(1)}, bf16[32,4608]{1,0:T(8,128)(2,1)S(1)}, u32[]{:S(2)}, u32[]{:S(2)}) collective-permute-start(bf16[32,4608]{1,0:T(8,128)(2,1)S(1)} %get-tuple-element.43), channel_id=1, source_target_pairs={{0,5},{1,4},{2,7},{3,6},{4,1},{5,0},{6,3},{7,2},{8,13},{9,12},{10,... | collective-permute-start | bytes 884744 | tf_op jit(solution)/shard_map/ppermute | solution.py:500
  179.1 11.2 %collective-permute-start.51 = (bf16[32,4608]{1,0:T(8,128)(2,1)S(1)}, bf16[32,4608]{1,0:T(8,128)(2,1)S(1)}, u32[]{:S(2)}, u32[]{:S(2)}) collective-permute-start(bf16[32,4608]{1,0:T(8,128)(2,1)S(1)} %get-tuple-element.44), channel_id=1, source_target_pairs={{0,7},{1,6},{2,1},{3,0},{4,3},{5,2},{6,5},{7,4},{8,15},{9,14},{10,... | collective-permute-start | bytes 884744 | tf_op jit(solution)/shard_map/ppermute | solution.py:500
  190.9 10.9 %collective-permute-start.52 = (bf16[32,4608]{1,0:T(8,128)(2,1)S(1)}, bf16[32,4608]{1,0:T(8,128)(2,1)S(1)}, u32[]{:S(2)}, u32[]{:S(2)}) collective-permute-start(bf16[32,4608]{1,0:T(8,128)(2,1)S(1)} %finish.1.refs_0_), channel_id=1, source_target_pairs={{0,8},{8,0},{1,9},{9,1},{2,10},{10,2},{3,11},{11,3},{4,12},{12,4},... | collective-permute-start | bytes 884744 | tf_op jit(solution)/shard_map/ppermute | solution.py:29
  203.9 9.7 %collective-permute-start.56 = (bf16[16,4608]{1,0:T(8,128)(2,1)S(1)}, bf16[16,4608]{1,0:T(8,128)(2,1)S(1)}, u32[]{:S(2)}, u32[]{:S(2)}) collective-permute-start(bf16[16,4608]{1,0:T(8,128)(2,1)S(1)} %get-tuple-element.47), channel_id=1, source_target_pairs={{0,64},{32,96},{64,0},{96,32},{1,65},{33,97},{65,1},{97,33},{2,66}... | collective-permute-start | bytes 442376 | tf_op jit(solution)/shard_map/ppermute | solution.py:29
  217.4 7.1 %collective-permute-start.59 = (bf16[16,4608]{1,0:T(8,128)(2,1)S(1)}, bf16[16,4608]{1,0:T(8,128)(2,1)S(1)}, u32[]{:S(2)}, u32[]{:S(2)}) collective-permute-start(bf16[16,4608]{1,0:T(8,128)(2,1)S(1)} %get-tuple-element.51), channel_id=1, source_target_pairs={{0,4},{2,6},{4,0},{6,2},{1,5},{3,7},{5,1},{7,3},{8,12},{10,14},{12... | collective-permute-start | bytes 442376 | tf_op jit(solution)/shard_map/ppermute | solution.py:29
  (40 other events, 421.3 us)
Sparse Core Ops, SparseCore 0:
  9.0 79.5 all-gather.1

commit v2 on v0

--- a/solution.py
+++ b/solution.py
@@ -81,18 +81,28 @@
         copy.wait()
 
 
-def join_kernel(key, value, query, joined, sems):
-    jobs, at = [], 0
-    for source, first, width in (
-        (key, 0, HEAD),
-        (value, 0, HEAD),
-        (key, HEAD, HEAD),
-        (value, HEAD, HEAD),
-        (query, 0, 4 * HEAD),
-    ):
-        jobs.append((source.at[:, first : first + width], joined.at[:, at : at + width]))
-        at += width
+def join_kernel(query, out_t, joined, sems):
+    half = 4 * HEAD
+    fetch([(query, joined.at[:, :half]), (out_t, joined.at[:, half:])], sems)
+
+
+def hold_kernel(key, value, after, held, sems):
+    del after
+    jobs = []
+    for n, source in enumerate((key, value, key, value)):
+        first = n // 2 * HEAD
+        jobs.append((source.at[:, first : first + HEAD], held.at[:, n * HEAD : (n + 1) * HEAD]))
     fetch(jobs, sems)
+
+
+def pack_kernel(flat, *refs):
+    parts, whole = refs[:16], refs[16]
+    x, yl, c, _, _ = spot(flat)
+    size = parts[0].shape[0]
+    for n, part in enumerate(parts):
+        w = jnp.bitwise_xor(2 * yl + c, n // 4)
+        first = (4 * jnp.bitwise_and(x - n % 4, 3) + w) * size
+        whole[pl.ds(pl.multiple_of(first, 32), size), :] = part[...]
 
 
 def leave_kernel(flat, old_blocks, order, x_old, *refs):
@@ -176,22 +186,8 @@
         resident[block * 16 : block * 16 + 16, :] = raw[source, :]
 
 
-def key_value_kernel(normed, weight, cos, sin, kv, buffer, total, sems):
-    step = buffer.shape[0] // sems.shape[0]
-
-    def copy(n):
-        rows = pl.ds(n * step, step)
-        return pltpu.make_async_copy(
-            weight.at[rows, : 4 * HEAD], buffer.at[rows, :], sems.at[n]
-        )
-
-    for n in range(sems.shape[0]):
-        copy(n).start()
-    for n in range(sems.shape[0]):
-        copy(n).wait()
-        rows = slice(n * step, (n + 1) * step)
-        part = jnp.dot(normed[:, rows], buffer[rows, :], preferred_element_type=F32)
-        total[...] = part if n == 0 else total[...] + part
+def key_value_kernel(normed, weight, cos, sin, kv):
+    total = jnp.dot(normed[...], weight[...], preferred_element_type=F32)
     for h in range(2):
         at = 2 * h * HEAD
         kv[:, at : at + HEAD] = rope(total[:, at : at + HEAD], cos[...], sin[...]).astype(BF16)
@@ -262,7 +258,8 @@
 
     def copy(n):
         rows = pl.ds(pl.multiple_of(n * tile, tile), tile)
-        return pltpu.make_async_copy(weight.at[rows, :], buffer.at[rows, :], sems.at[n])
+        source = weight.at[rows, 4 * HEAD :]
+        return pltpu.make_async_copy(source, buffer.at[rows, :], sems.at[n])
 
     @pl.loop(0, steps)
     def _(n):
@@ -371,22 +368,38 @@
         )(*tables, *far_off(arrays))
         return list(results)
 
+    def everywhere(part):
+        opposite = shift(part, "x", 2)
+        pair = shift(part, "yl", 1)
+        same = [part, shift(part, "x", 1), opposite, shift(part, "x", 3)]
+        other = [pair, shift(pair, "x", 1), shift(opposite, "yl", 1), shift(pair, "x", 3)]
+        result = []
+        for parts in (same, other):
+            result += parts
+            result += [shift(s, "c", 1) for s in parts]
+        return result
+
     (joined,) = bring(
-        join_kernel,
-        (),
-        (w_key, w_value, w_query),
-        [(w_key.shape[0], 8 * HEAD)],
-        5,
-        jax.ShapeDtypeStruct,
+        join_kernel, (), (w_query, w_out_t), [(w_query.shape[0], 8 * HEAD)], 2, jax.ShapeDtypeStruct
     )
-    qkv_full = lax.all_gather(joined, SEQ, axis=0, tiled=True)
-    out_full = lax.all_gather(w_out_t, SEQ, axis=0, tiled=True)
+    joined_full = lax.all_gather(joined, SEQ, axis=0, tiled=True)
 
     old = far_off((old_blocks, order))
     near = bring(leave_kernel, (flat, *old), (x_old.T,), [(width, BLOCK)] * 4, 4, pltpu.VMEM)
     near = near[:1] + [shift(near[d], "x", d) for d in range(1, 4)]
     far = [shift(part, "c", 1) for part in near]
     mine, cross = call(sort_kernel, old, near + far, [(width, count)] * 2)
+    (held,) = pl.pallas_call(
+        hold_kernel,
+        in_specs=[AWAY, AWAY, VMEM],
+        out_specs=[VMEM],
+        out_shape=[pltpu.VMEM((w_key.shape[0], 4 * HEAD), BF16)],
+        scratch_shapes=[pltpu.SemaphoreType.DMA((4,))],
+        compiler_params=grant(8),
+        name="hold",
+    )(*far_off((w_key, w_value)), *near_by((mine,)))
+    spread_weights = everywhere(held)
+
     cross = shift(cross, "yl", 1)
     (rows,) = call(settle_kernel, old, (mine, cross), [(width, count)])
 
@@ -424,32 +437,21 @@
             out_specs=VMEM,
             out_shape=pltpu.VMEM((count, 4 * HEAD), BF16),
             compiler_params=grant(24),
-        )(*near_by((normed,)), *far_off((qkv_full,)), *tables)
-
+        )(*near_by((normed,)), *far_off((joined_full,)), *tables)
+
+    (kv_weights,) = call(pack_kernel, (), spread_weights, [(D, 4 * HEAD)])
     kv = pl.pallas_call(
         key_value_kernel,
-        in_specs=[VMEM, AWAY, VMEM, VMEM],
+        in_specs=[VMEM] * 4,
         out_specs=VMEM,
         out_shape=pltpu.VMEM((count, 4 * HEAD), BF16),
-        scratch_shapes=[
-            pltpu.VMEM((D, 4 * HEAD), BF16),
-            pltpu.VMEM((count, 4 * HEAD), F32),
-            pltpu.SemaphoreType.DMA((4,)),
-        ],
-        compiler_params=grant(24),
+        compiler_params=grant(16),
         name="key_value",
-    )(*near_by((normed,)), *far_off((qkv_full,)), *tables)
-
-    opposite = shift(kv, "x", 2)
-    same = [kv, shift(kv, "x", 1), opposite, shift(kv, "x", 3)]
-    pair = shift(kv, "yl", 1)
-    other = [pair, shift(pair, "x", 1), shift(same[2], "yl", 1), shift(pair, "x", 3)]
-    spread = []
-    for part in (same, other):
-        spread += part
-        spread += [shift(s, "c", 1) for s in part]
-
-    query = heads(query_kernel, 2)
+    )(*near_by((normed, kv_weights)), *tables)
+
+    spread = everywhere(kv)
+
+    query = heads(query_kernel, 0)
     context = pl.pallas_call(
         attention_kernel,
         in_specs=[SMEM] + [VMEM] * 17,
@@ -473,7 +475,7 @@
         ],
         compiler_params=grant(16),
         name="project",
-    )(flat, *near_by((context,)), *far_off((out_full,)))
+    )(flat, *near_by((context,)), *far_off((joined_full,)))
     received = []
     for dy in range(2):
         for dz in range(4):

time: 218 us -> 239 us (1.096)
  local copies, waits for them, and re-layouts: 0.86 us -> 14 us
  starting transfers between devices: 70.3 us -> 79.8 us
  waiting for transfers between devices: 104 us -> 99.7 us
  Pallas kernels: 26 us -> 28.6 us
    unnamed x5 -> x53, local copies, waits for them, and re-layouts: 0.83 us -> 13.9 us
    ppermute x43 -> x58, starting transfers between devices: 65.4 us -> 76.3 us  [shift(): return lax.ppermute(value, axis, [(i, (i + by) % n) for i in range(n)])]
    all_gather x2 -> x1, waiting for transfers between devices: 4.84 us -> 0.01 us  [per_device(): joined_full = lax.all_gather(joined, SEQ, axis=0, tiled=True)]
    pallas_call x5 -> x6, Pallas kernels: 4.34 us -> 5.96 us  [call(): pl.pallas_call(kernel, in_specs=[SMEM] * (1 + len(tables)) + [VMEM] * len...]
    ppermute x43 -> x58, waiting for transfers between devices: 90.4 us -> 89.7 us  [shift(): return lax.ppermute(value, axis, [(i, (i + by) % n) for i in range(n)])]
  transfers between devices with their start and end apart: 48 -> 62, of which waited for: 22 -> 26; matrix products, arithmetic and copies ran while one was open for 0% -> 0% of each run, Pallas kernels for 8% -> 5%
where the time goes in v2:
time: 239 us; the launch traced here: 237 us
  waiting for transfers between devices  99.7 us (42%)
  starting transfers between devices  79.8 us (33%)
  Pallas kernels  28.6 us (12%)
  local copies, waits for them, and re-layouts  14 us (6%)
  between operations  13.9 us (6%)
    ppermute x58, waiting for transfers between devices, shift(): return lax.ppermute(value, axis, [(i, (i + by) % n) for i in range(n)])  89.7 us
    ppermute x58, starting transfers between devices, shift(): return lax.ppermute(value, axis, [(i, (i + by) % n) for i in range(n)])  76.3 us
    unnamed x53, local copies, waits for them, and re-layouts  13.9 us
    ppermute x3, waiting for transfers between devices, per_device(): lax.ppermute(part, TP, [(2 * i + j, 2 * ((i + dz) % 4) + (j ^ dy)) for i,...  10 us
    pallas_call x1, Pallas kernels, per_device(): pl.pallas_call(attention_kernel, in_specs=[SMEM] + [VMEM] * 17, out_specs...  7.01 us
    pallas_call x6, Pallas kernels, call(): pl.pallas_call(kernel, in_specs=[SMEM] * (1 + len(tables)) + [VMEM] * len...  5.96 us
  transfers between devices with their start and end apart: 62, of which 26 were waited for; matrix products, arithmetic and copies ran while one was open for 0% of the time, Pallas kernels for 5%

profile of v2, /device:TPU:1, one launch (start us, length us, event | category | flops | bytes accessed | tf_op | source)
XLA Modules:
  0.0 236.8 jit_solution(7288044190889872764)
XLA Ops:
  6.5 1.9 shard_map.103
  8.5 1.9 shard_map.100
  10.4 2.1 collective-permute-start
  12.5 2.5 %collective-permute-start.1 = (bf16[576,128]{1,0:T(8,128)(2,1)S(1)}, bf16[576,128]{1,0:T(8,128)(2,1)S(1)}, u32[]{:S(2)}, u32[]{:S(2)}) collective-permute-start(bf16[576,128]{1,0:T(8,128)(2,1)S(1)} %get-tuple-element.31), channel_id=1, source_target_pairs={{0,64},{32,96},{64,0},{96,32},{1,65},{33,97},{65,1},{97,33},{2,66}... | collective-permute-start | bytes 442376 | tf_op jit(solution)/shard_map/ppermute | solution.py:29
  18.5 2.8 %collective-permute-done.1.refs_2_ = bf16[576,128]{1,0:T(8,128)(2,1)S(1)} collective-permute-done((bf16[576,128]{1,0:T(8,128)(2,1)S(1)}, bf16[576,128]{1,0:T(8,128)(2,1)S(1)}, u32[]{:S(2)}, u32[]{:S(2)}) %collective-permute-start.1) | collective-permute-done | bytes 147488 | tf_op jit(solution)/shard_map/ppermute | solution.py:29
  21.3 1.5 collective-permute-start.5
  27.8 2.1 collective-permute-start.16
  30.1 2.6 %collective-permute-start.17 = (bf16[288,512]{1,0:T(8,128)(2,1)S(1)}, bf16[288,512]{1,0:T(8,128)(2,1)}, u32[]{:S(2)}, u32[]{:S(2)}) collective-permute-start(bf16[288,512]{1,0:T(8,128)(2,1)S(1)} %hold.1.refs_0_), channel_id=1, source_target_pairs={{0,96},{32,0},{64,32},{96,64},{1,97},{33,1},{65,33},{97,65},{2,98}... | collective-permute-start | bytes 884744 | tf_op jit(solution)/shard_map/ppermute | solution.py:29
  32.6 9.2 %collective-permute-done.22.refs_8_ = bf16[288,512]{1,0:T(8,128)(2,1)} collective-permute-done((bf16[288,512]{1,0:T(8,128)(2,1)S(1)}, bf16[288,512]{1,0:T(8,128)(2,1)}, u32[]{:S(2)}, u32[]{:S(2)}) %collective-permute-start.22) | collective-permute-done | bytes 294944 | tf_op jit(solution)/shard_map/ppermute | solution.py:29
  45.1 9.4 %collective-permute-done.7.crossed = bf16[576,256]{1,0:T(8,128)(2,1)S(1)} collective-permute-done((bf16[576,256]{1,0:T(8,128)(2,1)S(1)}, bf16[576,256]{1,0:T(8,128)(2,1)S(1)}, u32[]{:S(2)}, u32[]{:S(2)}) %collective-permute-start.7) | collective-permute-done | bytes 294944 | tf_op jit(solution)/shard_map/ppermute | solution.py:29
  56.7 1.6 collective-permute-start.25
  58.3 1.5 collective-permute-start.19
  60.6 2.6 %collective-permute-start.11 = (bf16[576,256]{1,0:T(8,128)(2,1)S(1)}, bf16[576,256]{1,0:T(8,128)(2,1)S(1)}, u32[]{:S(2)}, u32[]{:S(2)}) collective-permute-start(bf16[576,256]{1,0:T(8,128)(2,1)S(1)} %shard_map.102.refs_0_), channel_id=1, source_target_pairs={{0,1},{1,0},{2,3},{3,2},{4,5},{5,4},{6,7},{7,6},{8,9},{9,8},{10,11... | collective-permute-start | bytes 884744 | tf_op jit(solution)/shard_map/ppermute | solution.py:29
  63.2 5.0 %collective-permute-done.23.refs_9_ = bf16[288,512]{1,0:T(8,128)(2,1)} collective-permute-done((bf16[288,512]{1,0:T(8,128)(2,1)}, bf16[288,512]{1,0:T(8,128)(2,1)}, u32[]{:S(2)}, u32[]{:S(2)}) %collective-permute-start.23) | collective-permute-done | bytes 294944 | tf_op jit(solution)/shard_map/ppermute | solution.py:29
  69.7 3.7 %collective-permute-start.10 = (bf16[576,256]{1,0:T(8,128)(2,1)S(1)}, bf16[576,256]{1,0:T(8,128)(2,1)S(1)}, u32[]{:S(2)}, u32[]{:S(2)}) collective-permute-start(bf16[576,256]{1,0:T(8,128)(2,1)S(1)} %shard_map.102.refs_0_), channel_id=1, source_target_pairs={{0,6},{2,0},{4,2},{6,4},{1,7},{3,1},{5,3},{7,5},{8,14},{10,8},{12,... | collective-permute-start | bytes 884744 | tf_op jit(solution)/shard_map/ppermute | solution.py:29
  73.7 3.3 %collective-permute-start.9 = (bf16[576,256]{1,0:T(8,128)(2,1)S(1)}, bf16[576,256]{1,0:T(8,128)(2,1)S(1)}, u32[]{:S(2)}, u32[]{:S(2)}) collective-permute-start(bf16[576,256]{1,0:T(8,128)(2,1)S(1)} %shard_map.102.refs_0_), channel_id=1, source_target_pairs={{0,4},{2,6},{4,0},{6,2},{1,5},{3,7},{5,1},{7,3},{8,12},{10,14},{12... | collective-permute-start | bytes 884744 | tf_op jit(solution)/shard_map/ppermute | solution.py:29
  77.0 7.7 %collective-permute-done.11.refs_4_ = bf16[576,256]{1,0:T(8,128)(2,1)S(1)} collective-permute-done((bf16[576,256]{1,0:T(8,128)(2,1)S(1)}, bf16[576,256]{1,0:T(8,128)(2,1)S(1)}, u32[]{:S(2)}, u32[]{:S(2)}) %collective-permute-start.11) | collective-permute-done | bytes 294944 | tf_op jit(solution)/shard_map/ppermute | solution.py:29
  84.7 1.6 collective-permute-start.12
  87.0 3.4 %collective-permute-start.13 = (bf16[576,256]{1,0:T(8,128)(2,1)S(1)}, bf16[576,256]{1,0:T(8,128)(2,1)S(1)}, u32[]{:S(2)}, u32[]{:S(2)}) collective-permute-start(bf16[576,256]{1,0:T(8,128)(2,1)S(1)} %collective-permute-done.11.refs_4_), channel_id=1, source_target_pairs={{0,4},{2,6},{4,0},{6,2},{1,5},{3,7},{5,1},{7,3},{8,12},{10,14},{12... | collective-permute-start | bytes 884744 | tf_op jit(solution)/shard_map/ppermute | solution.py:29
  92.5 2.5 %collective-permute-start.26 = (bf16[288,512]{1,0:T(8,128)(2,1)}, bf16[288,512]{1,0:T(8,128)(2,1)S(1)}, u32[]{:S(2)}, u32[]{:S(2)}) collective-permute-start(bf16[288,512]{1,0:T(8,128)(2,1)} %collective-permute-done.22.refs_8_), channel_id=1, source_target_pairs={{0,8},{8,0},{1,9},{9,1},{2,10},{10,2},{3,11},{11,3},{4,12},{12,4},... | collective-permute-start | bytes 884744 | tf_op jit(solution)/shard_map/ppermute | solution.py:29
  95.1 2.7 %collective-permute-done.12.refs_5_ = bf16[576,256]{1,0:T(8,128)(2,1)S(1)} collective-permute-done((bf16[576,256]{1,0:T(8,128)(2,1)S(1)}, bf16[576,256]{1,0:T(8,128)(2,1)S(1)}, u32[]{:S(2)}, u32[]{:S(2)}) %collective-permute-start.12) | collective-permute-done | bytes 294944 | tf_op jit(solution)/shard_map/ppermute | solution.py:29
  97.9 1.6 collective-permute-start.27
  99.5 2.2 collective-permute-done.13.refs_6_
  101.6 2.4 %collective-permute-start.28 = (bf16[288,512]{1,0:T(8,128)(2,1)}, bf16[288,512]{1,0:T(8,128)(2,1)S(1)}, u32[]{:S(2)}, u32[]{:S(2)}) collective-permute-start(bf16[288,512]{1,0:T(8,128)(2,1)} %collective-permute-done.24.refs_10_), channel_id=1, source_target_pairs={{0,8},{8,0},{1,9},{9,1},{2,10},{10,2},{3,11},{11,3},{4,12},{12,4},... | collective-permute-start | bytes 884744 | tf_op jit(solution)/shard_map/ppermute | solution.py:29
  112.9 1.6 shard_map.105.weight
  117.3 1.5 collective-permute-start.30
  121.6 1.9 collective-permute-done.37.refs_8_
  123.5 2.1 collective-permute-start.38
  126.3 5.8 %collective-permute-done.30.refs_1_ = bf16[256,512]{1,0:T(8,128)(2,1)S(1)} collective-permute-done((bf16[256,512]{1,0:T(8,128)(2,1)S(1)}, bf16[256,512]{1,0:T(8,128)(2,1)S(1)}, u32[]{:S(2)}, u32[]{:S(2)}) %collective-permute-start.30) | collective-permute-done | bytes 262176 | tf_op jit(solution)/shard_map/ppermute | solution.py:29
  132.1 2.1 collective-permute-start.34
  136.3 1.5 collective-permute-done.38.refs_9_
  142.9 3.5 %shard_map.104.query = bf16[256,512]{1,0:T(8,128)(2,1)S(1)} custom-call(bf16[256,4608]{1,0:T(8,128)(2,1)S(1)} %get-tuple-element.36.normed, bf16[4608,1024]{1,0:T(8,128)(2,1)} %all-gather.2.cloned.1.call-done.weight, f32[256,128]{1,0:T(8,128)S(1)} %pad_maximum_fusion.cos, f32[256,128]{1,0:T(8,128)S(1)} %pad_maximum_fusion.1.sin), custom_call_target="tpu_custom_call" | custom-call | tf_op jit(solution)/shard_map/pallas_call | solution.py:433
  146.5 7.0 %attention.1.context = bf16[256,512]{1,0:T(8,128)(2,1)S(1)} custom-call(s32[1]{0:T(128)} %bitcast.flat, bf16[256,512]{1,0:T(8,128)(2,1)S(1)} %shard_map.104.query, bf16[256,512]{1,0:T(8,128)(2,1)S(1)} %key_value.1.refs_0_, bf16[256,512]{1,0:T(8,128)(2,1)S(1)} %copy-done.17, bf16[256,512]{1,0:T(8,128)(2,1)S(1)} %copy-done.15, ...), custom_call_target="tpu_custom_call" | custom-call | tf_op jit(solution)/shard_map/attention/pallas_call | solution.py:455
  153.5 4.3 %project.1 = (bf16[32,4608]{1,0:T(8,128)(2,1)S(1)}, bf16[32,4608]{1,0:T(8,128)(2,1)S(1)}, bf16[32,4608]{1,0:T(8,128)(2,1)S(1)}, bf16[32,4608]{1,0:T(8,128)(2,1)S...) custom-call(s32[1]{0:T(128)} %bitcast.flat, ...), custom_call_target="tpu_custom_call" | custom-call | tf_op jit(solution)/shard_map/project/pallas_call | solution.py:466
  158.6 2.2 collective-permute-start.46
  162.8 2.2 collective-permute-start.49
  165.0 2.7 %collective-permute-done.45.refs_1_ = bf16[32,4608]{1,0:T(8,128)(2,1)S(1)} collective-permute-done((bf16[32,4608]{1,0:T(8,128)(2,1)S(1)}, bf16[32,4608]{1,0:T(8,128)(2,1)S(1)}, u32[]{:S(2)}, u32[]{:S(2)}) %collective-permute-start.45) | collective-permute-done | bytes 294944 | tf_op jit(solution)/shard_map/ppermute | solution.py:29
  169.0 17.9 %collective-permute-done.46.refs_2_ = bf16[32,4608]{1,0:T(8,128)(2,1)S(1)} collective-permute-done((bf16[32,4608]{1,0:T(8,128)(2,1)S(1)}, bf16[32,4608]{1,0:T(8,128)(2,1)S(1)}, u32[]{:S(2)}, u32[]{:S(2)}) %collective-permute-start.46) | collective-permute-done | bytes 294944 | tf_op jit(solution)/shard_map/ppermute | solution.py:29
  186.9 10.0 %collective-permute-done.51.refs_7_ = bf16[32,4608]{1,0:T(8,128)(2,1)S(1)} collective-permute-done((bf16[32,4608]{1,0:T(8,128)(2,1)S(1)}, bf16[32,4608]{1,0:T(8,128)(2,1)S(1)}, u32[]{:S(2)}, u32[]{:S(2)}) %collective-permute-start.51) | collective-permute-done | bytes 294944 | tf_op jit(solution)/shard_map/ppermute | solution.py:485
  198.9 2.2 collective-permute-start.52
  201.2 3.2 %collective-permute-done.53.refs_2_ = bf16[32,4608]{1,0:T(8,128)(2,1)S(1)} collective-permute-done((bf16[32,4608]{1,0:T(8,128)(2,1)S(1)}, bf16[32,4608]{1,0:T(8,128)(2,1)S(1)}, u32[]{:S(2)}, u32[]{:S(2)}) %collective-permute-start.53) | collective-permute-done | bytes 294944 | tf_op jit(solution)/shard_map/ppermute | solution.py:29
  204.4 2.6 %collective-permute-start.54 = (bf16[32,4608]{1,0:T(8,128)(2,1)S(1)}, bf16[32,4608]{1,0:T(8,128)(2,1)S(1)}, u32[]{:S(2)}, u32[]{:S(2)}) collective-permute-start(bf16[32,4608]{1,0:T(8,128)(2,1)S(1)} %collective-permute-done.53.refs_2_), channel_id=1, source_target_pairs={{0,8},{8,0},{1,9},{9,1},{2,10},{10,2},{3,11},{11,3},{4,12},{12,4},... | collective-permute-start | bytes 884744 | tf_op jit(solution)/shard_map/ppermute | solution.py:29
  209.3 2.3 collective-permute-start.56
  212.8 2.9 %collective-permute-done.55.refs_1_ = bf16[16,4608]{1,0:T(8,128)(2,1)S(1)} collective-permute-done((bf16[16,4608]{1,0:T(8,128)(2,1)S(1)}, bf16[16,4608]{1,0:T(8,128)(2,1)S(1)}, u32[]{:S(2)}, u32[]{:S(2)}) %collective-permute-start.55) | collective-permute-done | bytes 147488 | tf_op jit(solution)/shard_map/ppermute | solution.py:29
  215.7 2.7 %collective-permute-done.56.refs_2_ = bf16[16,4608]{1,0:T(8,128)(2,1)S(1)} collective-permute-done((bf16[16,4608]{1,0:T(8,128)(2,1)S(1)}, bf16[16,4608]{1,0:T(8,128)(2,1)S(1)}, u32[]{:S(2)}, u32[]{:S(2)}) %collective-permute-start.56) | collective-permute-done | bytes 147488 | tf_op jit(solution)/shard_map/ppermute | solution.py:29
  219.7 1.9 collective-permute-start.59
  222.4 3.6 %collective-permute-done.58.refs_1_ = bf16[16,4608]{1,0:T(8,128)(2,1)S(1)} collective-permute-done((bf16[16,4608]{1,0:T(8,128)(2,1)S(1)}, bf16[16,4608]{1,0:T(8,128)(2,1)S(1)}, u32[]{:S(2)}, u32[]{:S(2)}) %collective-permute-start.58) | collective-permute-done | bytes 147488 | tf_op jit(solution)/shard_map/ppermute | solution.py:29
  226.0 1.7 collective-permute-done.59.refs_2_
  (153 shorter events, 55.7 us)
Async XLA Ops:
  6.5 136.3 %all-gather.2.cloned.1.call-start = ((), (), s32[]{:S(2)}) async-start(), calls=%async_computation | async-start | bytes 10027008 | tf_op jit(solution)/shard_map/all_gather | solution.py:385
  10.4 7.2 %collective-permute-start = (bf16[576,128]{1,0:T(8,128)(2,1)S(1)}, bf16[576,128]{1,0:T(8,128)(2,1)S(1)}, u32[]{:S(2)}, u32[]{:S(2)}) collective-permute-start(bf16[576,128]{1,0:T(8,128)(2,1)S(1)} %get-tuple-element.30), channel_id=1, source_target_pairs={{0,32},{32,64},{64,96},{96,0},{1,33},{33,65},{65,97},{97,1},{2,34}... | collective-permute-start | bytes 442376 | tf_op jit(solution)/shard_map/ppermute | solution.py:29
  12.5 8.9 %collective-permute-start.1 = (bf16[576,128]{1,0:T(8,128)(2,1)S(1)}, bf16[576,128]{1,0:T(8,128)(2,1)S(1)}, u32[]{:S(2)}, u32[]{:S(2)}) collective-permute-start(bf16[576,128]{1,0:T(8,128)(2,1)S(1)} %get-tuple-element.31), channel_id=1, source_target_pairs={{0,64},{32,96},{64,0},{96,32},{1,65},{33,97},{65,1},{97,33},{2,66}... | collective-permute-start | bytes 442376 | tf_op jit(solution)/shard_map/ppermute | solution.py:29
  14.9 8.0 %collective-permute-start.2 = (bf16[576,128]{1,0:T(8,128)(2,1)S(1)}, bf16[576,128]{1,0:T(8,128)(2,1)S(1)}, u32[]{:S(2)}, u32[]{:S(2)}) collective-permute-start(bf16[576,128]{1,0:T(8,128)(2,1)S(1)} %get-tuple-element.32), channel_id=1, source_target_pairs={{0,96},{32,0},{64,32},{96,64},{1,97},{33,1},{65,33},{97,65},{2,98}... | collective-permute-start | bytes 442376 | tf_op jit(solution)/shard_map/ppermute | solution.py:29
  26.4 15.5 %collective-permute-start.22 = (bf16[288,512]{1,0:T(8,128)(2,1)S(1)}, bf16[288,512]{1,0:T(8,128)(2,1)}, u32[]{:S(2)}, u32[]{:S(2)}) collective-permute-start(bf16[288,512]{1,0:T(8,128)(2,1)S(1)} %hold.1.refs_0_), channel_id=1, source_target_pairs={{0,16},{16,0},{1,17},{17,1},{2,18},{18,2},{3,19},{19,3},{4,20},{20... | collective-permute-start | bytes 884744 | tf_op jit(solution)/shard_map/ppermute | solution.py:29
  27.8 16.7 %collective-permute-start.16 = (bf16[288,512]{1,0:T(8,128)(2,1)S(1)}, bf16[288,512]{1,0:T(8,128)(2,1)S(1)}, u32[]{:S(2)}, u32[]{:S(2)}) collective-permute-start(bf16[288,512]{1,0:T(8,128)(2,1)S(1)} %hold.1.refs_0_), channel_id=1, source_target_pairs={{0,64},{32,96},{64,0},{96,32},{1,65},{33,97},{65,1},{97,33},{2,66}... | collective-permute-start | bytes 884744 | tf_op jit(solution)/shard_map/ppermute | solution.py:29
  29.9 24.7 %collective-permute-start.7 = (bf16[576,256]{1,0:T(8,128)(2,1)S(1)}, bf16[576,256]{1,0:T(8,128)(2,1)S(1)}, u32[]{:S(2)}, u32[]{:S(2)}) collective-permute-start(bf16[576,256]{1,0:T(8,128)(2,1)S(1)} %get-tuple-element.34), channel_id=1, source_target_pairs={{0,16},{16,0},{1,17},{17,1},{2,18},{18,2},{3,19},{19,3},{4,20},{20... | collective-permute-start | bytes 884744 | tf_op jit(solution)/shard_map/ppermute | solution.py:29
  30.0 26.7 %collective-permute-start.15 = (bf16[288,512]{1,0:T(8,128)(2,1)S(1)}, bf16[288,512]{1,0:T(8,128)(2,1)S(1)}, u32[]{:S(2)}, u32[]{:S(2)}) collective-permute-start(bf16[288,512]{1,0:T(8,128)(2,1)S(1)} %hold.1.refs_0_), channel_id=1, source_target_pairs={{0,32},{32,64},{64,96},{96,0},{1,33},{33,65},{65,97},{97,1},{2,34}... | collective-permute-start | bytes 884744 | tf_op jit(solution)/shard_map/ppermute | solution.py:29
  30.1 28.2 %collective-permute-start.17 = (bf16[288,512]{1,0:T(8,128)(2,1)S(1)}, bf16[288,512]{1,0:T(8,128)(2,1)}, u32[]{:S(2)}, u32[]{:S(2)}) collective-permute-start(bf16[288,512]{1,0:T(8,128)(2,1)S(1)} %hold.1.refs_0_), channel_id=1, source_target_pairs={{0,96},{32,0},{64,32},{96,64},{1,97},{33,1},{65,33},{97,65},{2,98}... | collective-permute-start | bytes 884744 | tf_op jit(solution)/shard_map/ppermute | solution.py:29
  41.9 18.0 %collective-permute-start.18 = (bf16[288,512]{1,0:T(8,128)(2,1)S(1)}, bf16[288,512]{1,0:T(8,128)(2,1)S(1)}, u32[]{:S(2)}, u32[]{:S(2)}) collective-permute-start(bf16[288,512]{1,0:T(8,128)(2,1)S(1)} %hold.1.refs_0_), channel_id=1, source_target_pairs={{0,8},{8,0},{1,9},{9,1},{2,10},{10,2},{3,11},{11,3},{4,12},{12,4},... | collective-permute-start | bytes 884744 | tf_op jit(solution)/shard_map/ppermute | solution.py:29
  44.5 23.7 %collective-permute-start.23 = (bf16[288,512]{1,0:T(8,128)(2,1)}, bf16[288,512]{1,0:T(8,128)(2,1)}, u32[]{:S(2)}, u32[]{:S(2)}) collective-permute-start(bf16[288,512]{1,0:T(8,128)(2,1)} %collective-permute-done.22.refs_8_), channel_id=1, source_target_pairs={{0,32},{32,64},{64,96},{96,0},{1,33},{33,65},{65,97},{97,1},{2,34}... | collective-permute-start | bytes 884744 | tf_op jit(solution)/shard_map/ppermute | solution.py:29
  54.5 15.2 %collective-permute-start.24 = (bf16[288,512]{1,0:T(8,128)(2,1)S(1)}, bf16[288,512]{1,0:T(8,128)(2,1)}, u32[]{:S(2)}, u32[]{:S(2)}) collective-permute-start(bf16[288,512]{1,0:T(8,128)(2,1)S(1)} %collective-permute-done.16.refs_2_), channel_id=1, source_target_pairs={{0,16},{16,0},{1,17},{17,1},{2,18},{18,2},{3,19},{19,3},{4,20},{20... | collective-permute-start | bytes 884744 | tf_op jit(solution)/shard_map/ppermute | solution.py:29
  56.7 16.8 %collective-permute-start.25 = (bf16[288,512]{1,0:T(8,128)(2,1)}, bf16[288,512]{1,0:T(8,128)(2,1)}, u32[]{:S(2)}, u32[]{:S(2)}) collective-permute-start(bf16[288,512]{1,0:T(8,128)(2,1)} %collective-permute-done.22.refs_8_), channel_id=1, source_target_pairs={{0,96},{32,0},{64,32},{96,64},{1,97},{33,1},{65,33},{97,65},{2,98}... | collective-permute-start | bytes 884744 | tf_op jit(solution)/shard_map/ppermute | solution.py:29
  58.3 15.4 %collective-permute-start.19 = (bf16[288,512]{1,0:T(8,128)(2,1)S(1)}, bf16[288,512]{1,0:T(8,128)(2,1)S(1)}, u32[]{:S(2)}, u32[]{:S(2)}) collective-permute-start(bf16[288,512]{1,0:T(8,128)(2,1)S(1)} %collective-permute-done.15.refs_1_), channel_id=1, source_target_pairs={{0,8},{8,0},{1,9},{9,1},{2,10},{10,2},{3,11},{11,3},{4,12},{12,4},... | collective-permute-start | bytes 884744 | tf_op jit(solution)/shard_map/ppermute | solution.py:29
  60.6 24.1 %collective-permute-start.11 = (bf16[576,256]{1,0:T(8,128)(2,1)S(1)}, bf16[576,256]{1,0:T(8,128)(2,1)S(1)}, u32[]{:S(2)}, u32[]{:S(2)}) collective-permute-start(bf16[576,256]{1,0:T(8,128)(2,1)S(1)} %shard_map.102.refs_0_), channel_id=1, source_target_pairs={{0,1},{1,0},{2,3},{3,2},{4,5},{5,4},{6,7},{7,6},{8,9},{9,8},{10,11... | collective-permute-start | bytes 884744 | tf_op jit(solution)/shard_map/ppermute | solution.py:29
  68.2 18.1 %collective-permute-start.20 = (bf16[288,512]{1,0:T(8,128)(2,1)S(1)}, bf16[288,512]{1,0:T(8,128)(2,1)S(1)}, u32[]{:S(2)}, u32[]{:S(2)}) collective-permute-start(bf16[288,512]{1,0:T(8,128)(2,1)S(1)} %collective-permute-done.16.refs_2_), channel_id=1, source_target_pairs={{0,8},{8,0},{1,9},{9,1},{2,10},{10,2},{3,11},{11,3},{4,12},{12,4},... | collective-permute-start | bytes 884744 | tf_op jit(solution)/shard_map/ppermute | solution.py:29
  69.7 20.7 %collective-permute-start.10 = (bf16[576,256]{1,0:T(8,128)(2,1)S(1)}, bf16[576,256]{1,0:T(8,128)(2,1)S(1)}, u32[]{:S(2)}, u32[]{:S(2)}) collective-permute-start(bf16[576,256]{1,0:T(8,128)(2,1)S(1)} %shard_map.102.refs_0_), channel_id=1, source_target_pairs={{0,6},{2,0},{4,2},{6,4},{1,7},{3,1},{5,3},{7,5},{8,14},{10,8},{12,... | collective-permute-start | bytes 884744 | tf_op jit(solution)/shard_map/ppermute | solution.py:29
  73.5 19.1 %collective-permute-start.8 = (bf16[576,256]{1,0:T(8,128)(2,1)S(1)}, bf16[576,256]{1,0:T(8,128)(2,1)S(1)}, u32[]{:S(2)}, u32[]{:S(2)}) collective-permute-start(bf16[576,256]{1,0:T(8,128)(2,1)S(1)} %shard_map.102.refs_0_), channel_id=1, source_target_pairs={{0,2},{2,4},{4,6},{6,0},{1,3},{3,5},{5,7},{7,1},{8,10},{10,12},{12... | collective-permute-start | bytes 884744 | tf_op jit(solution)/shard_map/ppermute | solution.py:29
  73.7 21.3 %collective-permute-start.9 = (bf16[576,256]{1,0:T(8,128)(2,1)S(1)}, bf16[576,256]{1,0:T(8,128)(2,1)S(1)}, u32[]{:S(2)}, u32[]{:S(2)}) collective-permute-start(bf16[576,256]{1,0:T(8,128)(2,1)S(1)} %shard_map.102.refs_0_), channel_id=1, source_target_pairs={{0,4},{2,6},{4,0},{6,2},{1,5},{3,7},{5,1},{7,3},{8,12},{10,14},{12... | collective-permute-start | bytes 884744 | tf_op jit(solution)/shard_map/ppermute | solution.py:29
  84.7 13.1 %collective-permute-start.12 = (bf16[576,256]{1,0:T(8,128)(2,1)S(1)}, bf16[576,256]{1,0:T(8,128)(2,1)S(1)}, u32[]{:S(2)}, u32[]{:S(2)}) collective-permute-start(bf16[576,256]{1,0:T(8,128)(2,1)S(1)} %collective-permute-done.11.refs_4_), channel_id=1, source_target_pairs={{0,2},{2,4},{4,6},{6,0},{1,3},{3,5},{5,7},{7,1},{8,10},{10,12},{12... | collective-permute-start | bytes 884744 | tf_op jit(solution)/shard_map/ppermute | solution.py:29
  87.0 14.6 %collective-permute-start.13 = (bf16[576,256]{1,0:T(8,128)(2,1)S(1)}, bf16[576,256]{1,0:T(8,128)(2,1)S(1)}, u32[]{:S(2)}, u32[]{:S(2)}) collective-permute-start(bf16[576,256]{1,0:T(8,128)(2,1)S(1)} %collective-permute-done.11.refs_4_), channel_id=1, source_target_pairs={{0,4},{2,6},{4,0},{6,2},{1,5},{3,7},{5,1},{7,3},{8,12},{10,14},{12... | collective-permute-start | bytes 884744 | tf_op jit(solution)/shard_map/ppermute | solution.py:29
  91.1 12.9 %collective-permute-start.14 = (bf16[576,256]{1,0:T(8,128)(2,1)S(1)}, bf16[576,256]{1,0:T(8,128)(2,1)S(1)}, u32[]{:S(2)}, u32[]{:S(2)}) collective-permute-start(bf16[576,256]{1,0:T(8,128)(2,1)S(1)} %collective-permute-done.11.refs_4_), channel_id=1, source_target_pairs={{0,6},{2,0},{4,2},{6,4},{1,7},{3,1},{5,3},{7,5},{8,14},{10,8},{12,... | collective-permute-start | bytes 884744 | tf_op jit(solution)/shard_map/ppermute | solution.py:29
  92.5 15.5 %collective-permute-start.26 = (bf16[288,512]{1,0:T(8,128)(2,1)}, bf16[288,512]{1,0:T(8,128)(2,1)S(1)}, u32[]{:S(2)}, u32[]{:S(2)}) collective-permute-start(bf16[288,512]{1,0:T(8,128)(2,1)} %collective-permute-done.22.refs_8_), channel_id=1, source_target_pairs={{0,8},{8,0},{1,9},{9,1},{2,10},{10,2},{3,11},{11,3},{4,12},{12,4},... | collective-permute-start | bytes 884744 | tf_op jit(solution)/shard_map/ppermute | solution.py:29
  95.0 13.0 %collective-permute-start.21 = (bf16[288,512]{1,0:T(8,128)(2,1)}, bf16[288,512]{1,0:T(8,128)(2,1)S(1)}, u32[]{:S(2)}, u32[]{:S(2)}) collective-permute-start(bf16[288,512]{1,0:T(8,128)(2,1)} %collective-permute-done.17.refs_3_), channel_id=1, source_target_pairs={{0,8},{8,0},{1,9},{9,1},{2,10},{10,2},{3,11},{11,3},{4,12},{12,4},... | collective-permute-start | bytes 884744 | tf_op jit(solution)/shard_map/ppermute | solution.py:29
  97.9 10.2 %collective-permute-start.27 = (bf16[288,512]{1,0:T(8,128)(2,1)}, bf16[288,512]{1,0:T(8,128)(2,1)S(1)}, u32[]{:S(2)}, u32[]{:S(2)}) collective-permute-start(bf16[288,512]{1,0:T(8,128)(2,1)} %collective-permute-done.23.refs_9_), channel_id=1, source_target_pairs={{0,8},{8,0},{1,9},{9,1},{2,10},{10,2},{3,11},{11,3},{4,12},{12,4},... | collective-permute-start | bytes 884744 | tf_op jit(solution)/shard_map/ppermute | solution.py:29
  115.9 7.6 %collective-permute-start.37 = (bf16[256,512]{1,0:T(8,128)(2,1)S(1)}, bf16[256,512]{1,0:T(8,128)(2,1)S(1)}, u32[]{:S(2)}, u32[]{:S(2)}) collective-permute-start(bf16[256,512]{1,0:T(8,128)(2,1)S(1)} %key_value.1.refs_0_), channel_id=1, source_target_pairs={{0,16},{16,0},{1,17},{17,1},{2,18},{18,2},{3,19},{19,3},{4,20},{20... | collective-permute-start | bytes 786440 | tf_op jit(solution)/shard_map/ppermute | solution.py:29
  116.8 8.9 %collective-permute-start.31 = (bf16[256,512]{1,0:T(8,128)(2,1)S(1)}, bf16[256,512]{1,0:T(8,128)(2,1)S(1)}, u32[]{:S(2)}, u32[]{:S(2)}) collective-permute-start(bf16[256,512]{1,0:T(8,128)(2,1)S(1)} %key_value.1.refs_0_), channel_id=1, source_target_pairs={{0,64},{32,96},{64,0},{96,32},{1,65},{33,97},{65,1},{97,33},{2,66}... | collective-permute-start | bytes 786440 | tf_op jit(solution)/shard_map/ppermute | solution.py:29
  117.3 14.8 %collective-permute-start.30 = (bf16[256,512]{1,0:T(8,128)(2,1)S(1)}, bf16[256,512]{1,0:T(8,128)(2,1)S(1)}, u32[]{:S(2)}, u32[]{:S(2)}) collective-permute-start(bf16[256,512]{1,0:T(8,128)(2,1)S(1)} %key_value.1.refs_0_), channel_id=1, source_target_pairs={{0,32},{32,64},{64,96},{96,0},{1,33},{33,65},{65,97},{97,1},{2,34}... | collective-permute-start | bytes 786440 | tf_op jit(solution)/shard_map/ppermute | solution.py:29
  118.9 13.2 %collective-permute-start.32 = (bf16[256,512]{1,0:T(8,128)(2,1)S(1)}, bf16[256,512]{1,0:T(8,128)(2,1)}, u32[]{:S(2)}, u32[]{:S(2)}) collective-permute-start(bf16[256,512]{1,0:T(8,128)(2,1)S(1)} %key_value.1.refs_0_), channel_id=1, source_target_pairs={{0,96},{32,0},{64,32},{96,64},{1,97},{33,1},{65,33},{97,65},{2,98}... | collective-permute-start | bytes 786440 | tf_op jit(solution)/shard_map/ppermute | solution.py:29
  120.3 14.7 %collective-permute-start.33 = (bf16[256,512]{1,0:T(8,128)(2,1)S(1)}, bf16[256,512]{1,0:T(8,128)(2,1)S(1)}, u32[]{:S(2)}, u32[]{:S(2)}) collective-permute-start(bf16[256,512]{1,0:T(8,128)(2,1)S(1)} %key_value.1.refs_0_), channel_id=1, source_target_pairs={{0,8},{8,0},{1,9},{9,1},{2,10},{10,2},{3,11},{11,3},{4,12},{12,4},... | collective-permute-start | bytes 786440 | tf_op jit(solution)/shard_map/ppermute | solution.py:29
  123.5 14.3 %collective-permute-start.38 = (bf16[256,512]{1,0:T(8,128)(2,1)S(1)}, bf16[256,512]{1,0:T(8,128)(2,1)}, u32[]{:S(2)}, u32[]{:S(2)}) collective-permute-start(bf16[256,512]{1,0:T(8,128)(2,1)S(1)} %collective-permute-done.37.refs_8_), channel_id=1, source_target_pairs={{0,32},{32,64},{64,96},{96,0},{1,33},{33,65},{65,97},{97,1},{2,34}... | collective-permute-start | bytes 786440 | tf_op jit(solution)/shard_map/ppermute | solution.py:29
  125.6 12.7 %collective-permute-start.39 = (bf16[256,512]{1,0:T(8,128)(2,1)S(1)}, bf16[256,512]{1,0:T(8,128)(2,1)}, u32[]{:S(2)}, u32[]{:S(2)}) collective-permute-start(bf16[256,512]{1,0:T(8,128)(2,1)S(1)} %collective-permute-done.31.refs_2_), channel_id=1, source_target_pairs={{0,16},{16,0},{1,17},{17,1},{2,18},{18,2},{3,19},{19,3},{4,20},{20... | collective-permute-start | bytes 786440 | tf_op jit(solution)/shard_map/ppermute | solution.py:29
  132.1 7.4 %collective-permute-start.40 = (bf16[256,512]{1,0:T(8,128)(2,1)S(1)}, bf16[256,512]{1,0:T(8,128)(2,1)}, u32[]{:S(2)}, u32[]{:S(2)}) collective-permute-start(bf16[256,512]{1,0:T(8,128)(2,1)S(1)} %collective-permute-done.37.refs_8_), channel_id=1, source_target_pairs={{0,96},{32,0},{64,32},{96,64},{1,97},{33,1},{65,33},{97,65},{2,98}... | collective-permute-start | bytes 786440 | tf_op jit(solution)/shard_map/ppermute | solution.py:29
  132.1 8.8 %collective-permute-start.34 = (bf16[256,512]{1,0:T(8,128)(2,1)S(1)}, bf16[256,512]{1,0:T(8,128)(2,1)S(1)}, u32[]{:S(2)}, u32[]{:S(2)}) collective-permute-start(bf16[256,512]{1,0:T(8,128)(2,1)S(1)} %collective-permute-done.30.refs_1_), channel_id=1, source_target_pairs={{0,8},{8,0},{1,9},{9,1},{2,10},{10,2},{3,11},{11,3},{4,12},{12,4},... | collective-permute-start | bytes 786440 | tf_op jit(solution)/shard_map/ppermute | solution.py:29
  137.8 8.6 %collective-permute-start.41 = (bf16[256,512]{1,0:T(8,128)(2,1)S(1)}, bf16[256,512]{1,0:T(8,128)(2,1)}, u32[]{:S(2)}, u32[]{:S(2)}) collective-permute-start(bf16[256,512]{1,0:T(8,128)(2,1)S(1)} %collective-permute-done.37.refs_8_), channel_id=1, source_target_pairs={{0,8},{8,0},{1,9},{9,1},{2,10},{10,2},{3,11},{11,3},{4,12},{12,4},... | collective-permute-start | bytes 786440 | tf_op jit(solution)/shard_map/ppermute | solution.py:29
  138.3 8.1 %collective-permute-start.36 = (bf16[256,512]{1,0:T(8,128)(2,1)}, bf16[256,512]{1,0:T(8,128)(2,1)}, u32[]{:S(2)}, u32[]{:S(2)}) collective-permute-start(bf16[256,512]{1,0:T(8,128)(2,1)} %collective-permute-done.32.refs_3_), channel_id=1, source_target_pairs={{0,8},{8,0},{1,9},{9,1},{2,10},{10,2},{3,11},{11,3},{4,12},{12,4},... | collective-permute-start | bytes 786440 | tf_op jit(solution)/shard_map/ppermute | solution.py:29
  139.5 6.9 %collective-permute-start.42 = (bf16[256,512]{1,0:T(8,128)(2,1)}, bf16[256,512]{1,0:T(8,128)(2,1)}, u32[]{:S(2)}, u32[]{:S(2)}) collective-permute-start(bf16[256,512]{1,0:T(8,128)(2,1)} %collective-permute-done.38.refs_9_), channel_id=1, source_target_pairs={{0,8},{8,0},{1,9},{9,1},{2,10},{10,2},{3,11},{11,3},{4,12},{12,4},... | collective-permute-start | bytes 786440 | tf_op jit(solution)/shard_map/ppermute | solution.py:29
  157.8 9.8 %collective-permute-start.45 = (bf16[32,4608]{1,0:T(8,128)(2,1)S(1)}, bf16[32,4608]{1,0:T(8,128)(2,1)S(1)}, u32[]{:S(2)}, u32[]{:S(2)}) collective-permute-start(bf16[32,4608]{1,0:T(8,128)(2,1)S(1)} %get-tuple-element.38), channel_id=1, source_target_pairs={{0,2},{2,4},{4,6},{6,0},{1,3},{3,5},{5,7},{7,1},{8,10},{10,12},{12... | collective-permute-start | bytes 884744 | tf_op jit(solution)/shard_map/ppermute | solution.py:29
  158.6 28.3 %collective-permute-start.46 = (bf16[32,4608]{1,0:T(8,128)(2,1)S(1)}, bf16[32,4608]{1,0:T(8,128)(2,1)S(1)}, u32[]{:S(2)}, u32[]{:S(2)}) collective-permute-start(bf16[32,4608]{1,0:T(8,128)(2,1)S(1)} %get-tuple-element.39), channel_id=1, source_target_pairs={{0,4},{2,6},{4,0},{6,2},{1,5},{3,7},{5,1},{7,3},{8,12},{10,14},{12... | collective-permute-start | bytes 884744 | tf_op jit(solution)/shard_map/ppermute | solution.py:29
  160.8 26.1 %collective-permute-start.47 = (bf16[32,4608]{1,0:T(8,128)(2,1)S(1)}, bf16[32,4608]{1,0:T(8,128)(2,1)S(1)}, u32[]{:S(2)}, u32[]{:S(2)}) collective-permute-start(bf16[32,4608]{1,0:T(8,128)(2,1)S(1)} %get-tuple-element.40), channel_id=1, source_target_pairs={{0,6},{2,0},{4,2},{6,4},{1,7},{3,1},{5,3},{7,5},{8,14},{10,8},{12,... | collective-permute-start | bytes 884744 | tf_op jit(solution)/shard_map/ppermute | solution.py:29
  161.8 25.1 %collective-permute-start.48 = (bf16[32,4608]{1,0:T(8,128)(2,1)S(1)}, bf16[32,4608]{1,0:T(8,128)(2,1)S(1)}, u32[]{:S(2)}, u32[]{:S(2)}) collective-permute-start(bf16[32,4608]{1,0:T(8,128)(2,1)S(1)} %get-tuple-element.41), channel_id=1, source_target_pairs={{0,1},{1,0},{2,3},{3,2},{4,5},{5,4},{6,7},{7,6},{8,9},{9,8},{10,11... | collective-permute-start | bytes 884744 | tf_op jit(solution)/shard_map/ppermute | solution.py:29
  162.8 24.1 %collective-permute-start.49 = (bf16[32,4608]{1,0:T(8,128)(2,1)S(1)}, bf16[32,4608]{1,0:T(8,128)(2,1)S(1)}, u32[]{:S(2)}, u32[]{:S(2)}) collective-permute-start(bf16[32,4608]{1,0:T(8,128)(2,1)S(1)} %get-tuple-element.42), channel_id=1, source_target_pairs={{0,3},{1,2},{2,5},{3,4},{4,7},{5,6},{6,1},{7,0},{8,11},{9,10},{10,... | collective-permute-start | bytes 884744 | tf_op jit(solution)/shard_map/ppermute | solution.py:485
  167.7 19.3 %collective-permute-start.50 = (bf16[32,4608]{1,0:T(8,128)(2,1)S(1)}, bf16[32,4608]{1,0:T(8,128)(2,1)S(1)}, u32[]{:S(2)}, u32[]{:S(2)}) collective-permute-start(bf16[32,4608]{1,0:T(8,128)(2,1)S(1)} %get-tuple-element.43), channel_id=1, source_target_pairs={{0,5},{1,4},{2,7},{3,6},{4,1},{5,0},{6,3},{7,2},{8,13},{9,12},{10,... | collective-permute-start | bytes 884744 | tf_op jit(solution)/shard_map/ppermute | solution.py:485
  186.9 10.1 %collective-permute-start.51 = (bf16[32,4608]{1,0:T(8,128)(2,1)S(1)}, bf16[32,4608]{1,0:T(8,128)(2,1)S(1)}, u32[]{:S(2)}, u32[]{:S(2)}) collective-permute-start(bf16[32,4608]{1,0:T(8,128)(2,1)S(1)} %get-tuple-element.44), channel_id=1, source_target_pairs={{0,7},{1,6},{2,1},{3,0},{4,3},{5,2},{6,5},{7,4},{8,15},{9,14},{10,... | collective-permute-start | bytes 884744 | tf_op jit(solution)/shard_map/ppermute | solution.py:485
  198.9 8.0 %collective-permute-start.52 = (bf16[32,4608]{1,0:T(8,128)(2,1)S(1)}, bf16[32,4608]{1,0:T(8,128)(2,1)S(1)}, u32[]{:S(2)}, u32[]{:S(2)}) collective-permute-start(bf16[32,4608]{1,0:T(8,128)(2,1)S(1)} %finish.1.refs_0_), channel_id=1, source_target_pairs={{0,8},{8,0},{1,9},{9,1},{2,10},{10,2},{3,11},{11,3},{4,12},{12,4},... | collective-permute-start | bytes 884744 | tf_op jit(solution)/shard_map/ppermute | solution.py:29
  209.3 9.0 %collective-permute-start.56 = (bf16[16,4608]{1,0:T(8,128)(2,1)S(1)}, bf16[16,4608]{1,0:T(8,128)(2,1)S(1)}, u32[]{:S(2)}, u32[]{:S(2)}) collective-permute-start(bf16[16,4608]{1,0:T(8,128)(2,1)S(1)} %get-tuple-element.47), channel_id=1, source_target_pairs={{0,64},{32,96},{64,0},{96,32},{1,65},{33,97},{65,1},{97,33},{2,66}... | collective-permute-start | bytes 442376 | tf_op jit(solution)/shard_map/ppermute | solution.py:29
  211.6 7.3 %collective-permute-start.57 = (bf16[16,4608]{1,0:T(8,128)(2,1)S(1)}, bf16[16,4608]{1,0:T(8,128)(2,1)S(1)}, u32[]{:S(2)}, u32[]{:S(2)}) collective-permute-start(bf16[16,4608]{1,0:T(8,128)(2,1)S(1)} %get-tuple-element.48), channel_id=1, source_target_pairs={{0,96},{32,0},{64,32},{96,64},{1,97},{33,1},{65,33},{97,65},{2,98}... | collective-permute-start | bytes 442376 | tf_op jit(solution)/shard_map/ppermute | solution.py:29
  219.7 8.0 %collective-permute-start.59 = (bf16[16,4608]{1,0:T(8,128)(2,1)S(1)}, bf16[16,4608]{1,0:T(8,128)(2,1)S(1)}, u32[]{:S(2)}, u32[]{:S(2)}) collective-permute-start(bf16[16,4608]{1,0:T(8,128)(2,1)S(1)} %get-tuple-element.51), channel_id=1, source_target_pairs={{0,4},{2,6},{4,0},{6,2},{1,5},{3,7},{5,1},{7,3},{8,12},{10,14},{12... | collective-permute-start | bytes 442376 | tf_op jit(solution)/shard_map/ppermute | solution.py:29
  (40 other events, 374.2 us)
Sparse Core Ops, SparseCore 0:
  9.0 85.8 all-gather.1

commit v3 on v2

--- a/solution.py
+++ b/solution.py
@@ -86,8 +86,7 @@
     fetch([(query, joined.at[:, :half]), (out_t, joined.at[:, half:])], sems)
 
 
-def hold_kernel(key, value, after, held, sems):
-    del after
+def hold_kernel(key, value, held, sems):
     jobs = []
     for n, source in enumerate((key, value, key, value)):
         first = n // 2 * HEAD
@@ -384,21 +383,21 @@
     )
     joined_full = lax.all_gather(joined, SEQ, axis=0, tiled=True)
 
+    (held,) = bring(hold_kernel, (), (w_key, w_value), [(w_key.shape[0], 4 * HEAD)], 4, pltpu.VMEM)
+    pair = shift(held, "yl", 1)
+
     old = far_off((old_blocks, order))
     near = bring(leave_kernel, (flat, *old), (x_old.T,), [(width, BLOCK)] * 4, 4, pltpu.VMEM)
     near = near[:1] + [shift(near[d], "x", d) for d in range(1, 4)]
     far = [shift(part, "c", 1) for part in near]
     mine, cross = call(sort_kernel, old, near + far, [(width, count)] * 2)
-    (held,) = pl.pallas_call(
-        hold_kernel,
-        in_specs=[AWAY, AWAY, VMEM],
-        out_specs=[VMEM],
-        out_shape=[pltpu.VMEM((w_key.shape[0], 4 * HEAD), BF16)],
-        scratch_shapes=[pltpu.SemaphoreType.DMA((4,))],
-        compiler_params=grant(8),
-        name="hold",
-    )(*far_off((w_key, w_value)), *near_by((mine,)))
-    spread_weights = everywhere(held)
+    same = [held] + [shift(held, "x", d) for d in range(1, 4)]
+    other = [pair] + [shift(pair, "x", d) for d in range(1, 4)]
+    spread_weights = [
+        w
+        for parts in (same, other)
+        for w in parts + [shift(s, "c", 1) for s in parts]
+    ]
 
     cross = shift(cross, "yl", 1)
     (rows,) = call(settle_kernel, old, (mine, cross), [(width, count)])

time: 239 us -> 251 us (1.050)
  waiting for transfers between devices: 99.7 us -> 123 us
  local copies, waits for them, and re-layouts: 14 us -> 7.76 us
  starting transfers between devices: 79.8 us -> 76.5 us
    ppermute x58, waiting for transfers between devices: 89.7 us -> 109 us  [shift(): return lax.ppermute(value, axis, [(i, (i + by) % n) for i in range(n)])]
    unnamed x53 -> x33, local copies, waits for them, and re-layouts: 13.9 us -> 7.73 us
    ppermute x3, waiting for transfers between devices: 10 us -> 13.6 us  [per_device(): lax.ppermute(part, TP, [(2 * i + j, 2 * ((i + dz) % 4) + (j ^ dy)) for i,...]
  transfers between devices with their start and end apart: 62 -> 62, of which waited for: 26 -> 23; matrix products, arithmetic and copies ran while one was open for 0% -> 0% of each run, Pallas kernels for 5% -> 5%
where the time goes in v3:
time: 251 us; the launch traced here: 250 us
  waiting for transfers between devices  123 us (49%)
  starting transfers between devices  76.5 us (30%)
  Pallas kernels  28.3 us (11%)
  between operations  13.8 us (5%)
  local copies, waits for them, and re-layouts  7.76 us (3%)
    ppermute x58, waiting for transfers between devices, shift(): return lax.ppermute(value, axis, [(i, (i + by) % n) for i in range(n)])  109 us
    ppermute x58, starting transfers between devices, shift(): return lax.ppermute(value, axis, [(i, (i + by) % n) for i in range(n)])  74.2 us
    ppermute x3, waiting for transfers between devices, per_device(): lax.ppermute(part, TP, [(2 * i + j, 2 * ((i + dz) % 4) + (j ^ dy)) for i,...  13.6 us
    unnamed x33, local copies, waits for them, and re-layouts  7.73 us
    pallas_call x1, Pallas kernels, per_device(): pl.pallas_call(attention_kernel, in_specs=[SMEM] + [VMEM] * 17, out_specs...  7 us
    pallas_call x6, Pallas kernels, call(): pl.pallas_call(kernel, in_specs=[SMEM] * (1 + len(tables)) + [VMEM] * len...  5.71 us
  transfers between devices with their start and end apart: 62, of which 23 were waited for; matrix products, arithmetic and copies ran while one was open for 0% of the time, Pallas kernels for 5%

profile of v3, /device:TPU:1, one launch (start us, length us, event | category | flops | bytes accessed | tf_op | source)
XLA Modules:
  0.0 250.1 jit_solution(3812701308323220172)
XLA Ops:
  6.5 1.9 shard_map.103
  8.5 1.9 shard_map.100
  10.4 2.1 collective-permute-start
  12.5 2.5 collective-permute-start.1
  16.1 1.5 collective-permute-start.3
  19.6 1.7 collective-permute-start.22
  21.8 2.9 %collective-permute-start.16 = (bf16[288,512]{1,0:T(8,128)(2,1)S(1)}, bf16[288,512]{1,0:T(8,128)(2,1)S(1)}, u32[]{:S(2)}, u32[]{:S(2)}) collective-permute-start(bf16[288,512]{1,0:T(8,128)(2,1)S(1)} %shard_map.105.refs_0_), channel_id=1, source_target_pairs={{0,64},{32,96},{64,0},{96,32},{1,65},{33,97},{65,1},{97,33},{2,66}... | collective-permute-start | bytes 884744 | tf_op jit(solution)/shard_map/ppermute | solution.py:29
  30.0 4.2 %collective-permute-done.22.refs_8_ = bf16[288,512]{1,0:T(8,128)(2,1)S(1)} collective-permute-done((bf16[288,512]{1,0:T(8,128)(2,1)S(1)}, bf16[288,512]{1,0:T(8,128)(2,1)S(1)}, u32[]{:S(2)}, u32[]{:S(2)}) %collective-permute-start.22) | collective-permute-done | bytes 294944 | tf_op jit(solution)/shard_map/ppermute | solution.py:29
  34.2 2.3 collective-permute-start.7
  36.6 14.2 %collective-permute-done.16.refs_2_ = bf16[288,512]{1,0:T(8,128)(2,1)S(1)} collective-permute-done((bf16[288,512]{1,0:T(8,128)(2,1)S(1)}, bf16[288,512]{1,0:T(8,128)(2,1)S(1)}, u32[]{:S(2)}, u32[]{:S(2)}) %collective-permute-start.16) | collective-permute-done | bytes 294944 | tf_op jit(solution)/shard_map/ppermute | solution.py:29
  51.0 2.8 %collective-permute-start.26 = (bf16[288,512]{1,0:T(8,128)(2,1)S(1)}, bf16[288,512]{1,0:T(8,128)(2,1)S(1)}, u32[]{:S(2)}, u32[]{:S(2)}) collective-permute-start(bf16[288,512]{1,0:T(8,128)(2,1)S(1)} %collective-permute-done.22.refs_8_), channel_id=1, source_target_pairs={{0,8},{8,0},{1,9},{9,1},{2,10},{10,2},{3,11},{11,3},{4,12},{12,4},... | collective-permute-start | bytes 884744 | tf_op jit(solution)/shard_map/ppermute | solution.py:29
  54.5 5.0 %collective-permute-done.23.refs_9_ = bf16[288,512]{1,0:T(8,128)(2,1)S(1)} collective-permute-done((bf16[288,512]{1,0:T(8,128)(2,1)S(1)}, bf16[288,512]{1,0:T(8,128)(2,1)S(1)}, u32[]{:S(2)}, u32[]{:S(2)}) %collective-permute-start.23) | collective-permute-done | bytes 294944 | tf_op jit(solution)/shard_map/ppermute | solution.py:29
  59.5 2.6 %collective-permute-start.20 = (bf16[288,512]{1,0:T(8,128)(2,1)S(1)}, bf16[288,512]{1,0:T(8,128)(2,1)}, u32[]{:S(2)}, u32[]{:S(2)}) collective-permute-start(bf16[288,512]{1,0:T(8,128)(2,1)S(1)} %collective-permute-done.16.refs_2_), channel_id=1, source_target_pairs={{0,8},{8,0},{1,9},{9,1},{2,10},{10,2},{3,11},{11,3},{4,12},{12,4},... | collective-permute-start | bytes 884744 | tf_op jit(solution)/shard_map/ppermute | solution.py:29
  62.1 13.9 %collective-permute-done.24.refs_10_ = bf16[288,512]{1,0:T(8,128)(2,1)S(1)} collective-permute-done((bf16[288,512]{1,0:T(8,128)(2,1)S(1)}, bf16[288,512]{1,0:T(8,128)(2,1)S(1)}, u32[]{:S(2)}, u32[]{:S(2)}) %collective-permute-start.24) | collective-permute-done | bytes 294944 | tf_op jit(solution)/shard_map/ppermute | solution.py:29
  80.1 2.7 %collective-permute-start.11 = (bf16[576,256]{1,0:T(8,128)(2,1)S(1)}, bf16[576,256]{1,0:T(8,128)(2,1)S(1)}, u32[]{:S(2)}, u32[]{:S(2)}) collective-permute-start(bf16[576,256]{1,0:T(8,128)(2,1)S(1)} %shard_map.102.refs_0_), channel_id=1, source_target_pairs={{0,1},{1,0},{2,3},{3,2},{4,5},{5,4},{6,7},{7,6},{8,9},{9,8},{10,11... | collective-permute-start | bytes 884744 | tf_op jit(solution)/shard_map/ppermute | solution.py:29
  82.8 3.9 %collective-permute-start.10 = (bf16[576,256]{1,0:T(8,128)(2,1)S(1)}, bf16[576,256]{1,0:T(8,128)(2,1)S(1)}, u32[]{:S(2)}, u32[]{:S(2)}) collective-permute-start(bf16[576,256]{1,0:T(8,128)(2,1)S(1)} %shard_map.102.refs_0_), channel_id=1, source_target_pairs={{0,6},{2,0},{4,2},{6,4},{1,7},{3,1},{5,3},{7,5},{8,14},{10,8},{12,... | collective-permute-start | bytes 884744 | tf_op jit(solution)/shard_map/ppermute | solution.py:29
  87.8 9.0 %collective-permute-done.11.refs_4_ = bf16[576,256]{1,0:T(8,128)(2,1)S(1)} collective-permute-done((bf16[576,256]{1,0:T(8,128)(2,1)S(1)}, bf16[576,256]{1,0:T(8,128)(2,1)S(1)}, u32[]{:S(2)}, u32[]{:S(2)}) %collective-permute-start.11) | collective-permute-done | bytes 294944 | tf_op jit(solution)/shard_map/ppermute | solution.py:29
  96.8 1.6 collective-permute-start.8
  98.4 3.6 %collective-permute-start.9 = (bf16[576,256]{1,0:T(8,128)(2,1)S(1)}, bf16[576,256]{1,0:T(8,128)(2,1)S(1)}, u32[]{:S(2)}, u32[]{:S(2)}) collective-permute-start(bf16[576,256]{1,0:T(8,128)(2,1)S(1)} %shard_map.102.refs_0_), channel_id=1, source_target_pairs={{0,4},{2,6},{4,0},{6,2},{1,5},{3,7},{5,1},{7,3},{8,12},{10,14},{12... | collective-permute-start | bytes 884744 | tf_op jit(solution)/shard_map/ppermute | solution.py:29
  102.0 1.7 collective-permute-start.13
  105.7 1.4 shard_map.106.weight
  107.5 7.3 %collective-permute-done.9.refs_2_ = bf16[576,256]{1,0:T(8,128)(2,1)S(1)} collective-permute-done((bf16[576,256]{1,0:T(8,128)(2,1)S(1)}, bf16[576,256]{1,0:T(8,128)(2,1)S(1)}, u32[]{:S(2)}, u32[]{:S(2)}) %collective-permute-start.9) | collective-permute-done | bytes 294944 | tf_op jit(solution)/shard_map/ppermute | solution.py:29
  114.8 5.4 %collective-permute-done.12.refs_5_ = bf16[576,256]{1,0:T(8,128)(2,1)S(1)} collective-permute-done((bf16[576,256]{1,0:T(8,128)(2,1)S(1)}, bf16[576,256]{1,0:T(8,128)(2,1)S(1)}, u32[]{:S(2)}, u32[]{:S(2)}) %collective-permute-start.12) | collective-permute-done | bytes 294944 | tf_op jit(solution)/shard_map/ppermute | solution.py:29
  120.2 7.3 %collective-permute-done.13.refs_6_ = bf16[576,256]{1,0:T(8,128)(2,1)S(1)} collective-permute-done((bf16[576,256]{1,0:T(8,128)(2,1)S(1)}, bf16[576,256]{1,0:T(8,128)(2,1)S(1)}, u32[]{:S(2)}, u32[]{:S(2)}) %collective-permute-start.13) | collective-permute-done | bytes 294944 | tf_op jit(solution)/shard_map/ppermute | solution.py:29
  128.6 1.4 key_value.1.refs_0_
  130.4 2.7 %collective-permute-start.32 = (bf16[256,512]{1,0:T(8,128)(2,1)S(1)}, bf16[256,512]{1,0:T(8,128)(2,1)}, u32[]{:S(2)}, u32[]{:S(2)}) collective-permute-start(bf16[256,512]{1,0:T(8,128)(2,1)S(1)} %key_value.1.refs_0_), channel_id=1, source_target_pairs={{0,96},{32,0},{64,32},{96,64},{1,97},{33,1},{65,33},{97,65},{2,98}... | collective-permute-start | bytes 786440 | tf_op jit(solution)/shard_map/ppermute | solution.py:29
  133.1 2.3 collective-permute-start.33
  136.5 1.6 collective-permute-done.31.refs_2_
  139.3 5.9 %collective-permute-done.30.refs_1_ = bf16[256,512]{1,0:T(8,128)(2,1)S(1)} collective-permute-done((bf16[256,512]{1,0:T(8,128)(2,1)S(1)}, bf16[256,512]{1,0:T(8,128)(2,1)S(1)}, u32[]{:S(2)}, u32[]{:S(2)}) %collective-permute-start.30) | collective-permute-done | bytes 262176 | tf_op jit(solution)/shard_map/ppermute | solution.py:29
  145.2 3.8 %collective-permute-start.34 = (bf16[256,512]{1,0:T(8,128)(2,1)S(1)}, bf16[256,512]{1,0:T(8,128)(2,1)S(1)}, u32[]{:S(2)}, u32[]{:S(2)}) collective-permute-start(bf16[256,512]{1,0:T(8,128)(2,1)S(1)} %collective-permute-done.30.refs_1_), channel_id=1, source_target_pairs={{0,8},{8,0},{1,9},{9,1},{2,10},{10,2},{3,11},{11,3},{4,12},{12,4},... | collective-permute-start | bytes 786440 | tf_op jit(solution)/shard_map/ppermute | solution.py:29
  152.0 2.0 collective-permute-start.42
  155.9 3.5 %shard_map.104.query = bf16[256,512]{1,0:T(8,128)(2,1)S(1)} custom-call(bf16[256,4608]{1,0:T(8,128)(2,1)S(1)} %get-tuple-element.36.normed, bf16[4608,1024]{1,0:T(8,128)(2,1)} %all-gather.2.cloned.1.call-done.weight, f32[256,128]{1,0:T(8,128)S(1)} %pad_maximum_fusion.cos, f32[256,128]{1,0:T(8,128)S(1)} %pad_maximum_fusion.1.sin), custom_call_target="tpu_custom_call" | custom-call | tf_op jit(solution)/shard_map/pallas_call | solution.py:432
  159.5 7.0 %attention.1.context = bf16[256,512]{1,0:T(8,128)(2,1)S(1)} custom-call(s32[1]{0:T(128)} %bitcast.flat, bf16[256,512]{1,0:T(8,128)(2,1)S(1)} %shard_map.104.query, bf16[256,512]{1,0:T(8,128)(2,1)S(1)} %key_value.1.refs_0_, bf16[256,512]{1,0:T(8,128)(2,1)S(1)} %copy-done.7, bf16[256,512]{1,0:T(8,128)(2,1)S(1)} %copy-done.5, ...), custom_call_target="tpu_custom_call" | custom-call | tf_op jit(solution)/shard_map/attention/pallas_call | solution.py:454
  166.6 4.3 %project.1 = (bf16[32,4608]{1,0:T(8,128)(2,1)S(1)}, bf16[32,4608]{1,0:T(8,128)(2,1)S(1)}, bf16[32,4608]{1,0:T(8,128)(2,1)S(1)}, bf16[32,4608]{1,0:T(8,128)(2,1)S...) custom-call(s32[1]{0:T(128)} %bitcast.flat, ...), custom_call_target="tpu_custom_call" | custom-call | tf_op jit(solution)/shard_map/project/pallas_call | solution.py:465
  171.0 2.6 %collective-permute-start.47 = (bf16[32,4608]{1,0:T(8,128)(2,1)S(1)}, bf16[32,4608]{1,0:T(8,128)(2,1)S(1)}, u32[]{:S(2)}, u32[]{:S(2)}) collective-permute-start(bf16[32,4608]{1,0:T(8,128)(2,1)S(1)} %get-tuple-element.40), channel_id=1, source_target_pairs={{0,6},{2,0},{4,2},{6,4},{1,7},{3,1},{5,3},{7,5},{8,14},{10,8},{12,... | collective-permute-start | bytes 884744 | tf_op jit(solution)/shard_map/ppermute | solution.py:29
  173.6 2.1 collective-permute-start.48
  176.9 16.5 %collective-permute-done.45.refs_1_ = bf16[32,4608]{1,0:T(8,128)(2,1)S(1)} collective-permute-done((bf16[32,4608]{1,0:T(8,128)(2,1)S(1)}, bf16[32,4608]{1,0:T(8,128)(2,1)S(1)}, u32[]{:S(2)}, u32[]{:S(2)}) %collective-permute-start.45) | collective-permute-done | bytes 294944 | tf_op jit(solution)/shard_map/ppermute | solution.py:29
  194.5 10.4 %collective-permute-done.50.refs_6_ = bf16[32,4608]{1,0:T(8,128)(2,1)S(1)} collective-permute-done((bf16[32,4608]{1,0:T(8,128)(2,1)S(1)}, bf16[32,4608]{1,0:T(8,128)(2,1)S(1)}, u32[]{:S(2)}, u32[]{:S(2)}) %collective-permute-start.50) | collective-permute-done | bytes 294944 | tf_op jit(solution)/shard_map/ppermute | solution.py:484
  204.9 3.2 %collective-permute-done.51.refs_7_ = bf16[32,4608]{1,0:T(8,128)(2,1)S(1)} collective-permute-done((bf16[32,4608]{1,0:T(8,128)(2,1)S(1)}, bf16[32,4608]{1,0:T(8,128)(2,1)S(1)}, u32[]{:S(2)}, u32[]{:S(2)}) %collective-permute-start.51) | collective-permute-done | bytes 294944 | tf_op jit(solution)/shard_map/ppermute | solution.py:484
  210.0 2.1 collective-permute-start.52
  212.1 3.5 %collective-permute-done.53.refs_2_ = bf16[32,4608]{1,0:T(8,128)(2,1)S(1)} collective-permute-done((bf16[32,4608]{1,0:T(8,128)(2,1)S(1)}, bf16[32,4608]{1,0:T(8,128)(2,1)S(1)}, u32[]{:S(2)}, u32[]{:S(2)}) %collective-permute-start.53) | collective-permute-done | bytes 294944 | tf_op jit(solution)/shard_map/ppermute | solution.py:29
  215.6 2.6 %collective-permute-start.54 = (bf16[32,4608]{1,0:T(8,128)(2,1)S(1)}, bf16[32,4608]{1,0:T(8,128)(2,1)S(1)}, u32[]{:S(2)}, u32[]{:S(2)}) collective-permute-start(bf16[32,4608]{1,0:T(8,128)(2,1)S(1)} %collective-permute-done.53.refs_2_), channel_id=1, source_target_pairs={{0,8},{8,0},{1,9},{9,1},{2,10},{10,2},{3,11},{11,3},{4,12},{12,4},... | collective-permute-start | bytes 884744 | tf_op jit(solution)/shard_map/ppermute | solution.py:29
  220.3 3.6 %collective-permute-start.56 = (bf16[16,4608]{1,0:T(8,128)(2,1)S(1)}, bf16[16,4608]{1,0:T(8,128)(2,1)S(1)}, u32[]{:S(2)}, u32[]{:S(2)}) collective-permute-start(bf16[16,4608]{1,0:T(8,128)(2,1)S(1)} %get-tuple-element.47), channel_id=1, source_target_pairs={{0,64},{32,96},{64,0},{96,32},{1,65},{33,97},{65,1},{97,33},{2,66}... | collective-permute-start | bytes 442376 | tf_op jit(solution)/shard_map/ppermute | solution.py:29
  223.9 2.6 %collective-permute-done.55.refs_1_ = bf16[16,4608]{1,0:T(8,128)(2,1)S(1)} collective-permute-done((bf16[16,4608]{1,0:T(8,128)(2,1)S(1)}, bf16[16,4608]{1,0:T(8,128)(2,1)S(1)}, u32[]{:S(2)}, u32[]{:S(2)}) %collective-permute-start.55) | collective-permute-done | bytes 147488 | tf_op jit(solution)/shard_map/ppermute | solution.py:29
  226.6 4.1 %collective-permute-done.56.refs_2_ = bf16[16,4608]{1,0:T(8,128)(2,1)S(1)} collective-permute-done((bf16[16,4608]{1,0:T(8,128)(2,1)S(1)}, bf16[16,4608]{1,0:T(8,128)(2,1)S(1)}, u32[]{:S(2)}, u32[]{:S(2)}) %collective-permute-start.56) | collective-permute-done | bytes 147488 | tf_op jit(solution)/shard_map/ppermute | solution.py:29
  231.4 2.9 %collective-permute-start.58 = (bf16[16,4608]{1,0:T(8,128)(2,1)S(1)}, bf16[16,4608]{1,0:T(8,128)(2,1)S(1)}, u32[]{:S(2)}, u32[]{:S(2)}) collective-permute-start(bf16[16,4608]{1,0:T(8,128)(2,1)S(1)} %get-tuple-element.50), channel_id=1, source_target_pairs={{0,2},{2,4},{4,6},{6,0},{1,3},{3,5},{5,7},{7,1},{8,10},{10,12},{12... | collective-permute-start | bytes 442376 | tf_op jit(solution)/shard_map/ppermute | solution.py:29
  235.4 1.4 collective-permute-start.60
  236.8 4.9 %collective-permute-done.59.refs_2_ = bf16[16,4608]{1,0:T(8,128)(2,1)S(1)} collective-permute-done((bf16[16,4608]{1,0:T(8,128)(2,1)S(1)}, bf16[16,4608]{1,0:T(8,128)(2,1)S(1)}, u32[]{:S(2)}, u32[]{:S(2)}) %collective-permute-start.59) | collective-permute-done | bytes 147488 | tf_op jit(solution)/shard_map/ppermute | solution.py:29
  (133 shorter events, 36.2 us)
Async XLA Ops:
  6.5 149.4 %all-gather.2.cloned.1.call-start = ((), (), s32[]{:S(2)}) async-start(), calls=%async_computation | async-start | bytes 10027008 | tf_op jit(solution)/shard_map/all_gather | solution.py:384
  10.4 7.2 %collective-permute-start = (bf16[576,128]{1,0:T(8,128)(2,1)S(1)}, bf16[576,128]{1,0:T(8,128)(2,1)S(1)}, u32[]{:S(2)}, u32[]{:S(2)}) collective-permute-start(bf16[576,128]{1,0:T(8,128)(2,1)S(1)} %get-tuple-element.30), channel_id=1, source_target_pairs={{0,32},{32,64},{64,96},{96,0},{1,33},{33,65},{65,97},{97,1},{2,34}... | collective-permute-start | bytes 442376 | tf_op jit(solution)/shard_map/ppermute | solution.py:29
  12.5 8.9 %collective-permute-start.1 = (bf16[576,128]{1,0:T(8,128)(2,1)S(1)}, bf16[576,128]{1,0:T(8,128)(2,1)S(1)}, u32[]{:S(2)}, u32[]{:S(2)}) collective-permute-start(bf16[576,128]{1,0:T(8,128)(2,1)S(1)} %get-tuple-element.31), channel_id=1, source_target_pairs={{0,64},{32,96},{64,0},{96,32},{1,65},{33,97},{65,1},{97,33},{2,66}... | collective-permute-start | bytes 442376 | tf_op jit(solution)/shard_map/ppermute | solution.py:29
  16.1 8.7 %collective-permute-start.3 = (bf16[576,128]{1,0:T(8,128)(2,1)S(1)}, bf16[576,128]{1,0:T(8,128)(2,1)S(1)}, u32[]{:S(2)}, u32[]{:S(2)}) collective-permute-start(bf16[576,128]{1,0:T(8,128)(2,1)S(1)} %get-tuple-element.29.refs_0_), channel_id=1, source_target_pairs={{0,8},{8,0},{1,9},{9,1},{2,10},{10,2},{3,11},{11,3},{4,12},{12,4},... | collective-permute-start | bytes 442376 | tf_op jit(solution)/shard_map/ppermute | solution.py:29
  17.6 8.0 %collective-permute-start.4 = (bf16[576,128]{1,0:T(8,128)(2,1)S(1)}, bf16[576,128]{1,0:T(8,128)(2,1)S(1)}, u32[]{:S(2)}, u32[]{:S(2)}) collective-permute-start(bf16[576,128]{1,0:T(8,128)(2,1)S(1)} %collective-permute-done.refs_1_), channel_id=1, source_target_pairs={{0,8},{8,0},{1,9},{9,1},{2,10},{10,2},{3,11},{11,3},{4,12},{12,4},... | collective-permute-start | bytes 442376 | tf_op jit(solution)/shard_map/ppermute | solution.py:29
  19.6 14.6 %collective-permute-start.22 = (bf16[288,512]{1,0:T(8,128)(2,1)S(1)}, bf16[288,512]{1,0:T(8,128)(2,1)S(1)}, u32[]{:S(2)}, u32[]{:S(2)}) collective-permute-start(bf16[288,512]{1,0:T(8,128)(2,1)S(1)} %shard_map.105.refs_0_), channel_id=1, source_target_pairs={{0,16},{16,0},{1,17},{17,1},{2,18},{18,2},{3,19},{19,3},{4,20},{20... | collective-permute-start | bytes 884744 | tf_op jit(solution)/shard_map/ppermute | solution.py:29
  21.3 15.1 %collective-permute-start.15 = (bf16[288,512]{1,0:T(8,128)(2,1)S(1)}, bf16[288,512]{1,0:T(8,128)(2,1)S(1)}, u32[]{:S(2)}, u32[]{:S(2)}) collective-permute-start(bf16[288,512]{1,0:T(8,128)(2,1)S(1)} %shard_map.105.refs_0_), channel_id=1, source_target_pairs={{0,32},{32,64},{64,96},{96,0},{1,33},{33,65},{65,97},{97,1},{2,34}... | collective-permute-start | bytes 884744 | tf_op jit(solution)/shard_map/ppermute | solution.py:29
  21.8 28.9 %collective-permute-start.16 = (bf16[288,512]{1,0:T(8,128)(2,1)S(1)}, bf16[288,512]{1,0:T(8,128)(2,1)S(1)}, u32[]{:S(2)}, u32[]{:S(2)}) collective-permute-start(bf16[288,512]{1,0:T(8,128)(2,1)S(1)} %shard_map.105.refs_0_), channel_id=1, source_target_pairs={{0,64},{32,96},{64,0},{96,32},{1,65},{33,97},{65,1},{97,33},{2,66}... | collective-permute-start | bytes 884744 | tf_op jit(solution)/shard_map/ppermute | solution.py:29
  26.6 24.2 %collective-permute-start.17 = (bf16[288,512]{1,0:T(8,128)(2,1)S(1)}, bf16[288,512]{1,0:T(8,128)(2,1)S(1)}, u32[]{:S(2)}, u32[]{:S(2)}) collective-permute-start(bf16[288,512]{1,0:T(8,128)(2,1)S(1)} %shard_map.105.refs_0_), channel_id=1, source_target_pairs={{0,96},{32,0},{64,32},{96,64},{1,97},{33,1},{65,33},{97,65},{2,98}... | collective-permute-start | bytes 884744 | tf_op jit(solution)/shard_map/ppermute | solution.py:29
  27.5 23.5 %collective-permute-start.18 = (bf16[288,512]{1,0:T(8,128)(2,1)S(1)}, bf16[288,512]{1,0:T(8,128)(2,1)S(1)}, u32[]{:S(2)}, u32[]{:S(2)}) collective-permute-start(bf16[288,512]{1,0:T(8,128)(2,1)S(1)} %shard_map.105.refs_0_), channel_id=1, source_target_pairs={{0,8},{8,0},{1,9},{9,1},{2,10},{10,2},{3,11},{11,3},{4,12},{12,4},... | collective-permute-start | bytes 884744 | tf_op jit(solution)/shard_map/ppermute | solution.py:29
  34.2 19.6 %collective-permute-start.7 = (bf16[576,256]{1,0:T(8,128)(2,1)S(1)}, bf16[576,256]{1,0:T(8,128)(2,1)S(1)}, u32[]{:S(2)}, u32[]{:S(2)}) collective-permute-start(bf16[576,256]{1,0:T(8,128)(2,1)S(1)} %get-tuple-element.34), channel_id=1, source_target_pairs={{0,16},{16,0},{1,17},{17,1},{2,18},{18,2},{3,19},{19,3},{4,20},{20... | collective-permute-start | bytes 884744 | tf_op jit(solution)/shard_map/ppermute | solution.py:29
  36.5 23.1 %collective-permute-start.23 = (bf16[288,512]{1,0:T(8,128)(2,1)S(1)}, bf16[288,512]{1,0:T(8,128)(2,1)S(1)}, u32[]{:S(2)}, u32[]{:S(2)}) collective-permute-start(bf16[288,512]{1,0:T(8,128)(2,1)S(1)} %collective-permute-done.22.refs_8_), channel_id=1, source_target_pairs={{0,32},{32,64},{64,96},{96,0},{1,33},{33,65},{65,97},{97,1},{2,34}... | collective-permute-start | bytes 884744 | tf_op jit(solution)/shard_map/ppermute | solution.py:29
  50.8 25.3 %collective-permute-start.24 = (bf16[288,512]{1,0:T(8,128)(2,1)S(1)}, bf16[288,512]{1,0:T(8,128)(2,1)S(1)}, u32[]{:S(2)}, u32[]{:S(2)}) collective-permute-start(bf16[288,512]{1,0:T(8,128)(2,1)S(1)} %collective-permute-done.22.refs_8_), channel_id=1, source_target_pairs={{0,64},{32,96},{64,0},{96,32},{1,65},{33,97},{65,1},{97,33},{2,66}... | collective-permute-start | bytes 884744 | tf_op jit(solution)/shard_map/ppermute | solution.py:29
  50.8 29.3 %collective-permute-start.25 = (bf16[288,512]{1,0:T(8,128)(2,1)S(1)}, bf16[288,512]{1,0:T(8,128)(2,1)S(1)}, u32[]{:S(2)}, u32[]{:S(2)}) collective-permute-start(bf16[288,512]{1,0:T(8,128)(2,1)S(1)} %collective-permute-done.22.refs_8_), channel_id=1, source_target_pairs={{0,96},{32,0},{64,32},{96,64},{1,97},{33,1},{65,33},{97,65},{2,98}... | collective-permute-start | bytes 884744 | tf_op jit(solution)/shard_map/ppermute | solution.py:29
  51.0 31.8 %collective-permute-start.26 = (bf16[288,512]{1,0:T(8,128)(2,1)S(1)}, bf16[288,512]{1,0:T(8,128)(2,1)S(1)}, u32[]{:S(2)}, u32[]{:S(2)}) collective-permute-start(bf16[288,512]{1,0:T(8,128)(2,1)S(1)} %collective-permute-done.22.refs_8_), channel_id=1, source_target_pairs={{0,8},{8,0},{1,9},{9,1},{2,10},{10,2},{3,11},{11,3},{4,12},{12,4},... | collective-permute-start | bytes 884744 | tf_op jit(solution)/shard_map/ppermute | solution.py:29
  54.5 32.2 %collective-permute-start.19 = (bf16[288,512]{1,0:T(8,128)(2,1)S(1)}, bf16[288,512]{1,0:T(8,128)(2,1)S(1)}, u32[]{:S(2)}, u32[]{:S(2)}) collective-permute-start(bf16[288,512]{1,0:T(8,128)(2,1)S(1)} %collective-permute-done.15.refs_1_), channel_id=1, source_target_pairs={{0,8},{8,0},{1,9},{9,1},{2,10},{10,2},{3,11},{11,3},{4,12},{12,4},... | collective-permute-start | bytes 884744 | tf_op jit(solution)/shard_map/ppermute | solution.py:29
  59.5 27.7 %collective-permute-start.20 = (bf16[288,512]{1,0:T(8,128)(2,1)S(1)}, bf16[288,512]{1,0:T(8,128)(2,1)}, u32[]{:S(2)}, u32[]{:S(2)}) collective-permute-start(bf16[288,512]{1,0:T(8,128)(2,1)S(1)} %collective-permute-done.16.refs_2_), channel_id=1, source_target_pairs={{0,8},{8,0},{1,9},{9,1},{2,10},{10,2},{3,11},{11,3},{4,12},{12,4},... | collective-permute-start | bytes 884744 | tf_op jit(solution)/shard_map/ppermute | solution.py:29
  76.0 11.3 %collective-permute-start.21 = (bf16[288,512]{1,0:T(8,128)(2,1)S(1)}, bf16[288,512]{1,0:T(8,128)(2,1)}, u32[]{:S(2)}, u32[]{:S(2)}) collective-permute-start(bf16[288,512]{1,0:T(8,128)(2,1)S(1)} %collective-permute-done.17.refs_3_), channel_id=1, source_target_pairs={{0,8},{8,0},{1,9},{9,1},{2,10},{10,2},{3,11},{11,3},{4,12},{12,4},... | collective-permute-start | bytes 884744 | tf_op jit(solution)/shard_map/ppermute | solution.py:29
  80.1 16.6 %collective-permute-start.11 = (bf16[576,256]{1,0:T(8,128)(2,1)S(1)}, bf16[576,256]{1,0:T(8,128)(2,1)S(1)}, u32[]{:S(2)}, u32[]{:S(2)}) collective-permute-start(bf16[576,256]{1,0:T(8,128)(2,1)S(1)} %shard_map.102.refs_0_), channel_id=1, source_target_pairs={{0,1},{1,0},{2,3},{3,2},{4,5},{5,4},{6,7},{7,6},{8,9},{9,8},{10,11... | collective-permute-start | bytes 884744 | tf_op jit(solution)/shard_map/ppermute | solution.py:29
  82.8 15.5 %collective-permute-start.10 = (bf16[576,256]{1,0:T(8,128)(2,1)S(1)}, bf16[576,256]{1,0:T(8,128)(2,1)S(1)}, u32[]{:S(2)}, u32[]{:S(2)}) collective-permute-start(bf16[576,256]{1,0:T(8,128)(2,1)S(1)} %shard_map.102.refs_0_), channel_id=1, source_target_pairs={{0,6},{2,0},{4,2},{6,4},{1,7},{3,1},{5,3},{7,5},{8,14},{10,8},{12,... | collective-permute-start | bytes 884744 | tf_op jit(solution)/shard_map/ppermute | solution.py:29
  86.7 15.3 %collective-permute-start.27 = (bf16[288,512]{1,0:T(8,128)(2,1)S(1)}, bf16[288,512]{1,0:T(8,128)(2,1)S(1)}, u32[]{:S(2)}, u32[]{:S(2)}) collective-permute-start(bf16[288,512]{1,0:T(8,128)(2,1)S(1)} %collective-permute-done.23.refs_9_), channel_id=1, source_target_pairs={{0,8},{8,0},{1,9},{9,1},{2,10},{10,2},{3,11},{11,3},{4,12},{12,4},... | collective-permute-start | bytes 884744 | tf_op jit(solution)/shard_map/ppermute | solution.py:29
  87.2 14.7 %collective-permute-start.28 = (bf16[288,512]{1,0:T(8,128)(2,1)S(1)}, bf16[288,512]{1,0:T(8,128)(2,1)S(1)}, u32[]{:S(2)}, u32[]{:S(2)}) collective-permute-start(bf16[288,512]{1,0:T(8,128)(2,1)S(1)} %collective-permute-done.24.refs_10_), channel_id=1, source_target_pairs={{0,8},{8,0},{1,9},{9,1},{2,10},{10,2},{3,11},{11,3},{4,12},{12,4},... | collective-permute-start | bytes 884744 | tf_op jit(solution)/shard_map/ppermute | solution.py:29
  87.3 16.4 %collective-permute-start.29 = (bf16[288,512]{1,0:T(8,128)(2,1)S(1)}, bf16[288,512]{1,0:T(8,128)(2,1)S(1)}, u32[]{:S(2)}, u32[]{:S(2)}) collective-permute-start(bf16[288,512]{1,0:T(8,128)(2,1)S(1)} %collective-permute-done.25.refs_11_), channel_id=1, source_target_pairs={{0,8},{8,0},{1,9},{9,1},{2,10},{10,2},{3,11},{11,3},{4,12},{12,4},... | collective-permute-start | bytes 884744 | tf_op jit(solution)/shard_map/ppermute | solution.py:29
  96.8 10.8 %collective-permute-start.8 = (bf16[576,256]{1,0:T(8,128)(2,1)S(1)}, bf16[576,256]{1,0:T(8,128)(2,1)S(1)}, u32[]{:S(2)}, u32[]{:S(2)}) collective-permute-start(bf16[576,256]{1,0:T(8,128)(2,1)S(1)} %shard_map.102.refs_0_), channel_id=1, source_target_pairs={{0,2},{2,4},{4,6},{6,0},{1,3},{3,5},{5,7},{7,1},{8,10},{10,12},{12... | collective-permute-start | bytes 884744 | tf_op jit(solution)/shard_map/ppermute | solution.py:29
  98.4 16.4 %collective-permute-start.9 = (bf16[576,256]{1,0:T(8,128)(2,1)S(1)}, bf16[576,256]{1,0:T(8,128)(2,1)S(1)}, u32[]{:S(2)}, u32[]{:S(2)}) collective-permute-start(bf16[576,256]{1,0:T(8,128)(2,1)S(1)} %shard_map.102.refs_0_), channel_id=1, source_target_pairs={{0,4},{2,6},{4,0},{6,2},{1,5},{3,7},{5,1},{7,3},{8,12},{10,14},{12... | collective-permute-start | bytes 884744 | tf_op jit(solution)/shard_map/ppermute | solution.py:29
  102.0 18.2 %collective-permute-start.12 = (bf16[576,256]{1,0:T(8,128)(2,1)S(1)}, bf16[576,256]{1,0:T(8,128)(2,1)S(1)}, u32[]{:S(2)}, u32[]{:S(2)}) collective-permute-start(bf16[576,256]{1,0:T(8,128)(2,1)S(1)} %collective-permute-done.11.refs_4_), channel_id=1, source_target_pairs={{0,2},{2,4},{4,6},{6,0},{1,3},{3,5},{5,7},{7,1},{8,10},{10,12},{12... | collective-permute-start | bytes 884744 | tf_op jit(solution)/shard_map/ppermute | solution.py:29
  102.0 25.5 %collective-permute-start.13 = (bf16[576,256]{1,0:T(8,128)(2,1)S(1)}, bf16[576,256]{1,0:T(8,128)(2,1)S(1)}, u32[]{:S(2)}, u32[]{:S(2)}) collective-permute-start(bf16[576,256]{1,0:T(8,128)(2,1)S(1)} %collective-permute-done.11.refs_4_), channel_id=1, source_target_pairs={{0,4},{2,6},{4,0},{6,2},{1,5},{3,7},{5,1},{7,3},{8,12},{10,14},{12... | collective-permute-start | bytes 884744 | tf_op jit(solution)/shard_map/ppermute | solution.py:29
  103.7 23.7 %collective-permute-start.14 = (bf16[576,256]{1,0:T(8,128)(2,1)S(1)}, bf16[576,256]{1,0:T(8,128)(2,1)S(1)}, u32[]{:S(2)}, u32[]{:S(2)}) collective-permute-start(bf16[576,256]{1,0:T(8,128)(2,1)S(1)} %collective-permute-done.11.refs_4_), channel_id=1, source_target_pairs={{0,6},{2,0},{4,2},{6,4},{1,7},{3,1},{5,3},{7,5},{8,14},{10,8},{12,... | collective-permute-start | bytes 884744 | tf_op jit(solution)/shard_map/ppermute | solution.py:29
  130.4 7.7 %collective-permute-start.31 = (bf16[256,512]{1,0:T(8,128)(2,1)S(1)}, bf16[256,512]{1,0:T(8,128)(2,1)S(1)}, u32[]{:S(2)}, u32[]{:S(2)}) collective-permute-start(bf16[256,512]{1,0:T(8,128)(2,1)S(1)} %key_value.1.refs_0_), channel_id=1, source_target_pairs={{0,64},{32,96},{64,0},{96,32},{1,65},{33,97},{65,1},{97,33},{2,66}... | collective-permute-start | bytes 786440 | tf_op jit(solution)/shard_map/ppermute | solution.py:29
  130.4 14.8 %collective-permute-start.30 = (bf16[256,512]{1,0:T(8,128)(2,1)S(1)}, bf16[256,512]{1,0:T(8,128)(2,1)S(1)}, u32[]{:S(2)}, u32[]{:S(2)}) collective-permute-start(bf16[256,512]{1,0:T(8,128)(2,1)S(1)} %key_value.1.refs_0_), channel_id=1, source_target_pairs={{0,32},{32,64},{64,96},{96,0},{1,33},{33,65},{65,97},{97,1},{2,34}... | collective-permute-start | bytes 786440 | tf_op jit(solution)/shard_map/ppermute | solution.py:29
  130.4 14.8 %collective-permute-start.32 = (bf16[256,512]{1,0:T(8,128)(2,1)S(1)}, bf16[256,512]{1,0:T(8,128)(2,1)}, u32[]{:S(2)}, u32[]{:S(2)}) collective-permute-start(bf16[256,512]{1,0:T(8,128)(2,1)S(1)} %key_value.1.refs_0_), channel_id=1, source_target_pairs={{0,96},{32,0},{64,32},{96,64},{1,97},{33,1},{65,33},{97,65},{2,98}... | collective-permute-start | bytes 786440 | tf_op jit(solution)/shard_map/ppermute | solution.py:29
  133.1 16.7 %collective-permute-start.33 = (bf16[256,512]{1,0:T(8,128)(2,1)S(1)}, bf16[256,512]{1,0:T(8,128)(2,1)S(1)}, u32[]{:S(2)}, u32[]{:S(2)}) collective-permute-start(bf16[256,512]{1,0:T(8,128)(2,1)S(1)} %key_value.1.refs_0_), channel_id=1, source_target_pairs={{0,8},{8,0},{1,9},{9,1},{2,10},{10,2},{3,11},{11,3},{4,12},{12,4},... | collective-permute-start | bytes 786440 | tf_op jit(solution)/shard_map/ppermute | solution.py:29
  136.5 14.7 %collective-permute-start.38 = (bf16[256,512]{1,0:T(8,128)(2,1)S(1)}, bf16[256,512]{1,0:T(8,128)(2,1)}, u32[]{:S(2)}, u32[]{:S(2)}) collective-permute-start(bf16[256,512]{1,0:T(8,128)(2,1)S(1)} %collective-permute-done.37.refs_8_), channel_id=1, source_target_pairs={{0,32},{32,64},{64,96},{96,0},{1,33},{33,65},{65,97},{97,1},{2,34}... | collective-permute-start | bytes 786440 | tf_op jit(solution)/shard_map/ppermute | solution.py:29
  138.1 13.6 %collective-permute-start.39 = (bf16[256,512]{1,0:T(8,128)(2,1)S(1)}, bf16[256,512]{1,0:T(8,128)(2,1)}, u32[]{:S(2)}, u32[]{:S(2)}) collective-permute-start(bf16[256,512]{1,0:T(8,128)(2,1)S(1)} %collective-permute-done.31.refs_2_), channel_id=1, source_target_pairs={{0,16},{16,0},{1,17},{17,1},{2,18},{18,2},{3,19},{19,3},{4,20},{20... | collective-permute-start | bytes 786440 | tf_op jit(solution)/shard_map/ppermute | solution.py:29
  145.2 8.8 %collective-permute-start.34 = (bf16[256,512]{1,0:T(8,128)(2,1)S(1)}, bf16[256,512]{1,0:T(8,128)(2,1)S(1)}, u32[]{:S(2)}, u32[]{:S(2)}) collective-permute-start(bf16[256,512]{1,0:T(8,128)(2,1)S(1)} %collective-permute-done.30.refs_1_), channel_id=1, source_target_pairs={{0,8},{8,0},{1,9},{9,1},{2,10},{10,2},{3,11},{11,3},{4,12},{12,4},... | collective-permute-start | bytes 786440 | tf_op jit(solution)/shard_map/ppermute | solution.py:29
  151.2 8.3 %collective-permute-start.41 = (bf16[256,512]{1,0:T(8,128)(2,1)S(1)}, bf16[256,512]{1,0:T(8,128)(2,1)}, u32[]{:S(2)}, u32[]{:S(2)}) collective-permute-start(bf16[256,512]{1,0:T(8,128)(2,1)S(1)} %collective-permute-done.37.refs_8_), channel_id=1, source_target_pairs={{0,8},{8,0},{1,9},{9,1},{2,10},{10,2},{3,11},{11,3},{4,12},{12,4},... | collective-permute-start | bytes 786440 | tf_op jit(solution)/shard_map/ppermute | solution.py:29
  151.7 7.8 %collective-permute-start.36 = (bf16[256,512]{1,0:T(8,128)(2,1)}, bf16[256,512]{1,0:T(8,128)(2,1)}, u32[]{:S(2)}, u32[]{:S(2)}) collective-permute-start(bf16[256,512]{1,0:T(8,128)(2,1)} %collective-permute-done.32.refs_3_), channel_id=1, source_target_pairs={{0,8},{8,0},{1,9},{9,1},{2,10},{10,2},{3,11},{11,3},{4,12},{12,4},... | collective-permute-start | bytes 786440 | tf_op jit(solution)/shard_map/ppermute | solution.py:29
  152.0 7.5 %collective-permute-start.42 = (bf16[256,512]{1,0:T(8,128)(2,1)}, bf16[256,512]{1,0:T(8,128)(2,1)}, u32[]{:S(2)}, u32[]{:S(2)}) collective-permute-start(bf16[256,512]{1,0:T(8,128)(2,1)} %collective-permute-done.38.refs_9_), channel_id=1, source_target_pairs={{0,8},{8,0},{1,9},{9,1},{2,10},{10,2},{3,11},{11,3},{4,12},{12,4},... | collective-permute-start | bytes 786440 | tf_op jit(solution)/shard_map/ppermute | solution.py:29
  170.8 22.5 %collective-permute-start.45 = (bf16[32,4608]{1,0:T(8,128)(2,1)S(1)}, bf16[32,4608]{1,0:T(8,128)(2,1)S(1)}, u32[]{:S(2)}, u32[]{:S(2)}) collective-permute-start(bf16[32,4608]{1,0:T(8,128)(2,1)S(1)} %get-tuple-element.38), channel_id=1, source_target_pairs={{0,2},{2,4},{4,6},{6,0},{1,3},{3,5},{5,7},{7,1},{8,10},{10,12},{12... | collective-permute-start | bytes 884744 | tf_op jit(solution)/shard_map/ppermute | solution.py:29
  170.9 22.4 %collective-permute-start.46 = (bf16[32,4608]{1,0:T(8,128)(2,1)S(1)}, bf16[32,4608]{1,0:T(8,128)(2,1)S(1)}, u32[]{:S(2)}, u32[]{:S(2)}) collective-permute-start(bf16[32,4608]{1,0:T(8,128)(2,1)S(1)} %get-tuple-element.39), channel_id=1, source_target_pairs={{0,4},{2,6},{4,0},{6,2},{1,5},{3,7},{5,1},{7,3},{8,12},{10,14},{12... | collective-permute-start | bytes 884744 | tf_op jit(solution)/shard_map/ppermute | solution.py:29
  171.0 23.4 %collective-permute-start.47 = (bf16[32,4608]{1,0:T(8,128)(2,1)S(1)}, bf16[32,4608]{1,0:T(8,128)(2,1)S(1)}, u32[]{:S(2)}, u32[]{:S(2)}) collective-permute-start(bf16[32,4608]{1,0:T(8,128)(2,1)S(1)} %get-tuple-element.40), channel_id=1, source_target_pairs={{0,6},{2,0},{4,2},{6,4},{1,7},{3,1},{5,3},{7,5},{8,14},{10,8},{12,... | collective-permute-start | bytes 884744 | tf_op jit(solution)/shard_map/ppermute | solution.py:29
  173.6 20.9 %collective-permute-start.48 = (bf16[32,4608]{1,0:T(8,128)(2,1)S(1)}, bf16[32,4608]{1,0:T(8,128)(2,1)S(1)}, u32[]{:S(2)}, u32[]{:S(2)}) collective-permute-start(bf16[32,4608]{1,0:T(8,128)(2,1)S(1)} %get-tuple-element.41), channel_id=1, source_target_pairs={{0,1},{1,0},{2,3},{3,2},{4,5},{5,4},{6,7},{7,6},{8,9},{9,8},{10,11... | collective-permute-start | bytes 884744 | tf_op jit(solution)/shard_map/ppermute | solution.py:29
  175.7 18.8 %collective-permute-start.49 = (bf16[32,4608]{1,0:T(8,128)(2,1)S(1)}, bf16[32,4608]{1,0:T(8,128)(2,1)S(1)}, u32[]{:S(2)}, u32[]{:S(2)}) collective-permute-start(bf16[32,4608]{1,0:T(8,128)(2,1)S(1)} %get-tuple-element.42), channel_id=1, source_target_pairs={{0,3},{1,2},{2,5},{3,4},{4,7},{5,6},{6,1},{7,0},{8,11},{9,10},{10,... | collective-permute-start | bytes 884744 | tf_op jit(solution)/shard_map/ppermute | solution.py:484
  193.3 11.6 %collective-permute-start.50 = (bf16[32,4608]{1,0:T(8,128)(2,1)S(1)}, bf16[32,4608]{1,0:T(8,128)(2,1)S(1)}, u32[]{:S(2)}, u32[]{:S(2)}) collective-permute-start(bf16[32,4608]{1,0:T(8,128)(2,1)S(1)} %get-tuple-element.43), channel_id=1, source_target_pairs={{0,5},{1,4},{2,7},{3,6},{4,1},{5,0},{6,3},{7,2},{8,13},{9,12},{10,... | collective-permute-start | bytes 884744 | tf_op jit(solution)/shard_map/ppermute | solution.py:484
  193.3 14.8 %collective-permute-start.51 = (bf16[32,4608]{1,0:T(8,128)(2,1)S(1)}, bf16[32,4608]{1,0:T(8,128)(2,1)S(1)}, u32[]{:S(2)}, u32[]{:S(2)}) collective-permute-start(bf16[32,4608]{1,0:T(8,128)(2,1)S(1)} %get-tuple-element.44), channel_id=1, source_target_pairs={{0,7},{1,6},{2,1},{3,0},{4,3},{5,2},{6,5},{7,4},{8,15},{9,14},{10,... | collective-permute-start | bytes 884744 | tf_op jit(solution)/shard_map/ppermute | solution.py:484
  210.0 8.2 %collective-permute-start.52 = (bf16[32,4608]{1,0:T(8,128)(2,1)S(1)}, bf16[32,4608]{1,0:T(8,128)(2,1)S(1)}, u32[]{:S(2)}, u32[]{:S(2)}) collective-permute-start(bf16[32,4608]{1,0:T(8,128)(2,1)S(1)} %finish.1.refs_0_), channel_id=1, source_target_pairs={{0,8},{8,0},{1,9},{9,1},{2,10},{10,2},{3,11},{11,3},{4,12},{12,4},... | collective-permute-start | bytes 884744 | tf_op jit(solution)/shard_map/ppermute | solution.py:29
  220.3 10.3 %collective-permute-start.56 = (bf16[16,4608]{1,0:T(8,128)(2,1)S(1)}, bf16[16,4608]{1,0:T(8,128)(2,1)S(1)}, u32[]{:S(2)}, u32[]{:S(2)}) collective-permute-start(bf16[16,4608]{1,0:T(8,128)(2,1)S(1)} %get-tuple-element.47), channel_id=1, source_target_pairs={{0,64},{32,96},{64,0},{96,32},{1,65},{33,97},{65,1},{97,33},{2,66}... | collective-permute-start | bytes 442376 | tf_op jit(solution)/shard_map/ppermute | solution.py:29
  234.3 7.4 %collective-permute-start.59 = (bf16[16,4608]{1,0:T(8,128)(2,1)S(1)}, bf16[16,4608]{1,0:T(8,128)(2,1)S(1)}, u32[]{:S(2)}, u32[]{:S(2)}) collective-permute-start(bf16[16,4608]{1,0:T(8,128)(2,1)S(1)} %get-tuple-element.51), channel_id=1, source_target_pairs={{0,4},{2,6},{4,0},{6,2},{1,5},{3,7},{5,1},{7,3},{8,12},{10,14},{12... | collective-permute-start | bytes 442376 | tf_op jit(solution)/shard_map/ppermute | solution.py:29
  (30 other events, 224.3 us)
Sparse Core Ops, SparseCore 0:
  9.0 90.2 all-gather.1

commit v4 on v3

--- a/solution.py
+++ b/solution.py
@@ -79,19 +79,6 @@
         copy.start()
     for copy in copies:
         copy.wait()
-
-
-def join_kernel(query, out_t, joined, sems):
-    half = 4 * HEAD
-    fetch([(query, joined.at[:, :half]), (out_t, joined.at[:, half:])], sems)
-
-
-def hold_kernel(key, value, held, sems):
-    jobs = []
-    for n, source in enumerate((key, value, key, value)):
-        first = n // 2 * HEAD
-        jobs.append((source.at[:, first : first + HEAD], held.at[:, n * HEAD : (n + 1) * HEAD]))
-    fetch(jobs, sems)
 
 
 def pack_kernel(flat, *refs):
@@ -104,14 +91,22 @@
         whole[pl.ds(pl.multiple_of(first, 32), size), :] = part[...]
 
 
-def leave_kernel(flat, old_blocks, order, x_old, *refs):
-    outs, sems = refs[:4], refs[4]
+def before(blocks, shard):
+    result = jnp.int32(0)
+    for m in range(16):
+        result = result + jnp.where(m < shard, blocks[m], 0)
+    return result
+
+
+def leave_kernel(flat, old_blocks, order, key, value, query, out_t, x_old, *refs):
+    joined, held, outs, sems = refs[0], refs[1], refs[2:6], refs[6]
     x, yl, c, _, _ = spot(flat)
-    shard = order[4 * x + 2 * yl + c]
-    first = jnp.int32(0)
-    for m in range(16):
-        first = first + jnp.where(m < shard, old_blocks[m], 0)
-    jobs = []
+    half = 4 * HEAD
+    jobs = [(query, joined.at[:, :half]), (out_t, joined.at[:, half:])]
+    for n, source in enumerate((key, value, key, value)):
+        first = n // 2 * HEAD
+        jobs.append((source.at[:, first : first + HEAD], held.at[:, n * HEAD : (n + 1) * HEAD]))
+    first = before(old_blocks, order[4 * x + 2 * yl + c])
     for d in range(4):
         row = jnp.bitwise_and(x + d - first, 3) * BLOCK
         jobs.append((x_old.at[:, lanes(row)], outs[d]))
@@ -288,13 +283,6 @@
     out[...] = (resident[...].astype(F32) + total * scale * gain[...]).astype(BF16)
 
 
-def before(blocks, shard):
-    result = jnp.int32(0)
-    for m in range(16):
-        result = result + jnp.where(m < shard, blocks[m], 0)
-    return result
-
-
 def owner_kernel(flat, new_blocks, *refs):
     by_w, outs = refs[:4], refs[4:]
     x, yl, c, _, _ = spot(flat)
@@ -356,17 +344,6 @@
         )(flat, *tables, *near_by(arrays))
         return list(results)
 
-    def bring(kernel, tables, arrays, shapes, copies, kind):
-        results = pl.pallas_call(
-            kernel,
-            in_specs=[SMEM] * len(tables) + [AWAY] * len(arrays),
-            out_specs=[VMEM] * len(shapes),
-            out_shape=[kind(s, BF16) for s in shapes],
-            scratch_shapes=[pltpu.SemaphoreType.DMA((copies,))],
-            compiler_params=grant(8),
-        )(*tables, *far_off(arrays))
-        return list(results)
-
     def everywhere(part):
         opposite = shift(part, "x", 2)
         pair = shift(part, "yl", 1)
@@ -378,33 +355,44 @@
             result += [shift(s, "c", 1) for s in parts]
         return result
 
-    (joined,) = bring(
-        join_kernel, (), (w_query, w_out_t), [(w_query.shape[0], 8 * HEAD)], 2, jax.ShapeDtypeStruct
+    old = far_off((old_blocks, order))
+    depth = w_key.shape[0]
+    joined, held, *near = pl.pallas_call(
+        leave_kernel,
+        in_specs=[SMEM] * 3 + [AWAY] * 5,
+        out_specs=[VMEM] * 6,
+        out_shape=[
+            jax.ShapeDtypeStruct((depth, 8 * HEAD), BF16),
+            pltpu.VMEM((depth, 4 * HEAD), BF16),
+        ]
+        + [pltpu.VMEM((width, BLOCK), BF16)] * 4,
+        scratch_shapes=[pltpu.SemaphoreType.DMA((10,))],
+        compiler_params=grant(8),
+        name="leave",
+    )(flat, *old, *far_off((w_key, w_value, w_query, w_out_t, x_old.T)))
+    joined_full = lax.all_gather(joined, SEQ, axis=0, tiled=True)
+    pair = shift(held, "yl", 1)
+    near = near[:1] + [shift(near[d], "x", d) for d in range(1, 4)]
+    same = [held] + [shift(held, "x", d) for d in range(1, 4)]
+    far = [shift(near[0], "c", 1)]
+    far += [shift(part, "c", 1) for part in near[1:]]
+    mine, cross = call(sort_kernel, old, near + far, [(width, count)] * 2)
+
+    crossed = shift(cross, "yl", 1)
+    both = [(a, b) for a in range(2) for b in range(2)]
+    diagonal = lax.ppermute(
+        cross, ("yl", "yh"), [(2 * a + b, 2 * (1 - a) + 1 - b) for a, b in both]
     )
-    joined_full = lax.all_gather(joined, SEQ, axis=0, tiled=True)
-
-    (held,) = bring(hold_kernel, (), (w_key, w_value), [(w_key.shape[0], 4 * HEAD)], 4, pltpu.VMEM)
-    pair = shift(held, "yl", 1)
-
-    old = far_off((old_blocks, order))
-    near = bring(leave_kernel, (flat, *old), (x_old.T,), [(width, BLOCK)] * 4, 4, pltpu.VMEM)
-    near = near[:1] + [shift(near[d], "x", d) for d in range(1, 4)]
-    far = [shift(part, "c", 1) for part in near]
-    mine, cross = call(sort_kernel, old, near + far, [(width, count)] * 2)
-    same = [held] + [shift(held, "x", d) for d in range(1, 4)]
-    other = [pair] + [shift(pair, "x", d) for d in range(1, 4)]
+    opposite = shift(mine, "yh", 1)
+    other = [pair, shift(pair, "x", 1), shift(pair, "x", 3)]
+    (rows,) = call(settle_kernel, old, (mine, crossed), [(width, count)])
+    pieces = [rows] + [shift(rows, "z", d) for d in range(1, 4)]
+    (facing,) = call(settle_kernel, old, (opposite, diagonal), [(width, count)])
+    pieces += [facing] + [shift(facing, "z", d) for d in range(1, 4)]
+    other.insert(2, shift(same[2], "yl", 1))
     spread_weights = [
-        w
-        for parts in (same, other)
-        for w in parts + [shift(s, "c", 1) for s in parts]
+        w for parts in (same, other) for w in parts + [shift(s, "c", 1) for s in parts]
     ]
-
-    cross = shift(cross, "yl", 1)
-    (rows,) = call(settle_kernel, old, (mine, cross), [(width, count)])
-
-    facing = shift(rows, "yh", 1)
-    pieces = [rows] + [shift(rows, "z", d) for d in range(1, 4)]
-    pieces += [facing] + [shift(facing, "z", d) for d in range(1, 4)]
 
     slot_rows = jnp.arange(BLOCK, dtype=jnp.int32)
     x, w = flat[0] >> 5, (flat[0] >> 3) & 3

time: 251 us -> 238 us (0.948)
  waiting for transfers between devices: 123 us -> 97 us
  starting transfers between devices: 76.5 us -> 87.6 us
    ppermute x58, waiting for transfers between devices: 109 us -> 86.9 us  [shift(): return lax.ppermute(value, axis, [(i, (i + by) % n) for i in range(n)])]
    ppermute x58, starting transfers between devices: 74.2 us -> 83.5 us  [shift(): return lax.ppermute(value, axis, [(i, (i + by) % n) for i in range(n)])]
    ppermute x3, waiting for transfers between devices: 13.6 us -> 10 us  [per_device(): lax.ppermute(part, TP, [(2 * i + j, 2 * ((i + dz) % 4) + (j ^ dy)) for i,...]
    unnamed x33 -> x45, local copies, waits for them, and re-layouts: 7.73 us -> 9.25 us
    pallas_call x6 -> x7, Pallas kernels: 5.71 us -> 6.81 us  [call(): pl.pallas_call(kernel, in_specs=[SMEM] * (1 + len(tables)) + [VMEM] * len...]
  transfers between devices with their start and end apart: 62 -> 63, of which waited for: 23 -> 22; matrix products, arithmetic and copies ran while one was open for 0% -> 0% of each run, Pallas kernels for 5% -> 4%
where the time goes in v4:
time: 238 us; the launch traced here: 236 us
  waiting for transfers between devices  97 us (41%)
  starting transfers between devices  87.6 us (37%)
  Pallas kernels  27.7 us (12%)
  between operations  13.9 us (6%)
  local copies, waits for them, and re-layouts  9.28 us (4%)
    ppermute x58, waiting for transfers between devices, shift(): return lax.ppermute(value, axis, [(i, (i + by) % n) for i in range(n)])  86.9 us
    ppermute x58, starting transfers between devices, shift(): return lax.ppermute(value, axis, [(i, (i + by) % n) for i in range(n)])  83.5 us
    ppermute x3, waiting for transfers between devices, per_device(): lax.ppermute(part, TP, [(2 * i + j, 2 * ((i + dz) % 4) + (j ^ dy)) for i,...  10 us
    unnamed x45, local copies, waits for them, and re-layouts  9.25 us
    pallas_call x1, Pallas kernels, per_device(): pl.pallas_call(attention_kernel, in_specs=[SMEM] + [VMEM] * 17, out_specs...  7 us
    pallas_call x7, Pallas kernels, call(): pl.pallas_call(kernel, in_specs=[SMEM] * (1 + len(tables)) + [VMEM] * len...  6.81 us
  transfers between devices with their start and end apart: 63, of which 22 were waited for; matrix products, arithmetic and copies ran while one was open for 0% of the time, Pallas kernels for 4%

profile of v4, /device:TPU:1, one launch (start us, length us, event | category | flops | bytes accessed | tf_op | source)
XLA Modules:
  0.0 236.2 jit_solution(3242722260573871248)
XLA Ops:
  6.5 3.0 %leave.1 = (bf16[288,1024]{1,0:T(8,128)(2,1)}, bf16[288,512]{1,0:T(8,128)(2,1)S(1)}, bf16[576,128]{1,0:T(8,128)(2,1)S(1)}, bf16[576,128]{1,0:T(8,128)(2,1)S(1)},...) custom-call(s32[1]{0:T(128)} %bitcast.flat, s32[16]{0:T(128)} %old_blocks.7, s32[16]{0:T(128)} %order.7, ...), custom_call_target="tpu_custom_call" | custom-call | tf_op jit(solution)/shard_map/leave/pallas_call | solution.py:360
  9.6 2.1 collective-permute-start
  11.7 2.5 %collective-permute-start.1 = (bf16[576,128]{1,0:T(8,128)(2,1)S(1)}, bf16[576,128]{1,0:T(8,128)(2,1)S(1)}, u32[]{:S(2)}, u32[]{:S(2)}) collective-permute-start(bf16[576,128]{1,0:T(8,128)(2,1)S(1)} %get-tuple-element.33), channel_id=1, source_target_pairs={{0,64},{32,96},{64,0},{96,32},{1,65},{33,97},{65,1},{97,33},{2,66}... | collective-permute-start | bytes 442376 | tf_op jit(solution)/shard_map/ppermute | solution.py:29
  15.3 1.5 collective-permute-start.3
  17.8 2.8 %collective-permute-done.1.refs_2_ = bf16[576,128]{1,0:T(8,128)(2,1)S(1)} collective-permute-done((bf16[576,128]{1,0:T(8,128)(2,1)S(1)}, bf16[576,128]{1,0:T(8,128)(2,1)S(1)}, u32[]{:S(2)}, u32[]{:S(2)}) %collective-permute-start.1) | collective-permute-done | bytes 147488 | tf_op jit(solution)/shard_map/ppermute | solution.py:29
  20.6 1.5 collective-permute-start.5
  23.4 2.4 %collective-permute-start.17 = (bf16[288,512]{1,0:T(8,128)(2,1)S(1)}, bf16[288,512]{1,0:T(8,128)(2,1)S(1)}, u32[]{:S(2)}, u32[]{:S(2)}) collective-permute-start(bf16[288,512]{1,0:T(8,128)(2,1)S(1)} %get-tuple-element.40.refs_0_), channel_id=1, source_target_pairs={{0,64},{32,96},{64,0},{96,32},{1,65},{33,97},{65,1},{97,33},{2,66}... | collective-permute-start | bytes 884744 | tf_op jit(solution)/shard_map/ppermute | solution.py:29
  26.9 2.7 %collective-permute-start.11 = (bf16[576,256]{1,0:T(8,128)(2,1)S(1)}, bf16[576,256]{1,0:T(8,128)(2,1)S(1)}, u32[]{:S(2)}, u32[]{:S(2)}) collective-permute-start(bf16[576,256]{1,0:T(8,128)(2,1)S(1)} %get-tuple-element.35.mine), channel_id=1, source_target_pairs={{0,1},{1,0},{2,3},{3,2},{4,5},{5,4},{6,7},{7,6},{8,9},{9,8},{10,11... | collective-permute-start | bytes 884744 | tf_op jit(solution)/shard_map/ppermute | solution.py:29
  29.8 7.1 %collective-permute-done.23.refs_8_ = bf16[288,512]{1,0:T(8,128)(2,1)S(1)} collective-permute-done((bf16[288,512]{1,0:T(8,128)(2,1)S(1)}, bf16[288,512]{1,0:T(8,128)(2,1)S(1)}, u32[]{:S(2)}, u32[]{:S(2)}) %collective-permute-start.23) | collective-permute-done | bytes 294944 | tf_op jit(solution)/shard_map/ppermute | solution.py:29
  36.9 2.2 collective-permute-start.18
  40.0 1.9 collective-permute-start.19
  41.9 10.3 %collective-permute-done.11.mine = bf16[576,256]{1,0:T(8,128)(2,1)S(1)} collective-permute-done((bf16[576,256]{1,0:T(8,128)(2,1)S(1)}, bf16[576,256]{1,0:T(8,128)(2,1)S(1)}, u32[]{:S(2)}, u32[]{:S(2)}) %collective-permute-start.11) | collective-permute-done | bytes 294944 | tf_op jit(solution)/shard_map/ppermute | solution.py:29
  53.1 2.7 %collective-permute-start.26 = (bf16[288,512]{1,0:T(8,128)(2,1)S(1)}, bf16[288,512]{1,0:T(8,128)(2,1)}, u32[]{:S(2)}, u32[]{:S(2)}) collective-permute-start(bf16[288,512]{1,0:T(8,128)(2,1)S(1)} %collective-permute-done.23.refs_8_), channel_id=1, source_target_pairs={{0,96},{32,0},{64,32},{96,64},{1,97},{33,1},{65,33},{97,65},{2,98}... | collective-permute-start | bytes 884744 | tf_op jit(solution)/shard_map/ppermute | solution.py:29
  55.8 1.5 collective-permute-start.25
  57.3 2.5 %collective-permute-start.27 = (bf16[288,512]{1,0:T(8,128)(2,1)S(1)}, bf16[288,512]{1,0:T(8,128)(2,1)S(1)}, u32[]{:S(2)}, u32[]{:S(2)}) collective-permute-start(bf16[288,512]{1,0:T(8,128)(2,1)S(1)} %collective-permute-done.23.refs_8_), channel_id=1, source_target_pairs={{0,8},{8,0},{1,9},{9,1},{2,10},{10,2},{3,11},{11,3},{4,12},{12,4},... | collective-permute-start | bytes 884744 | tf_op jit(solution)/shard_map/ppermute | solution.py:29
  59.8 5.2 %collective-permute-done.24.refs_9_ = bf16[288,512]{1,0:T(8,128)(2,1)} collective-permute-done((bf16[288,512]{1,0:T(8,128)(2,1)S(1)}, bf16[288,512]{1,0:T(8,128)(2,1)}, u32[]{:S(2)}, u32[]{:S(2)}) %collective-permute-start.24) | collective-permute-done | bytes 294944 | tf_op jit(solution)/shard_map/ppermute | solution.py:29
  65.0 1.8 collective-permute-start.21
  67.3 1.8 collective-permute-start.13
  69.9 3.4 %collective-permute-start.14 = (bf16[576,256]{1,0:T(8,128)(2,1)S(1)}, bf16[576,256]{1,0:T(8,128)(2,1)S(1)}, u32[]{:S(2)}, u32[]{:S(2)}) collective-permute-start(bf16[576,256]{1,0:T(8,128)(2,1)S(1)} %shard_map.102.refs_4_), channel_id=1, source_target_pairs={{0,4},{2,6},{4,0},{6,2},{1,5},{3,7},{5,1},{7,3},{8,12},{10,14},{12... | collective-permute-start | bytes 884744 | tf_op jit(solution)/shard_map/ppermute | solution.py:29
  73.3 6.6 %collective-permute-done.25.refs_10_ = bf16[288,512]{1,0:T(8,128)(2,1)} collective-permute-done((bf16[288,512]{1,0:T(8,128)(2,1)S(1)}, bf16[288,512]{1,0:T(8,128)(2,1)}, u32[]{:S(2)}, u32[]{:S(2)}) %collective-permute-start.25) | collective-permute-done | bytes 294944 | tf_op jit(solution)/shard_map/ppermute | solution.py:29
  79.9 4.0 %collective-permute-start.15 = (bf16[576,256]{1,0:T(8,128)(2,1)S(1)}, bf16[576,256]{1,0:T(8,128)(2,1)S(1)}, u32[]{:S(2)}, u32[]{:S(2)}) collective-permute-start(bf16[576,256]{1,0:T(8,128)(2,1)S(1)} %shard_map.102.refs_4_), channel_id=1, source_target_pairs={{0,6},{2,0},{4,2},{6,4},{1,7},{3,1},{5,3},{7,5},{8,14},{10,8},{12,... | collective-permute-start | bytes 884744 | tf_op jit(solution)/shard_map/ppermute | solution.py:29
  86.1 2.9 %collective-permute-start.20 = (bf16[288,512]{1,0:T(8,128)(2,1)}, bf16[288,512]{1,0:T(8,128)(2,1)S(1)}, u32[]{:S(2)}, u32[]{:S(2)}) collective-permute-start(bf16[288,512]{1,0:T(8,128)(2,1)} %collective-permute-done.16.refs_1_), channel_id=1, source_target_pairs={{0,8},{8,0},{1,9},{9,1},{2,10},{10,2},{3,11},{11,3},{4,12},{12,4},... | collective-permute-start | bytes 884744 | tf_op jit(solution)/shard_map/ppermute | solution.py:29
  89.0 4.7 %collective-permute-start.22 = (bf16[288,512]{1,0:T(8,128)(2,1)}, bf16[288,512]{1,0:T(8,128)(2,1)S(1)}, u32[]{:S(2)}, u32[]{:S(2)}) collective-permute-start(bf16[288,512]{1,0:T(8,128)(2,1)} %collective-permute-done.18.refs_3_), channel_id=1, source_target_pairs={{0,8},{8,0},{1,9},{9,1},{2,10},{10,2},{3,11},{11,3},{4,12},{12,4},... | collective-permute-start | bytes 884744 | tf_op jit(solution)/shard_map/ppermute | solution.py:29
  93.7 2.6 %collective-permute-done.10.refs_3_ = bf16[576,256]{1,0:T(8,128)(2,1)S(1)} collective-permute-done((bf16[576,256]{1,0:T(8,128)(2,1)S(1)}, bf16[576,256]{1,0:T(8,128)(2,1)S(1)}, u32[]{:S(2)}, u32[]{:S(2)}) %collective-permute-start.10) | collective-permute-done | bytes 294944 | tf_op jit(solution)/shard_map/ppermute | solution.py:29
  96.3 7.4 %collective-permute-start.28 = (bf16[288,512]{1,0:T(8,128)(2,1)}, bf16[288,512]{1,0:T(8,128)(2,1)S(1)}, u32[]{:S(2)}, u32[]{:S(2)}) collective-permute-start(bf16[288,512]{1,0:T(8,128)(2,1)} %collective-permute-done.24.refs_9_), channel_id=1, source_target_pairs={{0,8},{8,0},{1,9},{9,1},{2,10},{10,2},{3,11},{11,3},{4,12},{12,4},... | collective-permute-start | bytes 884744 | tf_op jit(solution)/shard_map/ppermute | solution.py:29
  111.1 1.6 shard_map.104.weight
  114.4 3.1 %collective-permute-start.31 = (bf16[256,512]{1,0:T(8,128)(2,1)S(1)}, bf16[256,512]{1,0:T(8,128)(2,1)S(1)}, u32[]{:S(2)}, u32[]{:S(2)}) collective-permute-start(bf16[256,512]{1,0:T(8,128)(2,1)S(1)} %key_value.1.refs_0_), channel_id=1, source_target_pairs={{0,32},{32,64},{64,96},{96,0},{1,33},{33,65},{65,97},{97,1},{2,34}... | collective-permute-start | bytes 786440 | tf_op jit(solution)/shard_map/ppermute | solution.py:29
  118.6 3.3 %collective-permute-done.38.refs_8_ = bf16[256,512]{1,0:T(8,128)(2,1)S(1)} collective-permute-done((bf16[256,512]{1,0:T(8,128)(2,1)S(1)}, bf16[256,512]{1,0:T(8,128)(2,1)S(1)}, u32[]{:S(2)}, u32[]{:S(2)}) %collective-permute-start.38) | collective-permute-done | bytes 262176 | tf_op jit(solution)/shard_map/ppermute | solution.py:29
  124.7 4.6 %collective-permute-done.31.refs_1_ = bf16[256,512]{1,0:T(8,128)(2,1)S(1)} collective-permute-done((bf16[256,512]{1,0:T(8,128)(2,1)S(1)}, bf16[256,512]{1,0:T(8,128)(2,1)S(1)}, u32[]{:S(2)}, u32[]{:S(2)}) %collective-permute-start.31) | collective-permute-done | bytes 262176 | tf_op jit(solution)/shard_map/ppermute | solution.py:29
  129.3 2.5 %collective-permute-start.35 = (bf16[256,512]{1,0:T(8,128)(2,1)S(1)}, bf16[256,512]{1,0:T(8,128)(2,1)S(1)}, u32[]{:S(2)}, u32[]{:S(2)}) collective-permute-start(bf16[256,512]{1,0:T(8,128)(2,1)S(1)} %collective-permute-done.31.refs_1_), channel_id=1, source_target_pairs={{0,8},{8,0},{1,9},{9,1},{2,10},{10,2},{3,11},{11,3},{4,12},{12,4},... | collective-permute-start | bytes 786440 | tf_op jit(solution)/shard_map/ppermute | solution.py:29
  133.2 1.8 collective-permute-done.39.refs_9_
  136.3 1.9 collective-permute-start.43
  140.1 3.5 %shard_map.103.query = bf16[256,512]{1,0:T(8,128)(2,1)S(1)} custom-call(bf16[256,4608]{1,0:T(8,128)(2,1)S(1)} %get-tuple-element.38.normed, bf16[4608,1024]{1,0:T(8,128)(2,1)} %all-gather.2.cloned.1.call-done.weight, f32[256,128]{1,0:T(8,128)S(1)} %pad_maximum_fusion.cos, f32[256,128]{1,0:T(8,128)S(1)} %pad_maximum_fusion.1.sin), custom_call_target="tpu_custom_call" | custom-call | tf_op jit(solution)/shard_map/pallas_call | solution.py:420
  143.7 7.0 %attention.1.context = bf16[256,512]{1,0:T(8,128)(2,1)S(1)} custom-call(s32[1]{0:T(128)} %bitcast.flat, bf16[256,512]{1,0:T(8,128)(2,1)S(1)} %shard_map.103.query, bf16[256,512]{1,0:T(8,128)(2,1)S(1)} %key_value.1.refs_0_, bf16[256,512]{1,0:T(8,128)(2,1)S(1)} %copy-done.13, bf16[256,512]{1,0:T(8,128)(2,1)S(1)} %collective-permute-done.32.refs_2_, ...), custom_call_target="tpu_custom_call" | custom-call | tf_op jit(solution)/shard_map/attention/pallas_call | solution.py:442
  150.7 4.3 %project.1 = (bf16[32,4608]{1,0:T(8,128)(2,1)S(1)}, bf16[32,4608]{1,0:T(8,128)(2,1)S(1)}, bf16[32,4608]{1,0:T(8,128)(2,1)S(1)}, bf16[32,4608]{1,0:T(8,128)(2,1)S...) custom-call(s32[1]{0:T(128)} %bitcast.flat, ...), custom_call_target="tpu_custom_call" | custom-call | tf_op jit(solution)/shard_map/project/pallas_call | solution.py:453
  156.0 3.7 %collective-permute-start.47 = (bf16[32,4608]{1,0:T(8,128)(2,1)S(1)}, bf16[32,4608]{1,0:T(8,128)(2,1)S(1)}, u32[]{:S(2)}, u32[]{:S(2)}) collective-permute-start(bf16[32,4608]{1,0:T(8,128)(2,1)S(1)} %get-tuple-element.43), channel_id=1, source_target_pairs={{0,4},{2,6},{4,0},{6,2},{1,5},{3,7},{5,1},{7,3},{8,12},{10,14},{12... | collective-permute-start | bytes 884744 | tf_op jit(solution)/shard_map/ppermute | solution.py:29
  160.6 3.3 %collective-permute-start.50 = (bf16[32,4608]{1,0:T(8,128)(2,1)S(1)}, bf16[32,4608]{1,0:T(8,128)(2,1)S(1)}, u32[]{:S(2)}, u32[]{:S(2)}) collective-permute-start(bf16[32,4608]{1,0:T(8,128)(2,1)S(1)} %get-tuple-element.46), channel_id=1, source_target_pairs={{0,3},{1,2},{2,5},{3,4},{4,7},{5,6},{6,1},{7,0},{8,11},{9,10},{10,... | collective-permute-start | bytes 884744 | tf_op jit(solution)/shard_map/ppermute | solution.py:472
  163.9 2.0 collective-permute-done.46.refs_1_
  166.7 19.1 %collective-permute-done.47.refs_2_ = bf16[32,4608]{1,0:T(8,128)(2,1)S(1)} collective-permute-done((bf16[32,4608]{1,0:T(8,128)(2,1)S(1)}, bf16[32,4608]{1,0:T(8,128)(2,1)S(1)}, u32[]{:S(2)}, u32[]{:S(2)}) %collective-permute-start.47) | collective-permute-done | bytes 294944 | tf_op jit(solution)/shard_map/ppermute | solution.py:29
  185.8 10.0 %collective-permute-done.52.refs_7_ = bf16[32,4608]{1,0:T(8,128)(2,1)S(1)} collective-permute-done((bf16[32,4608]{1,0:T(8,128)(2,1)S(1)}, bf16[32,4608]{1,0:T(8,128)(2,1)S(1)}, u32[]{:S(2)}, u32[]{:S(2)}) %collective-permute-start.52) | collective-permute-done | bytes 294944 | tf_op jit(solution)/shard_map/ppermute | solution.py:472
  197.7 2.2 collective-permute-start.53
  199.9 3.4 %collective-permute-done.54.refs_2_ = bf16[32,4608]{1,0:T(8,128)(2,1)S(1)} collective-permute-done((bf16[32,4608]{1,0:T(8,128)(2,1)S(1)}, bf16[32,4608]{1,0:T(8,128)(2,1)S(1)}, u32[]{:S(2)}, u32[]{:S(2)}) %collective-permute-start.54) | collective-permute-done | bytes 294944 | tf_op jit(solution)/shard_map/ppermute | solution.py:29
  203.3 2.6 %collective-permute-start.55 = (bf16[32,4608]{1,0:T(8,128)(2,1)S(1)}, bf16[32,4608]{1,0:T(8,128)(2,1)S(1)}, u32[]{:S(2)}, u32[]{:S(2)}) collective-permute-start(bf16[32,4608]{1,0:T(8,128)(2,1)S(1)} %collective-permute-done.54.refs_2_), channel_id=1, source_target_pairs={{0,8},{8,0},{1,9},{9,1},{2,10},{10,2},{3,11},{11,3},{4,12},{12,4},... | collective-permute-start | bytes 884744 | tf_op jit(solution)/shard_map/ppermute | solution.py:29
  208.1 2.4 %collective-permute-start.57 = (bf16[16,4608]{1,0:T(8,128)(2,1)S(1)}, bf16[16,4608]{1,0:T(8,128)(2,1)S(1)}, u32[]{:S(2)}, u32[]{:S(2)}) collective-permute-start(bf16[16,4608]{1,0:T(8,128)(2,1)S(1)} %get-tuple-element.51), channel_id=1, source_target_pairs={{0,64},{32,96},{64,0},{96,32},{1,65},{33,97},{65,1},{97,33},{2,66}... | collective-permute-start | bytes 442376 | tf_op jit(solution)/shard_map/ppermute | solution.py:29
  210.7 3.8 %collective-permute-done.56.refs_1_ = bf16[16,4608]{1,0:T(8,128)(2,1)S(1)} collective-permute-done((bf16[16,4608]{1,0:T(8,128)(2,1)S(1)}, bf16[16,4608]{1,0:T(8,128)(2,1)S(1)}, u32[]{:S(2)}, u32[]{:S(2)}) %collective-permute-start.56) | collective-permute-done | bytes 147488 | tf_op jit(solution)/shard_map/ppermute | solution.py:29
  214.6 2.6 %collective-permute-done.57.refs_2_ = bf16[16,4608]{1,0:T(8,128)(2,1)S(1)} collective-permute-done((bf16[16,4608]{1,0:T(8,128)(2,1)S(1)}, bf16[16,4608]{1,0:T(8,128)(2,1)S(1)}, u32[]{:S(2)}, u32[]{:S(2)}) %collective-permute-start.57) | collective-permute-done | bytes 147488 | tf_op jit(solution)/shard_map/ppermute | solution.py:29
  219.6 1.8 collective-permute-start.61
  221.4 6.4 %collective-permute-done.59.refs_1_ = bf16[16,4608]{1,0:T(8,128)(2,1)S(1)} collective-permute-done((bf16[16,4608]{1,0:T(8,128)(2,1)S(1)}, bf16[16,4608]{1,0:T(8,128)(2,1)S(1)}, u32[]{:S(2)}, u32[]{:S(2)}) %collective-permute-start.59) | collective-permute-done | bytes 147488 | tf_op jit(solution)/shard_map/ppermute | solution.py:29
  (146 shorter events, 38.0 us)
Async XLA Ops:
  6.5 133.5 %all-gather.2.cloned.1.call-start = ((), (), s32[]{:S(2)}) async-start(), calls=%async_computation | async-start | bytes 10027008 | tf_op jit(solution)/shard_map/all_gather | solution.py:373
  11.7 8.9 %collective-permute-start.1 = (bf16[576,128]{1,0:T(8,128)(2,1)S(1)}, bf16[576,128]{1,0:T(8,128)(2,1)S(1)}, u32[]{:S(2)}, u32[]{:S(2)}) collective-permute-start(bf16[576,128]{1,0:T(8,128)(2,1)S(1)} %get-tuple-element.33), channel_id=1, source_target_pairs={{0,64},{32,96},{64,0},{96,32},{1,65},{33,97},{65,1},{97,33},{2,66}... | collective-permute-start | bytes 442376 | tf_op jit(solution)/shard_map/ppermute | solution.py:29
  14.2 8.0 %collective-permute-start.2 = (bf16[576,128]{1,0:T(8,128)(2,1)S(1)}, bf16[576,128]{1,0:T(8,128)(2,1)S(1)}, u32[]{:S(2)}, u32[]{:S(2)}) collective-permute-start(bf16[576,128]{1,0:T(8,128)(2,1)S(1)} %get-tuple-element.34), channel_id=1, source_target_pairs={{0,96},{32,0},{64,32},{96,64},{1,97},{33,1},{65,33},{97,65},{2,98}... | collective-permute-start | bytes 442376 | tf_op jit(solution)/shard_map/ppermute | solution.py:29
  15.3 8.1 %collective-permute-start.3 = (bf16[576,128]{1,0:T(8,128)(2,1)S(1)}, bf16[576,128]{1,0:T(8,128)(2,1)S(1)}, u32[]{:S(2)}, u32[]{:S(2)}) collective-permute-start(bf16[576,128]{1,0:T(8,128)(2,1)S(1)} %get-tuple-element.31.refs_0_), channel_id=1, source_target_pairs={{0,8},{8,0},{1,9},{9,1},{2,10},{10,2},{3,11},{11,3},{4,12},{12,4},... | collective-permute-start | bytes 442376 | tf_op jit(solution)/shard_map/ppermute | solution.py:29
  16.8 9.0 %collective-permute-start.4 = (bf16[576,128]{1,0:T(8,128)(2,1)S(1)}, bf16[576,128]{1,0:T(8,128)(2,1)S(1)}, u32[]{:S(2)}, u32[]{:S(2)}) collective-permute-start(bf16[576,128]{1,0:T(8,128)(2,1)S(1)} %collective-permute-done.refs_1_), channel_id=1, source_target_pairs={{0,8},{8,0},{1,9},{9,1},{2,10},{10,2},{3,11},{11,3},{4,12},{12,4},... | collective-permute-start | bytes 442376 | tf_op jit(solution)/shard_map/ppermute | solution.py:29
  22.1 14.8 %collective-permute-start.23 = (bf16[288,512]{1,0:T(8,128)(2,1)S(1)}, bf16[288,512]{1,0:T(8,128)(2,1)S(1)}, u32[]{:S(2)}, u32[]{:S(2)}) collective-permute-start(bf16[288,512]{1,0:T(8,128)(2,1)S(1)} %get-tuple-element.40.refs_0_), channel_id=1, source_target_pairs={{0,16},{16,0},{1,17},{17,1},{2,18},{18,2},{3,19},{19,3},{4,20},{20... | collective-permute-start | bytes 884744 | tf_op jit(solution)/shard_map/ppermute | solution.py:29
  23.4 16.6 %collective-permute-start.17 = (bf16[288,512]{1,0:T(8,128)(2,1)S(1)}, bf16[288,512]{1,0:T(8,128)(2,1)S(1)}, u32[]{:S(2)}, u32[]{:S(2)}) collective-permute-start(bf16[288,512]{1,0:T(8,128)(2,1)S(1)} %get-tuple-element.40.refs_0_), channel_id=1, source_target_pairs={{0,64},{32,96},{64,0},{96,32},{1,65},{33,97},{65,1},{97,33},{2,66}... | collective-permute-start | bytes 884744 | tf_op jit(solution)/shard_map/ppermute | solution.py:29
  26.9 25.3 %collective-permute-start.11 = (bf16[576,256]{1,0:T(8,128)(2,1)S(1)}, bf16[576,256]{1,0:T(8,128)(2,1)S(1)}, u32[]{:S(2)}, u32[]{:S(2)}) collective-permute-start(bf16[576,256]{1,0:T(8,128)(2,1)S(1)} %get-tuple-element.35.mine), channel_id=1, source_target_pairs={{0,1},{1,0},{2,3},{3,2},{4,5},{5,4},{6,7},{7,6},{8,9},{9,8},{10,11... | collective-permute-start | bytes 884744 | tf_op jit(solution)/shard_map/ppermute | solution.py:29
  29.6 22.6 %collective-permute-start.12 = (bf16[576,256]{1,0:T(8,128)(2,1)S(1)}, bf16[576,256]{1,0:T(8,128)(2,1)S(1)}, u32[]{:S(2)}, u32[]{:S(2)}) collective-permute-start(bf16[576,256]{1,0:T(8,128)(2,1)S(1)} %get-tuple-element.36), channel_id=1, source_target_pairs={{0,17},{1,16},{16,1},{17,0},{2,19},{3,18},{18,3},{19,2},{4,21},{5,... | collective-permute-start | bytes 884744 | tf_op jit(solution)/shard_map/ppermute | solution.py:383
  29.6 23.4 %collective-permute-start.16 = (bf16[288,512]{1,0:T(8,128)(2,1)S(1)}, bf16[288,512]{1,0:T(8,128)(2,1)}, u32[]{:S(2)}, u32[]{:S(2)}) collective-permute-start(bf16[288,512]{1,0:T(8,128)(2,1)S(1)} %get-tuple-element.40.refs_0_), channel_id=1, source_target_pairs={{0,32},{32,64},{64,96},{96,0},{1,33},{33,65},{65,97},{97,1},{2,34}... | collective-permute-start | bytes 884744 | tf_op jit(solution)/shard_map/ppermute | solution.py:29
  36.9 18.9 %collective-permute-start.18 = (bf16[288,512]{1,0:T(8,128)(2,1)S(1)}, bf16[288,512]{1,0:T(8,128)(2,1)}, u32[]{:S(2)}, u32[]{:S(2)}) collective-permute-start(bf16[288,512]{1,0:T(8,128)(2,1)S(1)} %get-tuple-element.40.refs_0_), channel_id=1, source_target_pairs={{0,96},{32,0},{64,32},{96,64},{1,97},{33,1},{65,33},{97,65},{2,98}... | collective-permute-start | bytes 884744 | tf_op jit(solution)/shard_map/ppermute | solution.py:29
  40.0 17.3 %collective-permute-start.19 = (bf16[288,512]{1,0:T(8,128)(2,1)S(1)}, bf16[288,512]{1,0:T(8,128)(2,1)S(1)}, u32[]{:S(2)}, u32[]{:S(2)}) collective-permute-start(bf16[288,512]{1,0:T(8,128)(2,1)S(1)} %get-tuple-element.40.refs_0_), channel_id=1, source_target_pairs={{0,8},{8,0},{1,9},{9,1},{2,10},{10,2},{3,11},{11,3},{4,12},{12,4},... | collective-permute-start | bytes 884744 | tf_op jit(solution)/shard_map/ppermute | solution.py:29
  52.2 12.8 %collective-permute-start.24 = (bf16[288,512]{1,0:T(8,128)(2,1)S(1)}, bf16[288,512]{1,0:T(8,128)(2,1)}, u32[]{:S(2)}, u32[]{:S(2)}) collective-permute-start(bf16[288,512]{1,0:T(8,128)(2,1)S(1)} %collective-permute-done.23.refs_8_), channel_id=1, source_target_pairs={{0,32},{32,64},{64,96},{96,0},{1,33},{33,65},{65,97},{97,1},{2,34}... | collective-permute-start | bytes 884744 | tf_op jit(solution)/shard_map/ppermute | solution.py:29
  52.2 15.0 %collective-permute-start.7 = (bf16[576,256]{1,0:T(8,128)(2,1)S(1)}, bf16[576,256]{1,0:T(8,128)(2,1)S(1)}, u32[]{:S(2)}, u32[]{:S(2)}) collective-permute-start(bf16[576,256]{1,0:T(8,128)(2,1)S(1)} %get-tuple-element.36), channel_id=1, source_target_pairs={{0,16},{16,0},{1,17},{17,1},{2,18},{18,2},{3,19},{19,3},{4,20},{20... | collective-permute-start | bytes 884744 | tf_op jit(solution)/shard_map/ppermute | solution.py:29
  53.1 16.8 %collective-permute-start.26 = (bf16[288,512]{1,0:T(8,128)(2,1)S(1)}, bf16[288,512]{1,0:T(8,128)(2,1)}, u32[]{:S(2)}, u32[]{:S(2)}) collective-permute-start(bf16[288,512]{1,0:T(8,128)(2,1)S(1)} %collective-permute-done.23.refs_8_), channel_id=1, source_target_pairs={{0,96},{32,0},{64,32},{96,64},{1,97},{33,1},{65,33},{97,65},{2,98}... | collective-permute-start | bytes 884744 | tf_op jit(solution)/shard_map/ppermute | solution.py:29
  55.8 24.1 %collective-permute-start.25 = (bf16[288,512]{1,0:T(8,128)(2,1)S(1)}, bf16[288,512]{1,0:T(8,128)(2,1)}, u32[]{:S(2)}, u32[]{:S(2)}) collective-permute-start(bf16[288,512]{1,0:T(8,128)(2,1)S(1)} %collective-permute-done.17.refs_2_), channel_id=1, source_target_pairs={{0,16},{16,0},{1,17},{17,1},{2,18},{18,2},{3,19},{19,3},{4,20},{20... | collective-permute-start | bytes 884744 | tf_op jit(solution)/shard_map/ppermute | solution.py:29
  57.3 26.6 %collective-permute-start.27 = (bf16[288,512]{1,0:T(8,128)(2,1)S(1)}, bf16[288,512]{1,0:T(8,128)(2,1)S(1)}, u32[]{:S(2)}, u32[]{:S(2)}) collective-permute-start(bf16[288,512]{1,0:T(8,128)(2,1)S(1)} %collective-permute-done.23.refs_8_), channel_id=1, source_target_pairs={{0,8},{8,0},{1,9},{9,1},{2,10},{10,2},{3,11},{11,3},{4,12},{12,4},... | collective-permute-start | bytes 884744 | tf_op jit(solution)/shard_map/ppermute | solution.py:29
  65.0 19.0 %collective-permute-start.21 = (bf16[288,512]{1,0:T(8,128)(2,1)S(1)}, bf16[288,512]{1,0:T(8,128)(2,1)S(1)}, u32[]{:S(2)}, u32[]{:S(2)}) collective-permute-start(bf16[288,512]{1,0:T(8,128)(2,1)S(1)} %collective-permute-done.17.refs_2_), channel_id=1, source_target_pairs={{0,8},{8,0},{1,9},{9,1},{2,10},{10,2},{3,11},{11,3},{4,12},{12,4},... | collective-permute-start | bytes 884744 | tf_op jit(solution)/shard_map/ppermute | solution.py:29
  67.3 18.1 %collective-permute-start.13 = (bf16[576,256]{1,0:T(8,128)(2,1)S(1)}, bf16[576,256]{1,0:T(8,128)(2,1)S(1)}, u32[]{:S(2)}, u32[]{:S(2)}) collective-permute-start(bf16[576,256]{1,0:T(8,128)(2,1)S(1)} %shard_map.102.refs_4_), channel_id=1, source_target_pairs={{0,2},{2,4},{4,6},{6,0},{1,3},{3,5},{5,7},{7,1},{8,10},{10,12},{12... | collective-permute-start | bytes 884744 | tf_op jit(solution)/shard_map/ppermute | solution.py:29
  69.9 16.2 %collective-permute-start.14 = (bf16[576,256]{1,0:T(8,128)(2,1)S(1)}, bf16[576,256]{1,0:T(8,128)(2,1)S(1)}, u32[]{:S(2)}, u32[]{:S(2)}) collective-permute-start(bf16[576,256]{1,0:T(8,128)(2,1)S(1)} %shard_map.102.refs_4_), channel_id=1, source_target_pairs={{0,4},{2,6},{4,0},{6,2},{1,5},{3,7},{5,1},{7,3},{8,12},{10,14},{12... | collective-permute-start | bytes 884744 | tf_op jit(solution)/shard_map/ppermute | solution.py:29
  79.9 9.1 %collective-permute-start.15 = (bf16[576,256]{1,0:T(8,128)(2,1)S(1)}, bf16[576,256]{1,0:T(8,128)(2,1)S(1)}, u32[]{:S(2)}, u32[]{:S(2)}) collective-permute-start(bf16[576,256]{1,0:T(8,128)(2,1)S(1)} %shard_map.102.refs_4_), channel_id=1, source_target_pairs={{0,6},{2,0},{4,2},{6,4},{1,7},{3,1},{5,3},{7,5},{8,14},{10,8},{12,... | collective-permute-start | bytes 884744 | tf_op jit(solution)/shard_map/ppermute | solution.py:29
  83.9 12.4 %collective-permute-start.10 = (bf16[576,256]{1,0:T(8,128)(2,1)S(1)}, bf16[576,256]{1,0:T(8,128)(2,1)S(1)}, u32[]{:S(2)}, u32[]{:S(2)}) collective-permute-start(bf16[576,256]{1,0:T(8,128)(2,1)S(1)} %shard_map.101.refs_0_), channel_id=1, source_target_pairs={{0,6},{2,0},{4,2},{6,4},{1,7},{3,1},{5,3},{7,5},{8,14},{10,8},{12,... | collective-permute-start | bytes 884744 | tf_op jit(solution)/shard_map/ppermute | solution.py:29
  84.0 19.7 %collective-permute-start.8 = (bf16[576,256]{1,0:T(8,128)(2,1)S(1)}, bf16[576,256]{1,0:T(8,128)(2,1)S(1)}, u32[]{:S(2)}, u32[]{:S(2)}) collective-permute-start(bf16[576,256]{1,0:T(8,128)(2,1)S(1)} %shard_map.101.refs_0_), channel_id=1, source_target_pairs={{0,2},{2,4},{4,6},{6,0},{1,3},{3,5},{5,7},{7,1},{8,10},{10,12},{12... | collective-permute-start | bytes 884744 | tf_op jit(solution)/shard_map/ppermute | solution.py:29
  86.1 17.7 %collective-permute-start.9 = (bf16[576,256]{1,0:T(8,128)(2,1)S(1)}, bf16[576,256]{1,0:T(8,128)(2,1)S(1)}, u32[]{:S(2)}, u32[]{:S(2)}) collective-permute-start(bf16[576,256]{1,0:T(8,128)(2,1)S(1)} %shard_map.101.refs_0_), channel_id=1, source_target_pairs={{0,4},{2,6},{4,0},{6,2},{1,5},{3,7},{5,1},{7,3},{8,12},{10,14},{12... | collective-permute-start | bytes 884744 | tf_op jit(solution)/shard_map/ppermute | solution.py:29
  86.1 21.0 %collective-permute-start.20 = (bf16[288,512]{1,0:T(8,128)(2,1)}, bf16[288,512]{1,0:T(8,128)(2,1)S(1)}, u32[]{:S(2)}, u32[]{:S(2)}) collective-permute-start(bf16[288,512]{1,0:T(8,128)(2,1)} %collective-permute-done.16.refs_1_), channel_id=1, source_target_pairs={{0,8},{8,0},{1,9},{9,1},{2,10},{10,2},{3,11},{11,3},{4,12},{12,4},... | collective-permute-start | bytes 884744 | tf_op jit(solution)/shard_map/ppermute | solution.py:29
  89.0 18.2 %collective-permute-start.22 = (bf16[288,512]{1,0:T(8,128)(2,1)}, bf16[288,512]{1,0:T(8,128)(2,1)S(1)}, u32[]{:S(2)}, u32[]{:S(2)}) collective-permute-start(bf16[288,512]{1,0:T(8,128)(2,1)} %collective-permute-done.18.refs_3_), channel_id=1, source_target_pairs={{0,8},{8,0},{1,9},{9,1},{2,10},{10,2},{3,11},{11,3},{4,12},{12,4},... | collective-permute-start | bytes 884744 | tf_op jit(solution)/shard_map/ppermute | solution.py:29
  96.3 10.9 %collective-permute-start.28 = (bf16[288,512]{1,0:T(8,128)(2,1)}, bf16[288,512]{1,0:T(8,128)(2,1)S(1)}, u32[]{:S(2)}, u32[]{:S(2)}) collective-permute-start(bf16[288,512]{1,0:T(8,128)(2,1)} %collective-permute-done.24.refs_9_), channel_id=1, source_target_pairs={{0,8},{8,0},{1,9},{9,1},{2,10},{10,2},{3,11},{11,3},{4,12},{12,4},... | collective-permute-start | bytes 884744 | tf_op jit(solution)/shard_map/ppermute | solution.py:29
  114.3 9.0 %collective-permute-start.32 = (bf16[256,512]{1,0:T(8,128)(2,1)S(1)}, bf16[256,512]{1,0:T(8,128)(2,1)S(1)}, u32[]{:S(2)}, u32[]{:S(2)}) collective-permute-start(bf16[256,512]{1,0:T(8,128)(2,1)S(1)} %key_value.1.refs_0_), channel_id=1, source_target_pairs={{0,64},{32,96},{64,0},{96,32},{1,65},{33,97},{65,1},{97,33},{2,66}... | collective-permute-start | bytes 786440 | tf_op jit(solution)/shard_map/ppermute | solution.py:29
  114.4 14.9 %collective-permute-start.31 = (bf16[256,512]{1,0:T(8,128)(2,1)S(1)}, bf16[256,512]{1,0:T(8,128)(2,1)S(1)}, u32[]{:S(2)}, u32[]{:S(2)}) collective-permute-start(bf16[256,512]{1,0:T(8,128)(2,1)S(1)} %key_value.1.refs_0_), channel_id=1, source_target_pairs={{0,32},{32,64},{64,96},{96,0},{1,33},{33,65},{65,97},{97,1},{2,34}... | collective-permute-start | bytes 786440 | tf_op jit(solution)/shard_map/ppermute | solution.py:29
  117.6 11.8 %collective-permute-start.33 = (bf16[256,512]{1,0:T(8,128)(2,1)S(1)}, bf16[256,512]{1,0:T(8,128)(2,1)}, u32[]{:S(2)}, u32[]{:S(2)}) collective-permute-start(bf16[256,512]{1,0:T(8,128)(2,1)S(1)} %key_value.1.refs_0_), channel_id=1, source_target_pairs={{0,96},{32,0},{64,32},{96,64},{1,97},{33,1},{65,33},{97,65},{2,98}... | collective-permute-start | bytes 786440 | tf_op jit(solution)/shard_map/ppermute | solution.py:29
  117.6 15.0 %collective-permute-start.34 = (bf16[256,512]{1,0:T(8,128)(2,1)S(1)}, bf16[256,512]{1,0:T(8,128)(2,1)S(1)}, u32[]{:S(2)}, u32[]{:S(2)}) collective-permute-start(bf16[256,512]{1,0:T(8,128)(2,1)S(1)} %key_value.1.refs_0_), channel_id=1, source_target_pairs={{0,8},{8,0},{1,9},{9,1},{2,10},{10,2},{3,11},{11,3},{4,12},{12,4},... | collective-permute-start | bytes 786440 | tf_op jit(solution)/shard_map/ppermute | solution.py:29
  121.9 13.1 %collective-permute-start.39 = (bf16[256,512]{1,0:T(8,128)(2,1)S(1)}, bf16[256,512]{1,0:T(8,128)(2,1)}, u32[]{:S(2)}, u32[]{:S(2)}) collective-permute-start(bf16[256,512]{1,0:T(8,128)(2,1)S(1)} %collective-permute-done.38.refs_8_), channel_id=1, source_target_pairs={{0,32},{32,64},{64,96},{96,0},{1,33},{33,65},{65,97},{97,1},{2,34}... | collective-permute-start | bytes 786440 | tf_op jit(solution)/shard_map/ppermute | solution.py:29
  123.3 12.4 %collective-permute-start.40 = (bf16[256,512]{1,0:T(8,128)(2,1)S(1)}, bf16[256,512]{1,0:T(8,128)(2,1)}, u32[]{:S(2)}, u32[]{:S(2)}) collective-permute-start(bf16[256,512]{1,0:T(8,128)(2,1)S(1)} %collective-permute-done.32.refs_2_), channel_id=1, source_target_pairs={{0,16},{16,0},{1,17},{17,1},{2,18},{18,2},{3,19},{19,3},{4,20},{20... | collective-permute-start | bytes 786440 | tf_op jit(solution)/shard_map/ppermute | solution.py:29
  129.3 8.8 %collective-permute-start.35 = (bf16[256,512]{1,0:T(8,128)(2,1)S(1)}, bf16[256,512]{1,0:T(8,128)(2,1)S(1)}, u32[]{:S(2)}, u32[]{:S(2)}) collective-permute-start(bf16[256,512]{1,0:T(8,128)(2,1)S(1)} %collective-permute-done.31.refs_1_), channel_id=1, source_target_pairs={{0,8},{8,0},{1,9},{9,1},{2,10},{10,2},{3,11},{11,3},{4,12},{12,4},... | collective-permute-start | bytes 786440 | tf_op jit(solution)/shard_map/ppermute | solution.py:29
  135.0 8.6 %collective-permute-start.42 = (bf16[256,512]{1,0:T(8,128)(2,1)S(1)}, bf16[256,512]{1,0:T(8,128)(2,1)}, u32[]{:S(2)}, u32[]{:S(2)}) collective-permute-start(bf16[256,512]{1,0:T(8,128)(2,1)S(1)} %collective-permute-done.38.refs_8_), channel_id=1, source_target_pairs={{0,8},{8,0},{1,9},{9,1},{2,10},{10,2},{3,11},{11,3},{4,12},{12,4},... | collective-permute-start | bytes 786440 | tf_op jit(solution)/shard_map/ppermute | solution.py:29
  135.8 7.9 %collective-permute-start.37 = (bf16[256,512]{1,0:T(8,128)(2,1)}, bf16[256,512]{1,0:T(8,128)(2,1)}, u32[]{:S(2)}, u32[]{:S(2)}) collective-permute-start(bf16[256,512]{1,0:T(8,128)(2,1)} %collective-permute-done.33.refs_3_), channel_id=1, source_target_pairs={{0,8},{8,0},{1,9},{9,1},{2,10},{10,2},{3,11},{11,3},{4,12},{12,4},... | collective-permute-start | bytes 786440 | tf_op jit(solution)/shard_map/ppermute | solution.py:29
  155.0 10.9 %collective-permute-start.46 = (bf16[32,4608]{1,0:T(8,128)(2,1)S(1)}, bf16[32,4608]{1,0:T(8,128)(2,1)S(1)}, u32[]{:S(2)}, u32[]{:S(2)}) collective-permute-start(bf16[32,4608]{1,0:T(8,128)(2,1)S(1)} %get-tuple-element.42), channel_id=1, source_target_pairs={{0,2},{2,4},{4,6},{6,0},{1,3},{3,5},{5,7},{7,1},{8,10},{10,12},{12... | collective-permute-start | bytes 884744 | tf_op jit(solution)/shard_map/ppermute | solution.py:29
  156.0 29.7 %collective-permute-start.47 = (bf16[32,4608]{1,0:T(8,128)(2,1)S(1)}, bf16[32,4608]{1,0:T(8,128)(2,1)S(1)}, u32[]{:S(2)}, u32[]{:S(2)}) collective-permute-start(bf16[32,4608]{1,0:T(8,128)(2,1)S(1)} %get-tuple-element.43), channel_id=1, source_target_pairs={{0,4},{2,6},{4,0},{6,2},{1,5},{3,7},{5,1},{7,3},{8,12},{10,14},{12... | collective-permute-start | bytes 884744 | tf_op jit(solution)/shard_map/ppermute | solution.py:29
  159.7 26.1 %collective-permute-start.48 = (bf16[32,4608]{1,0:T(8,128)(2,1)S(1)}, bf16[32,4608]{1,0:T(8,128)(2,1)S(1)}, u32[]{:S(2)}, u32[]{:S(2)}) collective-permute-start(bf16[32,4608]{1,0:T(8,128)(2,1)S(1)} %get-tuple-element.44), channel_id=1, source_target_pairs={{0,6},{2,0},{4,2},{6,4},{1,7},{3,1},{5,3},{7,5},{8,14},{10,8},{12,... | collective-permute-start | bytes 884744 | tf_op jit(solution)/shard_map/ppermute | solution.py:29
  159.7 26.1 %collective-permute-start.49 = (bf16[32,4608]{1,0:T(8,128)(2,1)S(1)}, bf16[32,4608]{1,0:T(8,128)(2,1)S(1)}, u32[]{:S(2)}, u32[]{:S(2)}) collective-permute-start(bf16[32,4608]{1,0:T(8,128)(2,1)S(1)} %get-tuple-element.45), channel_id=1, source_target_pairs={{0,1},{1,0},{2,3},{3,2},{4,5},{5,4},{6,7},{7,6},{8,9},{9,8},{10,11... | collective-permute-start | bytes 884744 | tf_op jit(solution)/shard_map/ppermute | solution.py:29
  160.6 25.2 %collective-permute-start.50 = (bf16[32,4608]{1,0:T(8,128)(2,1)S(1)}, bf16[32,4608]{1,0:T(8,128)(2,1)S(1)}, u32[]{:S(2)}, u32[]{:S(2)}) collective-permute-start(bf16[32,4608]{1,0:T(8,128)(2,1)S(1)} %get-tuple-element.46), channel_id=1, source_target_pairs={{0,3},{1,2},{2,5},{3,4},{4,7},{5,6},{6,1},{7,0},{8,11},{9,10},{10,... | collective-permute-start | bytes 884744 | tf_op jit(solution)/shard_map/ppermute | solution.py:472
  165.9 19.9 %collective-permute-start.51 = (bf16[32,4608]{1,0:T(8,128)(2,1)S(1)}, bf16[32,4608]{1,0:T(8,128)(2,1)S(1)}, u32[]{:S(2)}, u32[]{:S(2)}) collective-permute-start(bf16[32,4608]{1,0:T(8,128)(2,1)S(1)} %get-tuple-element.47), channel_id=1, source_target_pairs={{0,5},{1,4},{2,7},{3,6},{4,1},{5,0},{6,3},{7,2},{8,13},{9,12},{10,... | collective-permute-start | bytes 884744 | tf_op jit(solution)/shard_map/ppermute | solution.py:472
  185.8 10.1 %collective-permute-start.52 = (bf16[32,4608]{1,0:T(8,128)(2,1)S(1)}, bf16[32,4608]{1,0:T(8,128)(2,1)S(1)}, u32[]{:S(2)}, u32[]{:S(2)}) collective-permute-start(bf16[32,4608]{1,0:T(8,128)(2,1)S(1)} %get-tuple-element.48), channel_id=1, source_target_pairs={{0,7},{1,6},{2,1},{3,0},{4,3},{5,2},{6,5},{7,4},{8,15},{9,14},{10,... | collective-permute-start | bytes 884744 | tf_op jit(solution)/shard_map/ppermute | solution.py:472
  197.7 8.2 %collective-permute-start.53 = (bf16[32,4608]{1,0:T(8,128)(2,1)S(1)}, bf16[32,4608]{1,0:T(8,128)(2,1)S(1)}, u32[]{:S(2)}, u32[]{:S(2)}) collective-permute-start(bf16[32,4608]{1,0:T(8,128)(2,1)S(1)} %finish.1.refs_0_), channel_id=1, source_target_pairs={{0,8},{8,0},{1,9},{9,1},{2,10},{10,2},{3,11},{11,3},{4,12},{12,4},... | collective-permute-start | bytes 884744 | tf_op jit(solution)/shard_map/ppermute | solution.py:29
  208.1 9.2 %collective-permute-start.57 = (bf16[16,4608]{1,0:T(8,128)(2,1)S(1)}, bf16[16,4608]{1,0:T(8,128)(2,1)S(1)}, u32[]{:S(2)}, u32[]{:S(2)}) collective-permute-start(bf16[16,4608]{1,0:T(8,128)(2,1)S(1)} %get-tuple-element.51), channel_id=1, source_target_pairs={{0,64},{32,96},{64,0},{96,32},{1,65},{33,97},{65,1},{97,33},{2,66}... | collective-permute-start | bytes 442376 | tf_op jit(solution)/shard_map/ppermute | solution.py:29
  218.6 9.2 %collective-permute-start.59 = (bf16[16,4608]{1,0:T(8,128)(2,1)S(1)}, bf16[16,4608]{1,0:T(8,128)(2,1)S(1)}, u32[]{:S(2)}, u32[]{:S(2)}) collective-permute-start(bf16[16,4608]{1,0:T(8,128)(2,1)S(1)} %get-tuple-element.54), channel_id=1, source_target_pairs={{0,2},{2,4},{4,6},{6,0},{1,3},{3,5},{5,7},{7,1},{8,10},{10,12},{12... | collective-permute-start | bytes 442376 | tf_op jit(solution)/shard_map/ppermute | solution.py:29
  218.7 9.1 %collective-permute-start.60 = (bf16[16,4608]{1,0:T(8,128)(2,1)S(1)}, bf16[16,4608]{1,0:T(8,128)(2,1)S(1)}, u32[]{:S(2)}, u32[]{:S(2)}) collective-permute-start(bf16[16,4608]{1,0:T(8,128)(2,1)S(1)} %get-tuple-element.55), channel_id=1, source_target_pairs={{0,4},{2,6},{4,0},{6,2},{1,5},{3,7},{5,1},{7,3},{8,12},{10,14},{12... | collective-permute-start | bytes 442376 | tf_op jit(solution)/shard_map/ppermute | solution.py:29
  219.6 8.2 %collective-permute-start.61 = (bf16[16,4608]{1,0:T(8,128)(2,1)S(1)}, bf16[16,4608]{1,0:T(8,128)(2,1)S(1)}, u32[]{:S(2)}, u32[]{:S(2)}) collective-permute-start(bf16[16,4608]{1,0:T(8,128)(2,1)S(1)} %get-tuple-element.56), channel_id=1, source_target_pairs={{0,6},{2,0},{4,2},{6,4},{1,7},{3,1},{5,3},{7,5},{8,14},{10,8},{12,... | collective-permute-start | bytes 442376 | tf_op jit(solution)/shard_map/ppermute | solution.py:29
  (37 other events, 445.7 us)
Sparse Core Ops, SparseCore 0:
  9.7 85.8 all-gather.1

commit v5 on v4

--- a/solution.py
+++ b/solution.py
@@ -199,7 +199,9 @@
 
 def attention_kernel(flat, query, *refs):
     kv = [refs[4 * k : 4 * k + 4] for k in range(4)]
-    context, numer, denom = refs[16:]
+    weight, context, ready, numer, denom, sems = refs[16:]
+    copy = pltpu.make_async_copy(weight.at[:, 4 * HEAD :], ready, sems.at[0])
+    copy.start()
     x, yl, c, _, _ = spot(flat)
     w = 2 * yl + c
     row = lax.broadcasted_iota(jnp.int32, (2 * BLOCK, BLOCK), 0) % BLOCK
@@ -244,27 +246,19 @@
             context[rows, pl.ds(first, HEAD)] = out[:BLOCK].astype(BF16)
             context[rows, pl.ds(first + HEAD, HEAD)] = out[BLOCK:].astype(BF16)
 
+    copy.wait()
+
 
 def out_kernel(flat, context, weight, *refs):
-    outs, (buffer, scratch, sems) = refs[:8], refs[8:]
+    outs, scratch = refs[:8], refs[8]
     _, _, _, z, yh = spot(flat)
-    tile, steps = scratch.shape[1], sems.shape[0]
-
-    def copy(n):
-        rows = pl.ds(pl.multiple_of(n * tile, tile), tile)
-        source = weight.at[rows, 4 * HEAD :]
-        return pltpu.make_async_copy(source, buffer.at[rows, :], sems.at[n])
-
-    @pl.loop(0, steps)
+    tile = scratch.shape[1]
+
+    @pl.loop(0, weight.shape[0] // tile)
     def _(n):
-        copy(n).start()
-
-    @pl.loop(0, steps)
-    def _(n):
-        copy(n).wait()
         cols = pl.ds(pl.multiple_of(n * tile, tile), tile)
         scratch[...] = lax.dot_general(
-            context[...], buffer[cols, :], (((1,), (1,)), ((), ())), preferred_element_type=F32
+            context[...], weight[cols, :], (((1,), (1,)), ((), ())), preferred_element_type=F32
         ).astype(BF16)
         for dy in range(2):
             for dz in range(4):
@@ -439,33 +433,33 @@
     spread = everywhere(kv)
 
     query = heads(query_kernel, 0)
-    context = pl.pallas_call(
+    context, out_weights = pl.pallas_call(
         attention_kernel,
-        in_specs=[SMEM] + [VMEM] * 17,
-        out_specs=VMEM,
-        out_shape=pltpu.VMEM((count, 4 * HEAD), BF16),
-        scratch_shapes=[pltpu.VMEM((2, 2 * BLOCK, HEAD), F32), pltpu.VMEM((2, 2 * BLOCK, HEAD), F32)],
+        in_specs=[SMEM] + [VMEM] * 17 + [AWAY],
+        out_specs=[VMEM] * 2,
+        out_shape=[pltpu.VMEM((count, 4 * HEAD), BF16), pltpu.VMEM((D, 4 * HEAD), BF16)],
+        scratch_shapes=[
+            pltpu.VMEM((2, 2 * BLOCK, HEAD), F32),
+            pltpu.VMEM((2, 2 * BLOCK, HEAD), F32),
+            pltpu.SemaphoreType.DMA((1,)),
+        ],
         compiler_params=grant(24),
         name="attention",
-    )(flat, *near_by((query, *spread)))
+    )(flat, *near_by((query, *spread)), *far_off((joined_full,)))
 
     tile = 512
     shares = pl.pallas_call(
         out_kernel,
-        in_specs=[SMEM, VMEM, AWAY],
+        in_specs=[SMEM, VMEM, VMEM],
         out_specs=[VMEM] * 8,
         out_shape=[pltpu.VMEM((32, D), BF16)] * 8,
-        scratch_shapes=[
-            pltpu.VMEM((D, 4 * HEAD), BF16),
-            pltpu.VMEM((count, tile), BF16),
-            pltpu.SemaphoreType.DMA((D // tile,)),
-        ],
+        scratch_shapes=[pltpu.VMEM((count, tile), BF16)],
         compiler_params=grant(16),
         name="project",
-    )(flat, *near_by((context,)), *far_off((joined_full,)))
+    )(flat, *near_by((context, out_weights)))
     received = []
-    for dy in range(2):
-        for dz in range(4):
+    for dy in (1, 0):
+        for dz in (2, 1, 3, 0):
             part = shares[4 * dy + dz]
             if dy and dz:
                 n = [(i, j) for i in range(4) for j in range(2)]

time: 238 us -> 232 us (0.975)
  waiting for transfers between devices: 97 us -> 94.1 us
    ppermute x58, waiting for transfers between devices: 86.9 us -> 77 us  [shift(): return lax.ppermute(value, axis, [(i, (i + by) % n) for i in range(n)])]
    ppermute x3, waiting for transfers between devices: 10 us -> 17 us  [per_device(): lax.ppermute(part, TP, [(2 * i + j, 2 * ((i + dz) % 4) + (j ^ dy)) for i,...]
    ppermute x58, starting transfers between devices: 83.5 us -> 79.7 us  [shift(): return lax.ppermute(value, axis, [(i, (i + by) % n) for i in range(n)])]
    ppermute x3, starting transfers between devices: 4.03 us -> 6.47 us  [per_device(): lax.ppermute(part, TP, [(2 * i + j, 2 * ((i + dz) % 4) + (j ^ dy)) for i,...]
  transfers between devices with their start and end apart: 63 -> 63, of which waited for: 22 -> 25; matrix products, arithmetic and copies ran while one was open for 0% -> 0% of each run, Pallas kernels for 4% -> 5%
where the time goes in v5:
time: 232 us; the launch traced here: 231 us
  waiting for transfers between devices  94.1 us (41%)
  starting transfers between devices  86.1 us (37%)
  Pallas kernels  26.6 us (11%)
  between operations  13.9 us (6%)
  local copies, waits for them, and re-layouts  9.27 us (4%)
    ppermute x58, starting transfers between devices, shift(): return lax.ppermute(value, axis, [(i, (i + by) % n) for i in range(n)])  79.7 us
    ppermute x58, waiting for transfers between devices, shift(): return lax.ppermute(value, axis, [(i, (i + by) % n) for i in range(n)])  77 us
    ppermute x3, waiting for transfers between devices, per_device(): lax.ppermute(part, TP, [(2 * i + j, 2 * ((i + dz) % 4) + (j ^ dy)) for i,...  17 us
    unnamed x45, local copies, waits for them, and re-layouts  9.24 us
    pallas_call x1, Pallas kernels, per_device(): pl.pallas_call(attention_kernel, in_specs=[SMEM] + [VMEM] * 17 + [AWAY],...  7.02 us
    pallas_call x7, Pallas kernels, call(): pl.pallas_call(kernel, in_specs=[SMEM] * (1 + len(tables)) + [VMEM] * len...  6.81 us
    ppermute x3, starting transfers between devices, per_device(): lax.ppermute(part, TP, [(2 * i + j, 2 * ((i + dz) % 4) + (j ^ dy)) for i,...  6.47 us
  transfers between devices with their start and end apart: 63, of which 25 were waited for; matrix products, arithmetic and copies ran while one was open for 0% of the time, Pallas kernels for 5%

profile of v5, /device:TPU:1, one launch (start us, length us, event | category | flops | bytes accessed | tf_op | source)
XLA Modules:
  0.0 230.7 jit_solution(13095651137681244560)
XLA Ops:
  6.5 3.0 %leave.1 = (bf16[288,1024]{1,0:T(8,128)(2,1)}, bf16[288,512]{1,0:T(8,128)(2,1)S(1)}, bf16[576,128]{1,0:T(8,128)(2,1)S(1)}, bf16[576,128]{1,0:T(8,128)(2,1)S(1)},...) custom-call(s32[1]{0:T(128)} %bitcast.flat, s32[16]{0:T(128)} %old_blocks.7, s32[16]{0:T(128)} %order.7, ...), custom_call_target="tpu_custom_call" | custom-call | tf_op jit(solution)/shard_map/leave/pallas_call | solution.py:354
  9.6 2.1 collective-permute-start
  11.7 2.5 %collective-permute-start.1 = (bf16[576,128]{1,0:T(8,128)(2,1)S(1)}, bf16[576,128]{1,0:T(8,128)(2,1)S(1)}, u32[]{:S(2)}, u32[]{:S(2)}) collective-permute-start(bf16[576,128]{1,0:T(8,128)(2,1)S(1)} %get-tuple-element.35), channel_id=1, source_target_pairs={{0,64},{32,96},{64,0},{96,32},{1,65},{33,97},{65,1},{97,33},{2,66}... | collective-permute-start | bytes 442376 | tf_op jit(solution)/shard_map/ppermute | solution.py:29
  17.8 2.8 %collective-permute-done.1.refs_2_ = bf16[576,128]{1,0:T(8,128)(2,1)S(1)} collective-permute-done((bf16[576,128]{1,0:T(8,128)(2,1)S(1)}, bf16[576,128]{1,0:T(8,128)(2,1)S(1)}, u32[]{:S(2)}, u32[]{:S(2)}) %collective-permute-start.1) | collective-permute-done | bytes 147488 | tf_op jit(solution)/shard_map/ppermute | solution.py:29
  20.6 1.5 collective-permute-start.5
  23.4 2.4 %collective-permute-start.17 = (bf16[288,512]{1,0:T(8,128)(2,1)S(1)}, bf16[288,512]{1,0:T(8,128)(2,1)S(1)}, u32[]{:S(2)}, u32[]{:S(2)}) collective-permute-start(bf16[288,512]{1,0:T(8,128)(2,1)S(1)} %get-tuple-element.42.refs_0_), channel_id=1, source_target_pairs={{0,64},{32,96},{64,0},{96,32},{1,65},{33,97},{65,1},{97,33},{2,66}... | collective-permute-start | bytes 884744 | tf_op jit(solution)/shard_map/ppermute | solution.py:29
  26.9 2.7 %collective-permute-start.11 = (bf16[576,256]{1,0:T(8,128)(2,1)S(1)}, bf16[576,256]{1,0:T(8,128)(2,1)S(1)}, u32[]{:S(2)}, u32[]{:S(2)}) collective-permute-start(bf16[576,256]{1,0:T(8,128)(2,1)S(1)} %get-tuple-element.37.mine), channel_id=1, source_target_pairs={{0,1},{1,0},{2,3},{3,2},{4,5},{5,4},{6,7},{7,6},{8,9},{9,8},{10,11... | collective-permute-start | bytes 884744 | tf_op jit(solution)/shard_map/ppermute | solution.py:29
  29.8 7.1 %collective-permute-done.23.refs_8_ = bf16[288,512]{1,0:T(8,128)(2,1)S(1)} collective-permute-done((bf16[288,512]{1,0:T(8,128)(2,1)S(1)}, bf16[288,512]{1,0:T(8,128)(2,1)S(1)}, u32[]{:S(2)}, u32[]{:S(2)}) %collective-permute-start.23) | collective-permute-done | bytes 294944 | tf_op jit(solution)/shard_map/ppermute | solution.py:29
  36.9 2.2 collective-permute-start.18
  40.0 1.9 collective-permute-start.19
  41.9 10.3 %collective-permute-done.11.mine = bf16[576,256]{1,0:T(8,128)(2,1)S(1)} collective-permute-done((bf16[576,256]{1,0:T(8,128)(2,1)S(1)}, bf16[576,256]{1,0:T(8,128)(2,1)S(1)}, u32[]{:S(2)}, u32[]{:S(2)}) %collective-permute-start.11) | collective-permute-done | bytes 294944 | tf_op jit(solution)/shard_map/ppermute | solution.py:29
  53.1 2.7 %collective-permute-start.26 = (bf16[288,512]{1,0:T(8,128)(2,1)S(1)}, bf16[288,512]{1,0:T(8,128)(2,1)}, u32[]{:S(2)}, u32[]{:S(2)}) collective-permute-start(bf16[288,512]{1,0:T(8,128)(2,1)S(1)} %collective-permute-done.23.refs_8_), channel_id=1, source_target_pairs={{0,96},{32,0},{64,32},{96,64},{1,97},{33,1},{65,33},{97,65},{2,98}... | collective-permute-start | bytes 884744 | tf_op jit(solution)/shard_map/ppermute | solution.py:29
  57.3 2.5 %collective-permute-start.27 = (bf16[288,512]{1,0:T(8,128)(2,1)S(1)}, bf16[288,512]{1,0:T(8,128)(2,1)S(1)}, u32[]{:S(2)}, u32[]{:S(2)}) collective-permute-start(bf16[288,512]{1,0:T(8,128)(2,1)S(1)} %collective-permute-done.23.refs_8_), channel_id=1, source_target_pairs={{0,8},{8,0},{1,9},{9,1},{2,10},{10,2},{3,11},{11,3},{4,12},{12,4},... | collective-permute-start | bytes 884744 | tf_op jit(solution)/shard_map/ppermute | solution.py:29
  59.8 5.2 %collective-permute-done.24.refs_9_ = bf16[288,512]{1,0:T(8,128)(2,1)} collective-permute-done((bf16[288,512]{1,0:T(8,128)(2,1)S(1)}, bf16[288,512]{1,0:T(8,128)(2,1)}, u32[]{:S(2)}, u32[]{:S(2)}) %collective-permute-start.24) | collective-permute-done | bytes 294944 | tf_op jit(solution)/shard_map/ppermute | solution.py:29
  65.0 1.8 collective-permute-start.21
  67.3 1.8 collective-permute-start.13
  69.9 3.4 %collective-permute-start.14 = (bf16[576,256]{1,0:T(8,128)(2,1)S(1)}, bf16[576,256]{1,0:T(8,128)(2,1)S(1)}, u32[]{:S(2)}, u32[]{:S(2)}) collective-permute-start(bf16[576,256]{1,0:T(8,128)(2,1)S(1)} %shard_map.102.refs_4_), channel_id=1, source_target_pairs={{0,4},{2,6},{4,0},{6,2},{1,5},{3,7},{5,1},{7,3},{8,12},{10,14},{12... | collective-permute-start | bytes 884744 | tf_op jit(solution)/shard_map/ppermute | solution.py:29
  73.3 6.6 %collective-permute-done.25.refs_10_ = bf16[288,512]{1,0:T(8,128)(2,1)} collective-permute-done((bf16[288,512]{1,0:T(8,128)(2,1)S(1)}, bf16[288,512]{1,0:T(8,128)(2,1)}, u32[]{:S(2)}, u32[]{:S(2)}) %collective-permute-start.25) | collective-permute-done | bytes 294944 | tf_op jit(solution)/shard_map/ppermute | solution.py:29
  79.9 4.0 %collective-permute-start.15 = (bf16[576,256]{1,0:T(8,128)(2,1)S(1)}, bf16[576,256]{1,0:T(8,128)(2,1)S(1)}, u32[]{:S(2)}, u32[]{:S(2)}) collective-permute-start(bf16[576,256]{1,0:T(8,128)(2,1)S(1)} %shard_map.102.refs_4_), channel_id=1, source_target_pairs={{0,6},{2,0},{4,2},{6,4},{1,7},{3,1},{5,3},{7,5},{8,14},{10,8},{12,... | collective-permute-start | bytes 884744 | tf_op jit(solution)/shard_map/ppermute | solution.py:29
  86.1 2.9 %collective-permute-start.20 = (bf16[288,512]{1,0:T(8,128)(2,1)}, bf16[288,512]{1,0:T(8,128)(2,1)S(1)}, u32[]{:S(2)}, u32[]{:S(2)}) collective-permute-start(bf16[288,512]{1,0:T(8,128)(2,1)} %collective-permute-done.16.refs_1_), channel_id=1, source_target_pairs={{0,8},{8,0},{1,9},{9,1},{2,10},{10,2},{3,11},{11,3},{4,12},{12,4},... | collective-permute-start | bytes 884744 | tf_op jit(solution)/shard_map/ppermute | solution.py:29
  89.0 4.7 %collective-permute-start.22 = (bf16[288,512]{1,0:T(8,128)(2,1)}, bf16[288,512]{1,0:T(8,128)(2,1)S(1)}, u32[]{:S(2)}, u32[]{:S(2)}) collective-permute-start(bf16[288,512]{1,0:T(8,128)(2,1)} %collective-permute-done.18.refs_3_), channel_id=1, source_target_pairs={{0,8},{8,0},{1,9},{9,1},{2,10},{10,2},{3,11},{11,3},{4,12},{12,4},... | collective-permute-start | bytes 884744 | tf_op jit(solution)/shard_map/ppermute | solution.py:29
  93.7 2.6 %collective-permute-done.10.refs_3_ = bf16[576,256]{1,0:T(8,128)(2,1)S(1)} collective-permute-done((bf16[576,256]{1,0:T(8,128)(2,1)S(1)}, bf16[576,256]{1,0:T(8,128)(2,1)S(1)}, u32[]{:S(2)}, u32[]{:S(2)}) %collective-permute-start.10) | collective-permute-done | bytes 294944 | tf_op jit(solution)/shard_map/ppermute | solution.py:29
  96.3 7.4 %collective-permute-start.28 = (bf16[288,512]{1,0:T(8,128)(2,1)}, bf16[288,512]{1,0:T(8,128)(2,1)S(1)}, u32[]{:S(2)}, u32[]{:S(2)}) collective-permute-start(bf16[288,512]{1,0:T(8,128)(2,1)} %collective-permute-done.24.refs_9_), channel_id=1, source_target_pairs={{0,8},{8,0},{1,9},{9,1},{2,10},{10,2},{3,11},{11,3},{4,12},{12,4},... | collective-permute-start | bytes 884744 | tf_op jit(solution)/shard_map/ppermute | solution.py:29
  111.1 1.6 shard_map.104.weight
  114.4 3.1 %collective-permute-start.31 = (bf16[256,512]{1,0:T(8,128)(2,1)S(1)}, bf16[256,512]{1,0:T(8,128)(2,1)S(1)}, u32[]{:S(2)}, u32[]{:S(2)}) collective-permute-start(bf16[256,512]{1,0:T(8,128)(2,1)S(1)} %key_value.1.refs_0_), channel_id=1, source_target_pairs={{0,32},{32,64},{64,96},{96,0},{1,33},{33,65},{65,97},{97,1},{2,34}... | collective-permute-start | bytes 786440 | tf_op jit(solution)/shard_map/ppermute | solution.py:29
  118.6 3.3 %collective-permute-done.38.refs_8_ = bf16[256,512]{1,0:T(8,128)(2,1)S(1)} collective-permute-done((bf16[256,512]{1,0:T(8,128)(2,1)S(1)}, bf16[256,512]{1,0:T(8,128)(2,1)S(1)}, u32[]{:S(2)}, u32[]{:S(2)}) %collective-permute-start.38) | collective-permute-done | bytes 262176 | tf_op jit(solution)/shard_map/ppermute | solution.py:29
  124.7 4.6 %collective-permute-done.31.refs_1_ = bf16[256,512]{1,0:T(8,128)(2,1)S(1)} collective-permute-done((bf16[256,512]{1,0:T(8,128)(2,1)S(1)}, bf16[256,512]{1,0:T(8,128)(2,1)S(1)}, u32[]{:S(2)}, u32[]{:S(2)}) %collective-permute-start.31) | collective-permute-done | bytes 262176 | tf_op jit(solution)/shard_map/ppermute | solution.py:29
  129.3 2.5 %collective-permute-start.35 = (bf16[256,512]{1,0:T(8,128)(2,1)S(1)}, bf16[256,512]{1,0:T(8,128)(2,1)S(1)}, u32[]{:S(2)}, u32[]{:S(2)}) collective-permute-start(bf16[256,512]{1,0:T(8,128)(2,1)S(1)} %collective-permute-done.31.refs_1_), channel_id=1, source_target_pairs={{0,8},{8,0},{1,9},{9,1},{2,10},{10,2},{3,11},{11,3},{4,12},{12,4},... | collective-permute-start | bytes 786440 | tf_op jit(solution)/shard_map/ppermute | solution.py:29
  133.2 1.8 collective-permute-done.39.refs_9_
  136.3 1.9 collective-permute-start.43
  140.1 3.5 %shard_map.103.query = bf16[256,512]{1,0:T(8,128)(2,1)S(1)} custom-call(bf16[256,4608]{1,0:T(8,128)(2,1)S(1)} %get-tuple-element.40.normed, bf16[4608,1024]{1,0:T(8,128)(2,1)} %all-gather.2.cloned.1.call-done.weight.refs_16_, f32[256,128]{1,0:T(8,128)S(1)} %pad_maximum_fusion.cos, f32[256,128]{1,0:T(8,128)S(1)} %pad_maximum_fusion.1.sin), custom_call_target="tpu_custom_call" | custom-call | tf_op jit(solution)/shard_map/pallas_call | solution.py:414
  143.7 7.0 %attention.1 = (bf16[256,512]{1,0:T(8,128)(2,1)S(1)}, bf16[4608,512]{1,0:T(8,128)(2,1)S(1)}) custom-call(s32[1]{0:T(128)} %bitcast.flat, bf16[256,512]{1,0:T(8,128)(2,1)S(1)} %shard_map.103.query, bf16[256,512]{1,0:T(8,128)(2,1)S(1)} %key_value.1.refs_0_, bf16[256,512]{1,0:T(8,128)(2,1)S(1)} %copy-done.13, ...), custom_call_target="tpu_custom_call" | custom-call | tf_op jit(solution)/shard_map/attention/pallas_call | solution.py:436
  150.7 3.1 %project.1 = (bf16[32,4608]{1,0:T(8,128)(2,1)S(1)}, bf16[32,4608]{1,0:T(8,128)(2,1)S(1)}, bf16[32,4608]{1,0:T(8,128)(2,1)S(1)}, bf16[32,4608]{1,0:T(8,128)(2,1)S...) custom-call(s32[1]{0:T(128)} %bitcast.flat, ...), custom_call_target="tpu_custom_call" | custom-call | tf_op jit(solution)/shard_map/project/pallas_call | solution.py:451
  154.0 6.4 %collective-permute-start.47 = (bf16[32,4608]{1,0:T(8,128)(2,1)S(1)}, bf16[32,4608]{1,0:T(8,128)(2,1)S(1)}, u32[]{:S(2)}, u32[]{:S(2)}) collective-permute-start(bf16[32,4608]{1,0:T(8,128)(2,1)S(1)} %get-tuple-element.46), channel_id=1, source_target_pairs={{0,3},{1,2},{2,5},{3,4},{4,7},{5,6},{6,1},{7,0},{8,11},{9,10},{10,... | collective-permute-start | bytes 884744 | tf_op jit(solution)/shard_map/ppermute | solution.py:466
  161.2 2.3 collective-permute-start.50
  163.5 2.9 %collective-permute-done.46.refs_0_ = bf16[32,4608]{1,0:T(8,128)(2,1)S(1)} collective-permute-done((bf16[32,4608]{1,0:T(8,128)(2,1)S(1)}, bf16[32,4608]{1,0:T(8,128)(2,1)S(1)}, u32[]{:S(2)}, u32[]{:S(2)}) %collective-permute-start.46) | collective-permute-done | bytes 294944 | tf_op jit(solution)/shard_map/ppermute | solution.py:466
  167.4 5.7 %collective-permute-done.47.refs_1_ = bf16[32,4608]{1,0:T(8,128)(2,1)S(1)} collective-permute-done((bf16[32,4608]{1,0:T(8,128)(2,1)S(1)}, bf16[32,4608]{1,0:T(8,128)(2,1)S(1)}, u32[]{:S(2)}, u32[]{:S(2)}) %collective-permute-start.47) | collective-permute-done | bytes 294944 | tf_op jit(solution)/shard_map/ppermute | solution.py:466
  173.1 8.4 %collective-permute-done.48.refs_2_ = bf16[32,4608]{1,0:T(8,128)(2,1)S(1)} collective-permute-done((bf16[32,4608]{1,0:T(8,128)(2,1)S(1)}, bf16[32,4608]{1,0:T(8,128)(2,1)S(1)}, u32[]{:S(2)}, u32[]{:S(2)}) %collective-permute-start.48) | collective-permute-done | bytes 294944 | tf_op jit(solution)/shard_map/ppermute | solution.py:466
  181.5 1.6 collective-permute-done.49.refs_3_
  183.1 2.9 %collective-permute-done.51.refs_5_ = bf16[32,4608]{1,0:T(8,128)(2,1)S(1)} collective-permute-done((bf16[32,4608]{1,0:T(8,128)(2,1)S(1)}, bf16[32,4608]{1,0:T(8,128)(2,1)S(1)}, u32[]{:S(2)}, u32[]{:S(2)}) %collective-permute-start.51) | collective-permute-done | bytes 294944 | tf_op jit(solution)/shard_map/ppermute | solution.py:29
  186.0 4.2 %collective-permute-done.52.refs_6_ = bf16[32,4608]{1,0:T(8,128)(2,1)S(1)} collective-permute-done((bf16[32,4608]{1,0:T(8,128)(2,1)S(1)}, bf16[32,4608]{1,0:T(8,128)(2,1)S(1)}, u32[]{:S(2)}, u32[]{:S(2)}) %collective-permute-start.52) | collective-permute-done | bytes 294944 | tf_op jit(solution)/shard_map/ppermute | solution.py:29
  190.7 1.6 collective-permute-start.54
  193.1 5.9 %collective-permute-done.54.refs_2_ = bf16[32,4608]{1,0:T(8,128)(2,1)S(1)} collective-permute-done((bf16[32,4608]{1,0:T(8,128)(2,1)S(1)}, bf16[32,4608]{1,0:T(8,128)(2,1)S(1)}, u32[]{:S(2)}, u32[]{:S(2)}) %collective-permute-start.54) | collective-permute-done | bytes 294944 | tf_op jit(solution)/shard_map/ppermute | solution.py:29
  202.5 2.3 %collective-permute-start.57 = (bf16[16,4608]{1,0:T(8,128)(2,1)S(1)}, bf16[16,4608]{1,0:T(8,128)(2,1)S(1)}, u32[]{:S(2)}, u32[]{:S(2)}) collective-permute-start(bf16[16,4608]{1,0:T(8,128)(2,1)S(1)} %get-tuple-element.55), channel_id=1, source_target_pairs={{0,64},{32,96},{64,0},{96,32},{1,65},{33,97},{65,1},{97,33},{2,66}... | collective-permute-start | bytes 442376 | tf_op jit(solution)/shard_map/ppermute | solution.py:29
  205.2 3.8 %collective-permute-done.56.refs_1_ = bf16[16,4608]{1,0:T(8,128)(2,1)S(1)} collective-permute-done((bf16[16,4608]{1,0:T(8,128)(2,1)S(1)}, bf16[16,4608]{1,0:T(8,128)(2,1)S(1)}, u32[]{:S(2)}, u32[]{:S(2)}) %collective-permute-start.56) | collective-permute-done | bytes 147488 | tf_op jit(solution)/shard_map/ppermute | solution.py:29
  209.0 2.5 %collective-permute-done.57.refs_2_ = bf16[16,4608]{1,0:T(8,128)(2,1)S(1)} collective-permute-done((bf16[16,4608]{1,0:T(8,128)(2,1)S(1)}, bf16[16,4608]{1,0:T(8,128)(2,1)S(1)}, u32[]{:S(2)}, u32[]{:S(2)}) %collective-permute-start.57) | collective-permute-done | bytes 147488 | tf_op jit(solution)/shard_map/ppermute | solution.py:29
  213.2 2.6 %collective-permute-start.61 = (bf16[16,4608]{1,0:T(8,128)(2,1)S(1)}, bf16[16,4608]{1,0:T(8,128)(2,1)S(1)}, u32[]{:S(2)}, u32[]{:S(2)}) collective-permute-start(bf16[16,4608]{1,0:T(8,128)(2,1)S(1)} %get-tuple-element.60), channel_id=1, source_target_pairs={{0,6},{2,0},{4,2},{6,4},{1,7},{3,1},{5,3},{7,5},{8,14},{10,8},{12,... | collective-permute-start | bytes 442376 | tf_op jit(solution)/shard_map/ppermute | solution.py:29
  215.8 6.5 %collective-permute-done.59.refs_1_ = bf16[16,4608]{1,0:T(8,128)(2,1)S(1)} collective-permute-done((bf16[16,4608]{1,0:T(8,128)(2,1)S(1)}, bf16[16,4608]{1,0:T(8,128)(2,1)S(1)}, u32[]{:S(2)}, u32[]{:S(2)}) %collective-permute-start.59) | collective-permute-done | bytes 147488 | tf_op jit(solution)/shard_map/ppermute | solution.py:29
  (146 shorter events, 40.4 us)
Async XLA Ops:
  6.5 133.5 %all-gather.2.cloned.1.call-start = ((), (), s32[]{:S(2)}) async-start(), calls=%async_computation | async-start | bytes 10027008 | tf_op jit(solution)/shard_map/all_gather | solution.py:367
  11.7 8.9 %collective-permute-start.1 = (bf16[576,128]{1,0:T(8,128)(2,1)S(1)}, bf16[576,128]{1,0:T(8,128)(2,1)S(1)}, u32[]{:S(2)}, u32[]{:S(2)}) collective-permute-start(bf16[576,128]{1,0:T(8,128)(2,1)S(1)} %get-tuple-element.35), channel_id=1, source_target_pairs={{0,64},{32,96},{64,0},{96,32},{1,65},{33,97},{65,1},{97,33},{2,66}... | collective-permute-start | bytes 442376 | tf_op jit(solution)/shard_map/ppermute | solution.py:29
  14.2 8.0 %collective-permute-start.2 = (bf16[576,128]{1,0:T(8,128)(2,1)S(1)}, bf16[576,128]{1,0:T(8,128)(2,1)S(1)}, u32[]{:S(2)}, u32[]{:S(2)}) collective-permute-start(bf16[576,128]{1,0:T(8,128)(2,1)S(1)} %get-tuple-element.36), channel_id=1, source_target_pairs={{0,96},{32,0},{64,32},{96,64},{1,97},{33,1},{65,33},{97,65},{2,98}... | collective-permute-start | bytes 442376 | tf_op jit(solution)/shard_map/ppermute | solution.py:29
  15.3 8.1 %collective-permute-start.3 = (bf16[576,128]{1,0:T(8,128)(2,1)S(1)}, bf16[576,128]{1,0:T(8,128)(2,1)S(1)}, u32[]{:S(2)}, u32[]{:S(2)}) collective-permute-start(bf16[576,128]{1,0:T(8,128)(2,1)S(1)} %get-tuple-element.33.refs_0_), channel_id=1, source_target_pairs={{0,8},{8,0},{1,9},{9,1},{2,10},{10,2},{3,11},{11,3},{4,12},{12,4},... | collective-permute-start | bytes 442376 | tf_op jit(solution)/shard_map/ppermute | solution.py:29
  16.8 9.0 %collective-permute-start.4 = (bf16[576,128]{1,0:T(8,128)(2,1)S(1)}, bf16[576,128]{1,0:T(8,128)(2,1)S(1)}, u32[]{:S(2)}, u32[]{:S(2)}) collective-permute-start(bf16[576,128]{1,0:T(8,128)(2,1)S(1)} %collective-permute-done.refs_1_), channel_id=1, source_target_pairs={{0,8},{8,0},{1,9},{9,1},{2,10},{10,2},{3,11},{11,3},{4,12},{12,4},... | collective-permute-start | bytes 442376 | tf_op jit(solution)/shard_map/ppermute | solution.py:29
  22.1 14.8 %collective-permute-start.23 = (bf16[288,512]{1,0:T(8,128)(2,1)S(1)}, bf16[288,512]{1,0:T(8,128)(2,1)S(1)}, u32[]{:S(2)}, u32[]{:S(2)}) collective-permute-start(bf16[288,512]{1,0:T(8,128)(2,1)S(1)} %get-tuple-element.42.refs_0_), channel_id=1, source_target_pairs={{0,16},{16,0},{1,17},{17,1},{2,18},{18,2},{3,19},{19,3},{4,20},{20... | collective-permute-start | bytes 884744 | tf_op jit(solution)/shard_map/ppermute | solution.py:29
  23.4 16.6 %collective-permute-start.17 = (bf16[288,512]{1,0:T(8,128)(2,1)S(1)}, bf16[288,512]{1,0:T(8,128)(2,1)S(1)}, u32[]{:S(2)}, u32[]{:S(2)}) collective-permute-start(bf16[288,512]{1,0:T(8,128)(2,1)S(1)} %get-tuple-element.42.refs_0_), channel_id=1, source_target_pairs={{0,64},{32,96},{64,0},{96,32},{1,65},{33,97},{65,1},{97,33},{2,66}... | collective-permute-start | bytes 884744 | tf_op jit(solution)/shard_map/ppermute | solution.py:29
  26.9 25.3 %collective-permute-start.11 = (bf16[576,256]{1,0:T(8,128)(2,1)S(1)}, bf16[576,256]{1,0:T(8,128)(2,1)S(1)}, u32[]{:S(2)}, u32[]{:S(2)}) collective-permute-start(bf16[576,256]{1,0:T(8,128)(2,1)S(1)} %get-tuple-element.37.mine), channel_id=1, source_target_pairs={{0,1},{1,0},{2,3},{3,2},{4,5},{5,4},{6,7},{7,6},{8,9},{9,8},{10,11... | collective-permute-start | bytes 884744 | tf_op jit(solution)/shard_map/ppermute | solution.py:29
  29.6 22.6 %collective-permute-start.12 = (bf16[576,256]{1,0:T(8,128)(2,1)S(1)}, bf16[576,256]{1,0:T(8,128)(2,1)S(1)}, u32[]{:S(2)}, u32[]{:S(2)}) collective-permute-start(bf16[576,256]{1,0:T(8,128)(2,1)S(1)} %get-tuple-element.38), channel_id=1, source_target_pairs={{0,17},{1,16},{16,1},{17,0},{2,19},{3,18},{18,3},{19,2},{4,21},{5,... | collective-permute-start | bytes 884744 | tf_op jit(solution)/shard_map/ppermute | solution.py:377
  29.6 23.4 %collective-permute-start.16 = (bf16[288,512]{1,0:T(8,128)(2,1)S(1)}, bf16[288,512]{1,0:T(8,128)(2,1)}, u32[]{:S(2)}, u32[]{:S(2)}) collective-permute-start(bf16[288,512]{1,0:T(8,128)(2,1)S(1)} %get-tuple-element.42.refs_0_), channel_id=1, source_target_pairs={{0,32},{32,64},{64,96},{96,0},{1,33},{33,65},{65,97},{97,1},{2,34}... | collective-permute-start | bytes 884744 | tf_op jit(solution)/shard_map/ppermute | solution.py:29
  36.9 18.9 %collective-permute-start.18 = (bf16[288,512]{1,0:T(8,128)(2,1)S(1)}, bf16[288,512]{1,0:T(8,128)(2,1)}, u32[]{:S(2)}, u32[]{:S(2)}) collective-permute-start(bf16[288,512]{1,0:T(8,128)(2,1)S(1)} %get-tuple-element.42.refs_0_), channel_id=1, source_target_pairs={{0,96},{32,0},{64,32},{96,64},{1,97},{33,1},{65,33},{97,65},{2,98}... | collective-permute-start | bytes 884744 | tf_op jit(solution)/shard_map/ppermute | solution.py:29
  40.0 17.3 %collective-permute-start.19 = (bf16[288,512]{1,0:T(8,128)(2,1)S(1)}, bf16[288,512]{1,0:T(8,128)(2,1)S(1)}, u32[]{:S(2)}, u32[]{:S(2)}) collective-permute-start(bf16[288,512]{1,0:T(8,128)(2,1)S(1)} %get-tuple-element.42.refs_0_), channel_id=1, source_target_pairs={{0,8},{8,0},{1,9},{9,1},{2,10},{10,2},{3,11},{11,3},{4,12},{12,4},... | collective-permute-start | bytes 884744 | tf_op jit(solution)/shard_map/ppermute | solution.py:29
  52.2 12.8 %collective-permute-start.24 = (bf16[288,512]{1,0:T(8,128)(2,1)S(1)}, bf16[288,512]{1,0:T(8,128)(2,1)}, u32[]{:S(2)}, u32[]{:S(2)}) collective-permute-start(bf16[288,512]{1,0:T(8,128)(2,1)S(1)} %collective-permute-done.23.refs_8_), channel_id=1, source_target_pairs={{0,32},{32,64},{64,96},{96,0},{1,33},{33,65},{65,97},{97,1},{2,34}... | collective-permute-start | bytes 884744 | tf_op jit(solution)/shard_map/ppermute | solution.py:29
  52.2 15.0 %collective-permute-start.7 = (bf16[576,256]{1,0:T(8,128)(2,1)S(1)}, bf16[576,256]{1,0:T(8,128)(2,1)S(1)}, u32[]{:S(2)}, u32[]{:S(2)}) collective-permute-start(bf16[576,256]{1,0:T(8,128)(2,1)S(1)} %get-tuple-element.38), channel_id=1, source_target_pairs={{0,16},{16,0},{1,17},{17,1},{2,18},{18,2},{3,19},{19,3},{4,20},{20... | collective-permute-start | bytes 884744 | tf_op jit(solution)/shard_map/ppermute | solution.py:29
  53.1 16.8 %collective-permute-start.26 = (bf16[288,512]{1,0:T(8,128)(2,1)S(1)}, bf16[288,512]{1,0:T(8,128)(2,1)}, u32[]{:S(2)}, u32[]{:S(2)}) collective-permute-start(bf16[288,512]{1,0:T(8,128)(2,1)S(1)} %collective-permute-done.23.refs_8_), channel_id=1, source_target_pairs={{0,96},{32,0},{64,32},{96,64},{1,97},{33,1},{65,33},{97,65},{2,98}... | collective-permute-start | bytes 884744 | tf_op jit(solution)/shard_map/ppermute | solution.py:29
  55.8 24.1 %collective-permute-start.25 = (bf16[288,512]{1,0:T(8,128)(2,1)S(1)}, bf16[288,512]{1,0:T(8,128)(2,1)}, u32[]{:S(2)}, u32[]{:S(2)}) collective-permute-start(bf16[288,512]{1,0:T(8,128)(2,1)S(1)} %collective-permute-done.17.refs_2_), channel_id=1, source_target_pairs={{0,16},{16,0},{1,17},{17,1},{2,18},{18,2},{3,19},{19,3},{4,20},{20... | collective-permute-start | bytes 884744 | tf_op jit(solution)/shard_map/ppermute | solution.py:29
  57.3 26.6 %collective-permute-start.27 = (bf16[288,512]{1,0:T(8,128)(2,1)S(1)}, bf16[288,512]{1,0:T(8,128)(2,1)S(1)}, u32[]{:S(2)}, u32[]{:S(2)}) collective-permute-start(bf16[288,512]{1,0:T(8,128)(2,1)S(1)} %collective-permute-done.23.refs_8_), channel_id=1, source_target_pairs={{0,8},{8,0},{1,9},{9,1},{2,10},{10,2},{3,11},{11,3},{4,12},{12,4},... | collective-permute-start | bytes 884744 | tf_op jit(solution)/shard_map/ppermute | solution.py:29
  65.0 19.0 %collective-permute-start.21 = (bf16[288,512]{1,0:T(8,128)(2,1)S(1)}, bf16[288,512]{1,0:T(8,128)(2,1)S(1)}, u32[]{:S(2)}, u32[]{:S(2)}) collective-permute-start(bf16[288,512]{1,0:T(8,128)(2,1)S(1)} %collective-permute-done.17.refs_2_), channel_id=1, source_target_pairs={{0,8},{8,0},{1,9},{9,1},{2,10},{10,2},{3,11},{11,3},{4,12},{12,4},... | collective-permute-start | bytes 884744 | tf_op jit(solution)/shard_map/ppermute | solution.py:29
  67.3 18.1 %collective-permute-start.13 = (bf16[576,256]{1,0:T(8,128)(2,1)S(1)}, bf16[576,256]{1,0:T(8,128)(2,1)S(1)}, u32[]{:S(2)}, u32[]{:S(2)}) collective-permute-start(bf16[576,256]{1,0:T(8,128)(2,1)S(1)} %shard_map.102.refs_4_), channel_id=1, source_target_pairs={{0,2},{2,4},{4,6},{6,0},{1,3},{3,5},{5,7},{7,1},{8,10},{10,12},{12... | collective-permute-start | bytes 884744 | tf_op jit(solution)/shard_map/ppermute | solution.py:29
  69.9 16.2 %collective-permute-start.14 = (bf16[576,256]{1,0:T(8,128)(2,1)S(1)}, bf16[576,256]{1,0:T(8,128)(2,1)S(1)}, u32[]{:S(2)}, u32[]{:S(2)}) collective-permute-start(bf16[576,256]{1,0:T(8,128)(2,1)S(1)} %shard_map.102.refs_4_), channel_id=1, source_target_pairs={{0,4},{2,6},{4,0},{6,2},{1,5},{3,7},{5,1},{7,3},{8,12},{10,14},{12... | collective-permute-start | bytes 884744 | tf_op jit(solution)/shard_map/ppermute | solution.py:29
  79.9 9.1 %collective-permute-start.15 = (bf16[576,256]{1,0:T(8,128)(2,1)S(1)}, bf16[576,256]{1,0:T(8,128)(2,1)S(1)}, u32[]{:S(2)}, u32[]{:S(2)}) collective-permute-start(bf16[576,256]{1,0:T(8,128)(2,1)S(1)} %shard_map.102.refs_4_), channel_id=1, source_target_pairs={{0,6},{2,0},{4,2},{6,4},{1,7},{3,1},{5,3},{7,5},{8,14},{10,8},{12,... | collective-permute-start | bytes 884744 | tf_op jit(solution)/shard_map/ppermute | solution.py:29
  83.9 12.4 %collective-permute-start.10 = (bf16[576,256]{1,0:T(8,128)(2,1)S(1)}, bf16[576,256]{1,0:T(8,128)(2,1)S(1)}, u32[]{:S(2)}, u32[]{:S(2)}) collective-permute-start(bf16[576,256]{1,0:T(8,128)(2,1)S(1)} %shard_map.101.refs_0_), channel_id=1, source_target_pairs={{0,6},{2,0},{4,2},{6,4},{1,7},{3,1},{5,3},{7,5},{8,14},{10,8},{12,... | collective-permute-start | bytes 884744 | tf_op jit(solution)/shard_map/ppermute | solution.py:29
  84.0 19.7 %collective-permute-start.8 = (bf16[576,256]{1,0:T(8,128)(2,1)S(1)}, bf16[576,256]{1,0:T(8,128)(2,1)S(1)}, u32[]{:S(2)}, u32[]{:S(2)}) collective-permute-start(bf16[576,256]{1,0:T(8,128)(2,1)S(1)} %shard_map.101.refs_0_), channel_id=1, source_target_pairs={{0,2},{2,4},{4,6},{6,0},{1,3},{3,5},{5,7},{7,1},{8,10},{10,12},{12... | collective-permute-start | bytes 884744 | tf_op jit(solution)/shard_map/ppermute | solution.py:29
  86.1 17.7 %collective-permute-start.9 = (bf16[576,256]{1,0:T(8,128)(2,1)S(1)}, bf16[576,256]{1,0:T(8,128)(2,1)S(1)}, u32[]{:S(2)}, u32[]{:S(2)}) collective-permute-start(bf16[576,256]{1,0:T(8,128)(2,1)S(1)} %shard_map.101.refs_0_), channel_id=1, source_target_pairs={{0,4},{2,6},{4,0},{6,2},{1,5},{3,7},{5,1},{7,3},{8,12},{10,14},{12... | collective-permute-start | bytes 884744 | tf_op jit(solution)/shard_map/ppermute | solution.py:29
  86.1 21.0 %collective-permute-start.20 = (bf16[288,512]{1,0:T(8,128)(2,1)}, bf16[288,512]{1,0:T(8,128)(2,1)S(1)}, u32[]{:S(2)}, u32[]{:S(2)}) collective-permute-start(bf16[288,512]{1,0:T(8,128)(2,1)} %collective-permute-done.16.refs_1_), channel_id=1, source_target_pairs={{0,8},{8,0},{1,9},{9,1},{2,10},{10,2},{3,11},{11,3},{4,12},{12,4},... | collective-permute-start | bytes 884744 | tf_op jit(solution)/shard_map/ppermute | solution.py:29
  89.0 18.2 %collective-permute-start.22 = (bf16[288,512]{1,0:T(8,128)(2,1)}, bf16[288,512]{1,0:T(8,128)(2,1)S(1)}, u32[]{:S(2)}, u32[]{:S(2)}) collective-permute-start(bf16[288,512]{1,0:T(8,128)(2,1)} %collective-permute-done.18.refs_3_), channel_id=1, source_target_pairs={{0,8},{8,0},{1,9},{9,1},{2,10},{10,2},{3,11},{11,3},{4,12},{12,4},... | collective-permute-start | bytes 884744 | tf_op jit(solution)/shard_map/ppermute | solution.py:29
  96.3 10.9 %collective-permute-start.28 = (bf16[288,512]{1,0:T(8,128)(2,1)}, bf16[288,512]{1,0:T(8,128)(2,1)S(1)}, u32[]{:S(2)}, u32[]{:S(2)}) collective-permute-start(bf16[288,512]{1,0:T(8,128)(2,1)} %collective-permute-done.24.refs_9_), channel_id=1, source_target_pairs={{0,8},{8,0},{1,9},{9,1},{2,10},{10,2},{3,11},{11,3},{4,12},{12,4},... | collective-permute-start | bytes 884744 | tf_op jit(solution)/shard_map/ppermute | solution.py:29
  114.3 9.0 %collective-permute-start.32 = (bf16[256,512]{1,0:T(8,128)(2,1)S(1)}, bf16[256,512]{1,0:T(8,128)(2,1)S(1)}, u32[]{:S(2)}, u32[]{:S(2)}) collective-permute-start(bf16[256,512]{1,0:T(8,128)(2,1)S(1)} %key_value.1.refs_0_), channel_id=1, source_target_pairs={{0,64},{32,96},{64,0},{96,32},{1,65},{33,97},{65,1},{97,33},{2,66}... | collective-permute-start | bytes 786440 | tf_op jit(solution)/shard_map/ppermute | solution.py:29
  114.4 14.9 %collective-permute-start.31 = (bf16[256,512]{1,0:T(8,128)(2,1)S(1)}, bf16[256,512]{1,0:T(8,128)(2,1)S(1)}, u32[]{:S(2)}, u32[]{:S(2)}) collective-permute-start(bf16[256,512]{1,0:T(8,128)(2,1)S(1)} %key_value.1.refs_0_), channel_id=1, source_target_pairs={{0,32},{32,64},{64,96},{96,0},{1,33},{33,65},{65,97},{97,1},{2,34}... | collective-permute-start | bytes 786440 | tf_op jit(solution)/shard_map/ppermute | solution.py:29
  117.6 11.8 %collective-permute-start.33 = (bf16[256,512]{1,0:T(8,128)(2,1)S(1)}, bf16[256,512]{1,0:T(8,128)(2,1)}, u32[]{:S(2)}, u32[]{:S(2)}) collective-permute-start(bf16[256,512]{1,0:T(8,128)(2,1)S(1)} %key_value.1.refs_0_), channel_id=1, source_target_pairs={{0,96},{32,0},{64,32},{96,64},{1,97},{33,1},{65,33},{97,65},{2,98}... | collective-permute-start | bytes 786440 | tf_op jit(solution)/shard_map/ppermute | solution.py:29
  117.6 14.9 %collective-permute-start.34 = (bf16[256,512]{1,0:T(8,128)(2,1)S(1)}, bf16[256,512]{1,0:T(8,128)(2,1)S(1)}, u32[]{:S(2)}, u32[]{:S(2)}) collective-permute-start(bf16[256,512]{1,0:T(8,128)(2,1)S(1)} %key_value.1.refs_0_), channel_id=1, source_target_pairs={{0,8},{8,0},{1,9},{9,1},{2,10},{10,2},{3,11},{11,3},{4,12},{12,4},... | collective-permute-start | bytes 786440 | tf_op jit(solution)/shard_map/ppermute | solution.py:29
  121.9 13.1 %collective-permute-start.39 = (bf16[256,512]{1,0:T(8,128)(2,1)S(1)}, bf16[256,512]{1,0:T(8,128)(2,1)}, u32[]{:S(2)}, u32[]{:S(2)}) collective-permute-start(bf16[256,512]{1,0:T(8,128)(2,1)S(1)} %collective-permute-done.38.refs_8_), channel_id=1, source_target_pairs={{0,32},{32,64},{64,96},{96,0},{1,33},{33,65},{65,97},{97,1},{2,34}... | collective-permute-start | bytes 786440 | tf_op jit(solution)/shard_map/ppermute | solution.py:29
  123.3 12.4 %collective-permute-start.40 = (bf16[256,512]{1,0:T(8,128)(2,1)S(1)}, bf16[256,512]{1,0:T(8,128)(2,1)}, u32[]{:S(2)}, u32[]{:S(2)}) collective-permute-start(bf16[256,512]{1,0:T(8,128)(2,1)S(1)} %collective-permute-done.32.refs_2_), channel_id=1, source_target_pairs={{0,16},{16,0},{1,17},{17,1},{2,18},{18,2},{3,19},{19,3},{4,20},{20... | collective-permute-start | bytes 786440 | tf_op jit(solution)/shard_map/ppermute | solution.py:29
  129.3 8.8 %collective-permute-start.35 = (bf16[256,512]{1,0:T(8,128)(2,1)S(1)}, bf16[256,512]{1,0:T(8,128)(2,1)S(1)}, u32[]{:S(2)}, u32[]{:S(2)}) collective-permute-start(bf16[256,512]{1,0:T(8,128)(2,1)S(1)} %collective-permute-done.31.refs_1_), channel_id=1, source_target_pairs={{0,8},{8,0},{1,9},{9,1},{2,10},{10,2},{3,11},{11,3},{4,12},{12,4},... | collective-permute-start | bytes 786440 | tf_op jit(solution)/shard_map/ppermute | solution.py:29
  135.0 8.6 %collective-permute-start.42 = (bf16[256,512]{1,0:T(8,128)(2,1)S(1)}, bf16[256,512]{1,0:T(8,128)(2,1)}, u32[]{:S(2)}, u32[]{:S(2)}) collective-permute-start(bf16[256,512]{1,0:T(8,128)(2,1)S(1)} %collective-permute-done.38.refs_8_), channel_id=1, source_target_pairs={{0,8},{8,0},{1,9},{9,1},{2,10},{10,2},{3,11},{11,3},{4,12},{12,4},... | collective-permute-start | bytes 786440 | tf_op jit(solution)/shard_map/ppermute | solution.py:29
  153.9 12.5 %collective-permute-start.46 = (bf16[32,4608]{1,0:T(8,128)(2,1)S(1)}, bf16[32,4608]{1,0:T(8,128)(2,1)S(1)}, u32[]{:S(2)}, u32[]{:S(2)}) collective-permute-start(bf16[32,4608]{1,0:T(8,128)(2,1)S(1)} %get-tuple-element.45), channel_id=1, source_target_pairs={{0,5},{1,4},{2,7},{3,6},{4,1},{5,0},{6,3},{7,2},{8,13},{9,12},{10,... | collective-permute-start | bytes 884744 | tf_op jit(solution)/shard_map/ppermute | solution.py:466
  154.0 19.1 %collective-permute-start.47 = (bf16[32,4608]{1,0:T(8,128)(2,1)S(1)}, bf16[32,4608]{1,0:T(8,128)(2,1)S(1)}, u32[]{:S(2)}, u32[]{:S(2)}) collective-permute-start(bf16[32,4608]{1,0:T(8,128)(2,1)S(1)} %get-tuple-element.46), channel_id=1, source_target_pairs={{0,3},{1,2},{2,5},{3,4},{4,7},{5,6},{6,1},{7,0},{8,11},{9,10},{10,... | collective-permute-start | bytes 884744 | tf_op jit(solution)/shard_map/ppermute | solution.py:466
  160.4 21.1 %collective-permute-start.48 = (bf16[32,4608]{1,0:T(8,128)(2,1)S(1)}, bf16[32,4608]{1,0:T(8,128)(2,1)S(1)}, u32[]{:S(2)}, u32[]{:S(2)}) collective-permute-start(bf16[32,4608]{1,0:T(8,128)(2,1)S(1)} %get-tuple-element.47), channel_id=1, source_target_pairs={{0,7},{1,6},{2,1},{3,0},{4,3},{5,2},{6,5},{7,4},{8,15},{9,14},{10,... | collective-permute-start | bytes 884744 | tf_op jit(solution)/shard_map/ppermute | solution.py:466
  160.4 22.7 %collective-permute-start.49 = (bf16[32,4608]{1,0:T(8,128)(2,1)S(1)}, bf16[32,4608]{1,0:T(8,128)(2,1)S(1)}, u32[]{:S(2)}, u32[]{:S(2)}) collective-permute-start(bf16[32,4608]{1,0:T(8,128)(2,1)S(1)} %get-tuple-element.48), channel_id=1, source_target_pairs={{0,1},{1,0},{2,3},{3,2},{4,5},{5,4},{6,7},{7,6},{8,9},{9,8},{10,11... | collective-permute-start | bytes 884744 | tf_op jit(solution)/shard_map/ppermute | solution.py:29
  161.2 21.8 %collective-permute-start.50 = (bf16[32,4608]{1,0:T(8,128)(2,1)S(1)}, bf16[32,4608]{1,0:T(8,128)(2,1)S(1)}, u32[]{:S(2)}, u32[]{:S(2)}) collective-permute-start(bf16[32,4608]{1,0:T(8,128)(2,1)S(1)} %get-tuple-element.49), channel_id=1, source_target_pairs={{0,4},{2,6},{4,0},{6,2},{1,5},{3,7},{5,1},{7,3},{8,12},{10,14},{12... | collective-permute-start | bytes 884744 | tf_op jit(solution)/shard_map/ppermute | solution.py:29
  166.4 19.6 %collective-permute-start.51 = (bf16[32,4608]{1,0:T(8,128)(2,1)S(1)}, bf16[32,4608]{1,0:T(8,128)(2,1)S(1)}, u32[]{:S(2)}, u32[]{:S(2)}) collective-permute-start(bf16[32,4608]{1,0:T(8,128)(2,1)S(1)} %get-tuple-element.50), channel_id=1, source_target_pairs={{0,2},{2,4},{4,6},{6,0},{1,3},{3,5},{5,7},{7,1},{8,10},{10,12},{12... | collective-permute-start | bytes 884744 | tf_op jit(solution)/shard_map/ppermute | solution.py:29
  173.1 17.1 %collective-permute-start.52 = (bf16[32,4608]{1,0:T(8,128)(2,1)S(1)}, bf16[32,4608]{1,0:T(8,128)(2,1)S(1)}, u32[]{:S(2)}, u32[]{:S(2)}) collective-permute-start(bf16[32,4608]{1,0:T(8,128)(2,1)S(1)} %get-tuple-element.51), channel_id=1, source_target_pairs={{0,6},{2,0},{4,2},{6,4},{1,7},{3,1},{5,3},{7,5},{8,14},{10,8},{12,... | collective-permute-start | bytes 884744 | tf_op jit(solution)/shard_map/ppermute | solution.py:29
  190.7 8.3 %collective-permute-start.54 = (bf16[32,4608]{1,0:T(8,128)(2,1)S(1)}, bf16[32,4608]{1,0:T(8,128)(2,1)S(1)}, u32[]{:S(2)}, u32[]{:S(2)}) collective-permute-start(bf16[32,4608]{1,0:T(8,128)(2,1)S(1)} %finish.1.refs_0_), channel_id=1, source_target_pairs={{0,16},{16,0},{1,17},{17,1},{2,18},{18,2},{3,19},{19,3},{4,20},{20... | collective-permute-start | bytes 884744 | tf_op jit(solution)/shard_map/ppermute | solution.py:29
  192.3 8.0 %collective-permute-start.53 = (bf16[32,4608]{1,0:T(8,128)(2,1)S(1)}, bf16[32,4608]{1,0:T(8,128)(2,1)S(1)}, u32[]{:S(2)}, u32[]{:S(2)}) collective-permute-start(bf16[32,4608]{1,0:T(8,128)(2,1)S(1)} %finish.1.refs_0_), channel_id=1, source_target_pairs={{0,8},{8,0},{1,9},{9,1},{2,10},{10,2},{3,11},{11,3},{4,12},{12,4},... | collective-permute-start | bytes 884744 | tf_op jit(solution)/shard_map/ppermute | solution.py:29
  202.5 9.1 %collective-permute-start.57 = (bf16[16,4608]{1,0:T(8,128)(2,1)S(1)}, bf16[16,4608]{1,0:T(8,128)(2,1)S(1)}, u32[]{:S(2)}, u32[]{:S(2)}) collective-permute-start(bf16[16,4608]{1,0:T(8,128)(2,1)S(1)} %get-tuple-element.55), channel_id=1, source_target_pairs={{0,64},{32,96},{64,0},{96,32},{1,65},{33,97},{65,1},{97,33},{2,66}... | collective-permute-start | bytes 442376 | tf_op jit(solution)/shard_map/ppermute | solution.py:29
  213.0 9.3 %collective-permute-start.59 = (bf16[16,4608]{1,0:T(8,128)(2,1)S(1)}, bf16[16,4608]{1,0:T(8,128)(2,1)S(1)}, u32[]{:S(2)}, u32[]{:S(2)}) collective-permute-start(bf16[16,4608]{1,0:T(8,128)(2,1)S(1)} %get-tuple-element.58), channel_id=1, source_target_pairs={{0,2},{2,4},{4,6},{6,0},{1,3},{3,5},{5,7},{7,1},{8,10},{10,12},{12... | collective-permute-start | bytes 442376 | tf_op jit(solution)/shard_map/ppermute | solution.py:29
  213.1 9.2 %collective-permute-start.60 = (bf16[16,4608]{1,0:T(8,128)(2,1)S(1)}, bf16[16,4608]{1,0:T(8,128)(2,1)S(1)}, u32[]{:S(2)}, u32[]{:S(2)}) collective-permute-start(bf16[16,4608]{1,0:T(8,128)(2,1)S(1)} %get-tuple-element.59), channel_id=1, source_target_pairs={{0,4},{2,6},{4,0},{6,2},{1,5},{3,7},{5,1},{7,3},{8,12},{10,14},{12... | collective-permute-start | bytes 442376 | tf_op jit(solution)/shard_map/ppermute | solution.py:29
  213.2 9.1 %collective-permute-start.61 = (bf16[16,4608]{1,0:T(8,128)(2,1)S(1)}, bf16[16,4608]{1,0:T(8,128)(2,1)S(1)}, u32[]{:S(2)}, u32[]{:S(2)}) collective-permute-start(bf16[16,4608]{1,0:T(8,128)(2,1)S(1)} %get-tuple-element.60), channel_id=1, source_target_pairs={{0,6},{2,0},{4,2},{6,4},{1,7},{3,1},{5,3},{7,5},{8,14},{10,8},{12,... | collective-permute-start | bytes 442376 | tf_op jit(solution)/shard_map/ppermute | solution.py:29
  (37 other events, 427.0 us)
Sparse Core Ops, SparseCore 0:
  9.7 85.8 all-gather.1
